TPU v7x, 32 devices: a whole 2x2x4 slice. The times are simulated.
32 devices in a mesh: tm: 2 (over core), stn: 4 (over z), chan: 4 (over y, x).
Axes of the slice: x: 2, y: 2, z: 4, core: 2. Of those that a mesh axis runs over, the one named last changes fastest.
Arguments:
- voltages: bfloat16 [2, 8, 512, 32, 2, 256], P(None, 'chan', 'stn', 'tm'), may hold values from -100 to 100
- fir_taps: float32 [16, 256], replicated, may hold values from -1.5 to 1.5
- station_map: int32 [512], P('stn'), may hold values from 0 to 31, as said below
- beam_index: int32 [512], P('stn'), may hold values from 0 to 15
- weight_table: bfloat16 [2, 16, 8, 8], P(None, None, 'chan'), may hold values from -1.5 to 1.5
Outputs:
- visibilities: float32 [2, 2, 8, 32, 32, 8, 2, 2, 256], P('tm', None, 'chan', 'stn')
Inputs may be any that keep to these rules, and one draw needn't show every extreme that they name: `station_map`: each station number names exactly 16 dishes; of the dishes g * 128 up to (g + 1) * 128 - 1, exactly 32 name a station of the block h * 8 up to (h + 1) * 8 - 1, for every g and h.
All inputs are finite; a program needn't handle non-finite values.
Results may differ from a plain program's by a relative error of at most 0.017.
Values may be sent and summed in bfloat16 or wider, within the bound.
No kernel may reach another device: no remote copies, remote signals or barrier semaphores. Data moves between devices by JAX's collectives and lax.ppermute only.
A program may use at most 512 MiB of HBM per device.

v0:
```python
import jax
import jax.numpy as jnp
from jax import lax
from jax.sharding import PartitionSpec as P

STATIONS = 32
COARSE = 8


epsilon = 1e-06


def shifted(value, axis, steps):
    count = lax.axis_size(axis)
    first, last = (max(0, -steps), min(count, count - steps))
    return lax.ppermute(value, axis, [(source, source + steps) for source in range(first, last)])


def dft_tables(length):
    bin_index = jnp.arange(length, dtype=jnp.int32)
    phase_step = bin_index[:, None] * bin_index[None, :] % length
    angles = phase_step.astype(jnp.float32) * (2.0 * jnp.pi / length)
    return (jnp.cos(angles).astype(jnp.bfloat16), jnp.sin(angles).astype(jnp.bfloat16))


def power_terms(formed):
    values = formed.astype(jnp.float32)
    return jnp.sum(values * values, axis=(1, 3, 4, 6))


def normalise(formed, power_sum, denominator):
    inverse_rms = lax.rsqrt(power_sum / denominator + epsilon)
    return (formed.astype(jnp.float32) * inverse_rms[:, None, :, None, None, :, None]).astype(
        jnp.bfloat16
    )


def correlate(left_beams, right_beams, frames_dev):

    def product(first_part, second_part):
        return jnp.einsum(
            "sbcfpk,tbcfqk->cstbpqk", first_part, second_part, preferred_element_type=jnp.float32
        )

    left_re = left_beams[:, 0]
    left_im = left_beams[:, 1]
    right_re = right_beams[:, 0]
    right_im = right_beams[:, 1]
    vis_re = product(left_re, right_re) + product(left_im, right_im)
    vis_im = product(left_im, right_re) - product(left_re, right_im)
    return jnp.stack([vis_re, vis_im]) / frames_dev


def mixing_of(row_hot, weight_table):
    weights = jnp.einsum("dt,otcb->ocdb", row_hot, weight_table, preferred_element_type=jnp.float32)
    weight_re = weights[0]
    weight_im = weights[1]
    return jnp.stack([jnp.stack([weight_re, -weight_im]), jnp.stack([weight_im, weight_re])])


def per_device(voltages, fir_taps, station_map, beam_index, weight_table):
    components, coarse_dev, dishes_dev, frames_dev, polars, fine_bins = voltages.shape
    history = fir_taps.shape[0] - 1
    table_rows = weight_table.shape[1]
    cosine, sine_table = dft_tables(fine_bins)
    earlier = shifted(voltages[:, :, :, frames_dev - history :], "tm", 1)
    extended = jnp.concatenate([earlier, voltages], axis=3)
    filtered = jnp.zeros(voltages.shape, jnp.float32)
    for tap_index in range(history + 1):
        offset = history - tap_index
        filtered = filtered + fir_taps[tap_index] * extended[
            :, :, :, offset : offset + frames_dev
        ].astype(jnp.float32)
    filtered = filtered.astype(jnp.bfloat16)
    real_part = filtered[0].reshape(-1, fine_bins)
    imag_part = filtered[1].reshape(-1, fine_bins)
    spec_re = jnp.dot(real_part, cosine, preferred_element_type=jnp.float32) + jnp.dot(
        imag_part, sine_table, preferred_element_type=jnp.float32
    )
    spec_im = jnp.dot(imag_part, cosine, preferred_element_type=jnp.float32) - jnp.dot(
        real_part, sine_table, preferred_element_type=jnp.float32
    )
    spectra = jnp.stack([spec_re, spec_im]).reshape(voltages.shape).astype(jnp.bfloat16)
    denominator = COARSE * frames_dev * fine_bins
    own_count = STATIONS // lax.axis_size("stn")
    station_hot = (station_map[:, None] == jnp.arange(STATIONS, dtype=jnp.int32)[None, :]).astype(
        jnp.float32
    )
    table_hot = (beam_index[:, None] == jnp.arange(table_rows, dtype=jnp.int32)[None, :]).astype(
        jnp.bfloat16
    )
    mixing = mixing_of(table_hot, weight_table)
    steering = (station_hot[None, None, None, :, :, None] * mixing[:, :, :, :, None, :]).astype(
        jnp.bfloat16
    )
    full_sums = jnp.einsum(
        "oicdsb,icdfpk->sobcfpk", steering, spectra, preferred_element_type=jnp.float32
    )
    formed = lax.psum(full_sums.astype(jnp.bfloat16), "stn")
    power_sum = lax.psum(power_terms(formed), "chan")
    normed = normalise(formed, power_sum, denominator)
    own_rows = lax.dynamic_slice_in_dim(normed, lax.axis_index("stn") * own_count, own_count, 0)
    visibility = correlate(own_rows, normed, frames_dev)
    return visibility[None]


def solution(mesh):
    in_specs = (
        P(None, "chan", "stn", "tm", None, None),
        P(),
        P("stn"),
        P("stn"),
        P(None, None, "chan", None),
    )
    out_specs = P("tm", None, "chan", "stn", None, None, None, None, None)
    return jax.shard_map(
        per_device, mesh=mesh, in_specs=in_specs, out_specs=out_specs, check_vma=False
    )
```

profile of v0, /device:TPU:0, one launch (start us, length us, event | category | flops | bytes accessed | tf_op | source)
XLA Modules:
  0.0 1312.8 jit_solution(9741827098668168143)
XLA Ops:
  6.5 0.0 copy-start
  6.5 0.0 all-reduce.2.cloned.1.call-start
  6.5 0.0 slice-start
  6.5 6.9 slice.122
  13.5 5.5 collective-permute-start
  18.9 0.0 copy-done
  18.9 0.8 fusion.20
  19.7 0.0 slice-start.1
  19.8 0.8 fusion.19
  20.6 1.1 fusion.40
  21.6 6.4 collective-permute-done
  28.0 6.8 constant_dynamic-update-slice_fusion.1
  34.8 0.0 slice-done
  34.8 0.0 slice-done.1
  34.8 8.4 constant_dynamic-update-slice_fusion
  43.3 108.3 %add_convert_fusion = bf16[2,2,128,16,2,256]{5,4,3,2,1,0:T(2,128)(2,1)} fusion(bf16[2,2,128,16,2,256]{5,4,3,2,1,0:T(2,128)(2,1)S(1)} %bitcast.86, bf16[2,2,128,31,2,256]{5,4,3,2,1,0:T(2,128)(2,1)S(1)} %constant_dynamic-update-slice_fusion, f32[256]{0:T(256)S(1)} %bitcast.102, f32[256]{0:T(256)S(1)} %bitcast.103, f32[256]{0:T(256)S(1)} %bitcast.89, ...), kind=kLoop, calls=%fused_computation.8 | loop fusion | flops 201326592 | bytes 142622720 | tf_op jit(solution)/shard_map/convert_element_type | solution.py:74
  151.6 10.2 fusion.39
  161.8 7.2 reshape_squeeze.6
  168.9 7.2 reshape_squeeze.7
  176.1 0.0 copy-start.3
  176.1 4.5 fusion.17
  180.6 0.0 copy-done.3
  180.6 5.6 fusion.18
  186.2 4.2 fusion.4
  190.4 7.3 stack.35
  197.8 0.0 copy-start.2
  197.8 7.7 copy.19
  205.5 0.0 copy-done.2
  205.5 6.4 fusion.3
  211.9 7.2 stack.34
  219.1 5.6 copy.18
  224.7 10.1 fusion.2
  234.8 0.0 all-reduce.2.cloned.1.call-update
  234.9 564.4 %all-reduce.2.cloned.1.call-done = bf16[32,2,8,2,16,2,256]{6,0,2,1,5,4,3:T(8,128)(2,1)} async-done(((bf16[32,2,8,2,16,2,256]{6,0,2,1,5,4,3:T(8,128)(2,1)}), bf16[32,2,8,2,16,2,256]{6,0,2,1,5,4,3:T(8,128)(2,1)}) %all-reduce.2.cloned.1.call-update) | async-done | bytes 16777232 | tf_op jit(solution)/shard_map/psum | solution.py:99
  799.3 7.4 fusion
  806.7 10.0 psum.15
  816.7 12.7 fusion.1
  829.4 6.4 slice_bitcast_fusion
  835.8 2.0 dynamic-slice_bitcast_fusion.1
  837.8 22.6 %copy.36 = bf16[8,8,2,16,2,256,1]{3,0,4,6,5,1,2:T(8,128)(2,1)} copy(bf16[8,8,2,16,2,256,1]{5,0,1,4,3,2,6:T(8,128)(2,1)} %get-tuple-element.5) | data formatting | bytes 4194304 | tf_op jit(solution)/shard_map/squeeze | solution.py:45
  860.4 16.6 %copy.38 = bf16[8,8,2,16,2,256,1]{3,0,4,6,5,1,2:T(8,128)(2,1)} copy(bf16[8,8,2,16,2,256,1]{5,0,1,4,3,2,6:T(8,128)(2,1)S(1)} %get-tuple-element.6) | data formatting | bytes 4194304 | tf_op jit(solution)/shard_map/squeeze | solution.py:46
  877.0 44.4 %copy.37 = bf16[32,8,2,16,2,256,1]{0,3,6,4,5,1,2:T(8,128)(2,1)} copy(bf16[32,8,2,16,2,256,1]{5,0,1,4,3,2,6:T(8,128)(2,1)} %get-tuple-element.7) | data formatting | bytes 16777216 | tf_op jit(solution)/shard_map/squeeze | solution.py:48
  921.4 44.4 %copy.35 = bf16[32,8,2,16,2,256,1]{0,3,6,4,5,1,2:T(8,128)(2,1)} copy(bf16[32,8,2,16,2,256,1]{5,0,1,4,3,2,6:T(8,128)(2,1)} %get-tuple-element.8) | data formatting | bytes 16777216 | tf_op jit(solution)/shard_map/squeeze | solution.py:47
  965.8 39.2 %fusion.42 = f32[2,8,256,32,2,8,2]{3,5,6,4,2,1,0:T(8,128)} fusion(bf16[32,8,2,16,2,256,1]{0,3,6,4,5,1,2:T(8,128)(2,1)} %copy.35, bf16[8,8,2,16,2,256,1]{3,0,4,6,5,1,2:T(8,128)(2,1)} %copy.38), kind=kOutput, calls=%fused_computation.70 | convolution fusion | flops 134217728 | bytes 27262976 | tf_op jit(solution)/shard_map/sbcfpk,tbcfqk->cstbpqk/dot_general | solution.py:41
  1005.0 39.2 %fusion.41 = f32[2,8,256,32,2,8,2]{3,5,6,4,2,1,0:T(8,128)} fusion(bf16[32,8,2,16,2,256,1]{0,3,6,4,5,1,2:T(8,128)(2,1)} %copy.35, bf16[8,8,2,16,2,256,1]{3,0,4,6,5,1,2:T(8,128)(2,1)} %copy.36), kind=kOutput, calls=%fused_computation.69 | convolution fusion | flops 134217728 | bytes 27262976 | tf_op jit(solution)/shard_map/sbcfpk,tbcfqk->cstbpqk/dot_general | solution.py:41
  1044.2 60.2 %subtract_bitcast_fusion = f32[1,1,2,8,32,8,2,2,256]{4,3,6,7,8,5,2,1,0:T(8,128)} fusion(f32[2,8,256,32,2,8,2]{3,5,6,4,2,1,0:T(8,128)} %fusion.42, bf16[32,8,2,16,2,256,1]{0,3,6,4,5,1,2:T(8,128)(2,1)} %copy.37, bf16[8,8,2,16,2,256,1]{3,0,4,6,5,1,2:T(8,128)(2,1)} %copy.36), kind=kOutput, calls=%fused_computation | convolution fusion | flops 138412032 | bytes 44040192 | tf_op jit(solution)/shard_map/sbcfpk,tbcfqk->cstbpqk/dot_general | solution.py:41
  1104.4 34.7 %copy.30 = f32[1,1,2,8,32,8,2,2,256]{8,5,7,6,4,3,2,1,0:T(8,128)} copy(f32[1,1,2,8,32,8,2,2,256]{4,3,6,7,8,5,2,1,0:T(8,128)} %subtract_bitcast_fusion) | data formatting | bytes 33554432 | tf_op jit(solution)/shard_map/stack | solution.py:51
  1139.1 60.5 %add_bitcast_fusion = f32[1,1,2,8,32,8,2,2,256]{4,3,6,7,8,5,2,1,0:T(8,128)} fusion(f32[2,8,256,32,2,8,2]{3,5,6,4,2,1,0:T(8,128)} %fusion.41, bf16[32,8,2,16,2,256,1]{0,3,6,4,5,1,2:T(8,128)(2,1)} %copy.37, bf16[8,8,2,16,2,256,1]{3,0,4,6,5,1,2:T(8,128)(2,1)} %copy.38), kind=kOutput, calls=%fused_computation.1 | convolution fusion | flops 138412032 | bytes 44040192 | tf_op jit(solution)/shard_map/sbcfpk,tbcfqk->cstbpqk/dot_general | solution.py:41
  1199.5 34.8 %copy.29 = f32[1,1,2,8,32,8,2,2,256]{8,5,7,6,4,3,2,1,0:T(8,128)} copy(f32[1,1,2,8,32,8,2,2,256]{4,3,6,7,8,5,2,1,0:T(8,128)} %add_bitcast_fusion) | data formatting | bytes 33554432 | tf_op jit(solution)/shard_map/stack | solution.py:51
  1234.3 24.9 %maximum_multiply_fusion = f32[1,2,2,8,32,8,2,2,256]{8,5,7,6,4,3,2,1,0:T(8,128)} fusion(f32[1,1,2,8,32,8,2,2,256]{8,5,7,6,4,3,2,1,0:T(8,128)} %copy.30, f32[1,1,2,8,32,8,2,2,256]{8,5,7,6,4,3,2,1,0:T(8,128)} %copy.29), kind=kLoop, calls=%fused_computation.6 | loop fusion | flops 16777216 | bytes 67108864 | tf_op jit(solution)/shard_map/div | solution.py:51
  1259.2 0.0 copy-start.1
  1259.2 46.3 %copy.31 = f32[1,2,2,8,32,8,2,2,256]{8,7,6,5,4,3,2,1,0:T(2,128)} copy(f32[1,2,2,8,32,8,2,2,256]{8,5,7,6,4,3,2,1,0:T(8,128)} %maximum_multiply_fusion) | data formatting | bytes 67108864 | tf_op jit(solution)/shard_map/div | solution.py:51
  1305.5 0.0 copy-done.1
  (6 shorter events, 0.0 us)
Async XLA Ops:
  6.5 12.4 copy-start
  6.5 792.8 %all-reduce.2.cloned.1.call-start = ((), (), s32[]{:S(2)}) async-start(), calls=%async_computation | async-start | bytes 33554432 | tf_op jit(solution)/shard_map/psum | solution.py:99
  6.5 28.2 %slice-start = ((s8[8388608]{0:T(1024)(128)(4,1)}), s8[4194304]{0:T(1024)(128)(4,1)S(1)}, s32[]{:S(2)}) async-start(s8[8388608]{0:T(1024)(128)(4,1)} %bitcast.85), calls=%async_computation.1 | async-start | bytes 8388608
  13.5 14.6 %collective-permute-start = (bf16[2,2,128,15,2,256]{5,4,3,2,1,0:T(2,128)(2,1)S(1)}, bf16[2,2,128,15,2,256]{5,4,3,2,1,0:T(2,128)(2,1)}, u32[]{:S(2)}, u32[]{:S(2)}) collective-permute-start(bf16[2,2,128,15,2,256]{5,4,3,2,1,0:T(2,128)(2,1)S(1)} %slice.122), channel_id=1, source_target_pairs={{0,16},{1,17},{2,18},{3,19},{4,20},{5,21},{6,22},{7,23},{8,24},{9,... | collective-permute-start | bytes 23592968 | tf_op jit(solution)/shard_map/ppermute | solution.py:16
  19.7 15.1 %slice-start.1 = ((s8[8388608]{0:T(1024)(128)(4,1)}), s8[4194304]{0:T(1024)(128)(4,1)S(1)}, s32[]{:S(2)}) async-start(s8[8388608]{0:T(1024)(128)(4,1)} %bitcast.85), calls=%async_computation.2 | async-start | bytes 8388608
  176.1 4.5 copy-start.3
  197.8 7.7 copy-start.2
  1259.2 46.3 %copy-start.1 = (bf16[2,16,2,8]{1,3,2,0:T(8,128)(2,1)S(1)}, bf16[2,16,2,8]{1,3,2,0:T(8,128)(2,1)}, u32[]{:S(2)}) copy-start(bf16[2,16,2,8]{1,3,2,0:T(8,128)(2,1)} %param.9) | copy-start | bytes 3076
Sparse Core Ops, SparseCore 0:
  235.0 564.2 all-reduce.1
where the time goes:
time: 1320 us; the launch traced here: 1310 us
  waiting for transfers between devices  571 us (43%)
  local copies, waits for them, and re-layouts  328 us (25%)
  matrix products  231 us (18%)
  other arithmetic  154 us (12%)
  between operations  14 us (1%)
    psum x1, waiting for transfers between devices, per_device(): formed = lax.psum(full_sums.astype(jnp.bfloat16), 'stn')  564 us
    dot_general x4, matrix products, product(): jnp.einsum('sbcfpk,tbcfqk->cstbpqk', first_part, second_part, preferred_e...  199 us
    convert_element_type x1, other arithmetic, per_device(): filtered = filtered.astype(jnp.bfloat16)  108 us
    another operation x2, local copies, waits for them, and re-layouts, correlate(): return jnp.stack([vis_re, vis_im]) / frames_dev  69.5 us
    squeeze x2, local copies, waits for them, and re-layouts, correlate(): right_im = right_beams[:, 1]  50.9 us
    div x1, local copies, waits for them, and re-layouts, correlate(): return jnp.stack([vis_re, vis_im]) / frames_dev  46.3 us
    squeeze x1, local copies, waits for them, and re-layouts, correlate(): right_re = right_beams[:, 0]  44.4 us
    another operation x4, local copies, waits for them, and re-layouts, per_device(): jnp.stack([spec_re, spec_im]).reshape(voltages.shape).astype(jnp.bfloat16)  27.9 us
  transfers between devices with their start and end apart: 2, of which 2 were waited for; matrix products, arithmetic and copies ran while one was open for 0% of the time, Pallas kernels for 0%

commit v1 on v0

v1 whole, which is shorter than its diff:
```python
import jax
import jax.numpy as jnp
from jax import lax
from jax.experimental import pallas as pl
from jax.experimental.pallas import tpu as pltpu
from jax.sharding import PartitionSpec as P


STATIONS = 32
COARSE = 8
LANES = 128
UNROLL = 8
PREPARE = 4
PAIRS = (2, 4)

epsilon = 1e-06


def shifted(value, axis, steps):
    count = lax.axis_size(axis)
    first, last = (max(0, -steps), min(count, count - steps))
    return lax.ppermute(value, axis, [(source, source + steps) for source in range(first, last)])


def dft_tables(length):
    bin_index = jnp.arange(length, dtype=jnp.int32)
    phase_step = bin_index[:, None] * bin_index[None, :] % length
    angles = phase_step.astype(jnp.float32) * (2.0 * jnp.pi / length)
    return (jnp.cos(angles).astype(jnp.bfloat16), jnp.sin(angles).astype(jnp.bfloat16))


def block_ranks(station_map, block_stations, share):
    block = station_map // block_stations
    position = jnp.arange(station_map.shape[-1], dtype=jnp.int32)
    same = block[..., :, None] == block[..., None, :]
    before = position[None, :] < position[:, None]
    return block * share + jnp.sum((same & before).astype(jnp.int32), axis=-1)


def sort_dishes(voltages, order, coarse, parts, share):
    comps, _, _, frames, pols, fine = voltages.shape
    tiles = fine // LANES

    def body(order_ref, x_ref, *refs):
        outs, sems = refs[: len(parts)], refs[len(parts) :]

        def issue(place, carry):
            for part, out_ref, sem in zip(parts, outs, sems):
                dish = order_ref[part * share + place]
                for tile in range(tiles):
                    lanes = pl.ds(tile * LANES, LANES)
                    pltpu.make_async_copy(
                        x_ref.at[:, coarse, dish, :, :, lanes], out_ref.at[:, :, tile, place], sem
                    ).start()
            return carry

        lax.fori_loop(0, share, issue, 0)
        for out_ref, sem in zip(outs, sems):
            pltpu.make_async_copy(out_ref, out_ref, sem).wait()

    results = pl.pallas_call(
        body,
        out_shape=[jax.ShapeDtypeStruct((comps, frames, tiles, share, pols, LANES), voltages.dtype)] * len(parts),
        in_specs=[pl.BlockSpec(memory_space=pltpu.SMEM), pl.BlockSpec(memory_space=pl.ANY)],
        out_specs=[pl.BlockSpec(memory_space=pltpu.VMEM)] * len(parts),
        scratch_shapes=[pltpu.SemaphoreType.DMA] * len(parts),
        name="sort_dishes",
    )(order, voltages)

    return [array.reshape(comps, frames, tiles, share * pols, LANES) for array in results]


def beam_sums(weights, sources, frames_step=4):
    comps, frames, tiles, rows, _ = sources[0].shape
    out_rows, contract = weights.shape

    def body(w_ref, *refs):
        out_ref = refs[-1]
        for frame in range(frames_step):
            pieces = []
            for ref in refs[:-1]:
                for comp in range(comps):
                    pieces.append(jnp.concatenate([ref[comp, frame, t] for t in range(tiles)], axis=1))
            stacked = jnp.concatenate(pieces, axis=0)
            out_ref[frame] = jnp.dot(
                w_ref[...], stacked, preferred_element_type=jnp.float32
            ).astype(out_ref.dtype)

    return pl.pallas_call(
        body,
        grid=(frames // frames_step,),
        in_specs=[pl.BlockSpec((out_rows, contract), lambda i: (0, 0))]
        + [pl.BlockSpec((comps, frames_step, tiles, rows, LANES), lambda i: (0, i, 0, 0, 0))] * len(sources),
        out_specs=pl.BlockSpec((frames_step, out_rows, tiles * LANES), lambda i: (i, 0, 0)),
        out_shape=jax.ShapeDtypeStruct((frames, out_rows, tiles * LANES), jnp.bfloat16),
        name="beam_sums",
    )(weights, *sources)


def channelize(previous, current, taps, cosine, sine, beams):
    frames, out_rows, fine = current.shape
    taps_count = taps.shape[0]
    history = taps_count - 1
    rows = out_rows // (2 * beams)
    tiles = fine // LANES
    previous = previous.reshape(frames, 2, beams * rows, fine)
    current = current.reshape(frames, 2, beams * rows, fine)
    wide_taps = jnp.broadcast_to(taps[:, None, :], (taps_count, 8, fine))

    def body(prev_ref, cur_ref, taps_ref, cos_ref, sin_ref, out_ref, pow_ref, wide_ref, filt_ref):
        for frame in range(history):
            wide_ref[frame] = prev_ref[frames - history + frame].astype(jnp.float32)
        for frame in range(frames):
            wide_ref[history + frame] = cur_ref[frame].astype(jnp.float32)
        for comp in range(2):
            for tile in range(tiles):
                lanes = slice(tile * LANES, (tile + 1) * LANES)
                for low in range(0, rows, 8):
                    for frame in range(frames):
                        terms = [
                            taps_ref[tap, :, lanes]
                            * wide_ref[history + frame - tap, comp, low : low + 8, lanes]
                            for tap in range(taps_count)
                        ]
                        while len(terms) > 1:
                            terms = [
                                a + b for a, b in zip(terms[::2], terms[1::2])
                            ] + terms[len(terms) // 2 * 2 :]
                        filt_ref[comp, frame * rows + low : frame * rows + low + 8, lanes] = terms[0]
        real_part = filt_ref[0].astype(jnp.bfloat16)
        imag_part = filt_ref[1].astype(jnp.bfloat16)

        def dot(a, b):
            return jnp.dot(a, b, preferred_element_type=jnp.float32)

        spec_re = dot(real_part, cos_ref[...]) + dot(imag_part, sin_ref[...])
        spec_im = dot(imag_part, cos_ref[...]) - dot(real_part, sin_ref[...])
        power = jnp.zeros((rows, LANES), jnp.float32)
        for comp, spectrum in enumerate((spec_re, spec_im)):
            rounded = spectrum.astype(jnp.bfloat16)
            squares = rounded.astype(jnp.float32)
            squares = squares * squares
            for tile in range(tiles):
                lanes = slice(tile * LANES, (tile + 1) * LANES)
                for frame in range(frames):
                    out_ref[0, comp, frame, tile * rows : (tile + 1) * rows, :] = rounded[
                        frame * rows : (frame + 1) * rows, lanes
                    ]
                    power = power + squares[frame * rows : (frame + 1) * rows, lanes]
        pow_ref[0] = power

    return pl.pallas_call(
        body,
        grid=(beams,),
        in_specs=[
            pl.BlockSpec((frames, 2, rows, fine), lambda b: (0, 0, b, 0)),
            pl.BlockSpec((frames, 2, rows, fine), lambda b: (0, 0, b, 0)),
            pl.BlockSpec((taps_count, 8, fine), lambda b: (0, 0, 0)),
            pl.BlockSpec((fine, fine), lambda b: (0, 0)),
            pl.BlockSpec((fine, fine), lambda b: (0, 0)),
        ],
        out_specs=[
            pl.BlockSpec((1, 2, frames, tiles * rows, LANES), lambda b: (b, 0, 0, 0, 0)),
            pl.BlockSpec((1, rows, LANES), lambda b: (b, 0, 0)),
        ],
        out_shape=[
            jax.ShapeDtypeStruct((beams, 2, frames, tiles * rows, LANES), jnp.bfloat16),
            jax.ShapeDtypeStruct((beams, rows, LANES), jnp.float32),
        ],
        scratch_shapes=[
            pltpu.VMEM((history + frames, 2, rows, fine), jnp.float32),
            pltpu.VMEM((2, frames * rows, fine), jnp.float32),
        ],
        name="channelize",
    )(previous, current, wide_taps, cosine, sine)


def spread_matrix(stations, pols, tiles, left):
    shape = (stations, pols, tiles, pols)
    station, p, tile, q = (lax.broadcasted_iota(jnp.int32, shape, axis).reshape(-1) for axis in range(4))
    source = (tile * stations + station) * pols + (p if left else q)
    column = jnp.arange(tiles * stations * pols, dtype=jnp.int32)
    return (source[:, None] == column[None, :]).astype(jnp.bfloat16)


def correlate(out, left, rights, left_scale, right_scale, coarse, coarse_count, block, pols):
    beams, _, frames, rows, _ = left.shape
    _, own, unit, _ = left_scale.shape
    stations = right_scale.shape[1]
    tiles = unit // (pols * pols)
    blocks = len(rights)
    others = own * blocks
    size = own * unit
    spread_left = spread_matrix(own, pols, tiles, True)
    spread_right = spread_matrix(own, pols, tiles, False)
    pair_left, pair_right = PAIRS
    choice = [right if isinstance(right, tuple) else (right,) for right in rights]
    flag = next((right[2] for right in choice if len(right) == 3), 0)
    arrays = [array for right in choice for array in right[:2]]
    scalars = jnp.stack([jnp.asarray(block, jnp.int32), jnp.asarray(flag, jnp.int32)])

    def body(scalar_ref, *refs):
        left_ref, sl_ref, pl_ref, pr_ref = refs[:4]
        right_refs = list(refs[4 : 4 + len(arrays)])
        sr_ref = refs[4 + len(arrays)]
        out_ref, l_ref, r_ref = refs[-3:]

        def spread(matrix_ref, pieces, scale):
            wide = jnp.dot(
                matrix_ref[...], jnp.concatenate(pieces, axis=1), preferred_element_type=jnp.float32
            )
            return [wide[:, i * LANES : (i + 1) * LANES] * scale for i in range(len(pieces))]

        def chosen(index, frame):
            place = sum(min(len(c), 2) for c in choice[:index])
            halves = [right_refs[place][0, o, frame] for o in range(2)]
            if len(choice[index]) == 3:
                second = right_refs[place + 1]
                halves = [jnp.where(scalar_ref[1] == 0, halves[o], second[0, o, frame]) for o in range(2)]
            return halves

        span = PREPARE
        left_scales = sl_ref[0].reshape(size, LANES)
        for first in range(0, frames, span):
            those = range(first, first + span)
            parts = spread(pl_ref, [left_ref[0, o, f] for f in those for o in range(2)], left_scales)
            for frame in those:
                real, imag = parts[2 * (frame - first)], parts[2 * (frame - first) + 1]
                l_ref[frame, 0] = real
                l_ref[frame, 1] = imag
                l_ref[frame, 2] = real + imag
        for index in range(blocks):
            low, high = index * size, (index + 1) * size
            scale = sr_ref[0, index * own : (index + 1) * own].reshape(size, LANES)
            for first in range(0, frames, span):
                those = range(first, first + span)
                parts = spread(pr_ref, [half for f in those for half in chosen(index, f)], scale)
                for frame in those:
                    real, imag = parts[2 * (frame - first)], parts[2 * (frame - first) + 1]
                    r_ref[frame, 0, low:high] = real
                    r_ref[frame, 1, low:high] = imag
                    r_ref[frame, 2, low:high] = real - imag

        left_groups = own // pair_left

        def products(step, carry):
            first_left = (step % left_groups) * pair_left
            first_right = (step // left_groups) * pair_right
            pairs = [(i, j) for i in range(pair_left) for j in range(pair_right)]

            def add_frame(frame, sums):
                lefts = [
                    [l_ref[frame, k, pl.ds((first_left + i) * unit, unit)] for k in range(3)]
                    for i in range(pair_left)
                ]
                result = []
                for j in range(pair_right):
                    right = [r_ref[frame, k, pl.ds((first_right + j) * unit, unit)] for k in range(3)]
                    for i in range(pair_left):
                        for k in range(3):
                            result.append(sums[(j * pair_left + i) * 3 + k] + lefts[i][k] * right[k])
                return tuple(result)

            zeros = tuple(jnp.zeros((unit, LANES), jnp.float32) for _ in range(3 * len(pairs)))
            sums = lax.fori_loop(0, frames, add_frame, zeros, unroll=UNROLL)
            for i, j in pairs:
                rr, ii, mixed = sums[(j * pair_left + i) * 3 : (j * pair_left + i) * 3 + 3]
                out_ref[0, 0, first_left + i, first_right + j, 0] = rr + ii
                out_ref[1, 0, first_left + i, first_right + j, 0] = mixed - rr + ii
            return carry

        lax.fori_loop(0, left_groups * (others // pair_right), products, 0)

    beam_spec = pl.BlockSpec((1, 2, frames, rows, LANES), lambda b, s: (b, 0, 0, 0, 0))
    operands = [left, left_scale, spread_left, spread_right, *arrays, right_scale]
    in_specs = [
        beam_spec,
        pl.BlockSpec((1, own, unit, LANES), lambda b, s: (b, 0, 0, 0)),
        pl.BlockSpec(spread_left.shape, lambda b, s: (0, 0)),
        pl.BlockSpec(spread_right.shape, lambda b, s: (0, 0)),
        *[beam_spec for _ in arrays],
        pl.BlockSpec((1, others, unit, LANES), lambda b, s: (b, s[0] // blocks, 0, 0)),
    ]
    aliases = {}
    if out is not None:
        aliases = {1 + len(operands): 0}
        operands.append(out)
        in_specs.append(pl.BlockSpec(memory_space=pl.ANY))
    shape = (2, coarse_count, own, stations, beams, unit, LANES)
    return pl.pallas_call(
        body,
        grid_spec=pltpu.PrefetchScalarGridSpec(
            num_scalar_prefetch=1,
            grid=(beams,),
            in_specs=in_specs,
            out_specs=pl.BlockSpec(
                (2, 1, own, others, 1, unit, LANES), lambda b, s: (0, coarse, 0, s[0] // blocks, b, 0, 0)
            ),
            scratch_shapes=[
                pltpu.VMEM((frames, 3, size, LANES), jnp.float32),
                pltpu.VMEM((frames, 3, others * unit, LANES), jnp.float32),
            ],
        ),
        out_shape=jax.ShapeDtypeStruct(shape, jnp.float32),
        input_output_aliases=aliases,
    )(scalars, *operands)


def block_weights(maps, weight_table, target, block_stations, share, pols):
    stations, rows = maps[:, 0], maps[:, 1]
    groups = maps.shape[0]
    _, table_rows, coarse, beams = weight_table.shape
    ranks = block_ranks(stations, block_stations, share)
    place = target * share + jnp.arange(share, dtype=jnp.int32)
    chosen = ranks[:, None, :] == place[None, :, None]
    station = jnp.sum(jnp.where(chosen, stations[:, None, :], 0), axis=-1) - target * block_stations
    row = jnp.sum(jnp.where(chosen, rows[:, None, :], 0), axis=-1)
    columns = (groups, 2, share, pols)
    out_rows = (2, beams, block_stations, pols)
    station = jnp.broadcast_to(station[:, None, :, None], columns).reshape(1, -1)
    row = jnp.broadcast_to(row[:, None, :, None], columns).reshape(1, -1)
    part, pol = (lax.broadcasted_iota(jnp.int32, columns, axis).reshape(1, -1) for axis in (1, 3))
    own_station, own_pol = (lax.broadcasted_iota(jnp.int32, out_rows, axis).reshape(-1, 1) for axis in (2, 3))
    term = jnp.arange(2 * table_rows, dtype=jnp.int32)[:, None]
    hot = (term == part * table_rows + row).astype(jnp.bfloat16)
    kept = (station == own_station) & (pol == own_pol)
    real, imag = weight_table[0], weight_table[1]
    mixing = jnp.stack([jnp.concatenate([real, -imag]), jnp.concatenate([imag, real])])
    result = []
    for channel in range(coarse):
        table = mixing[:, :, channel].swapaxes(1, 2)[:, :, None, None]
        table = jnp.broadcast_to(table, out_rows + (2 * table_rows,)).reshape(-1, 2 * table_rows)
        values = jnp.dot(table, hot, preferred_element_type=jnp.float32)
        result.append(jnp.where(kept, values, 0.0).astype(jnp.bfloat16))
    return result


def scales(power, denominator, frames, own_index, tiles):
    inverse = lax.rsqrt(power / denominator + epsilon)
    blocks, beams, own_count, pols = inverse.shape
    inverse = jnp.moveaxis(inverse, 1, 0).reshape(beams, blocks * own_count, pols)
    full = (beams, blocks * own_count, pols, tiles, pols, LANES)
    unit = pols * tiles * pols
    right = jnp.broadcast_to(inverse[:, :, None, None, :, None] / frames, full)
    mine = lax.dynamic_slice_in_dim(inverse, own_index * own_count, own_count, 1)
    left = jnp.broadcast_to(mine[:, :, :, None, None, None], (beams, own_count) + full[2:])
    return left.reshape(beams, own_count, unit, LANES), right.reshape(beams, blocks * own_count, unit, LANES)


def per_device(voltages, fir_taps, station_map, beam_index, weight_table):
    _, coarse_dev, dishes_dev, frames, pols, fine = voltages.shape
    groups = lax.axis_size("stn")
    own_index = lax.axis_index("stn")
    beams = weight_table.shape[3]
    share = dishes_dev // groups
    own_count = STATIONS // groups
    tiles = fine // LANES
    denominator = COARSE * frames * fine
    cosine, sine = dft_tables(fine)
    places = jnp.arange(dishes_dev, dtype=jnp.int32)
    line = groups == 4
    side = own_index // 2 if line else 0
    ranks = block_ranks(station_map, own_count, share)
    ranks = (ranks + 2 * side * share) % dishes_dev
    order = jnp.sum(jnp.where(ranks[None, :] == places[:, None], places[None, :], 0), axis=1)
    maps = jnp.stack([station_map, beam_index])

    def form(weights, sources):
        sums = beam_sums(weights, sources)
        earlier = shifted(sums, "tm", 1)
        formed, lane_power = channelize(earlier, sums, fir_taps, cosine, sine, beams)
        return formed, jnp.sum(lane_power, axis=-1)

    def place_power(power):
        return power.reshape(groups, beams, own_count, pols)

    out = None
    if not line:
        maps = lax.all_gather(maps, "stn")
        weights = block_weights(maps, weight_table, own_index, own_count, share, pols)
        formed, power = [], 0.0
        for coarse in range(coarse_dev):
            blocks = jnp.stack(sort_dishes(voltages, order, coarse, range(groups), share))
            arrived = lax.all_to_all(blocks, "stn", 0, 0, tiled=True)
            own, more = form(weights[coarse], [arrived[g] for g in range(groups)])
            power = power + more
            formed.append((own, lax.all_gather(own, "stn")))
        power = place_power(lax.psum(lax.all_gather(power, "stn"), "chan"))
        left_scale, right_scale = scales(power, denominator, frames, own_index, tiles)
        for coarse in range(coarse_dev):
            own, everyone = formed[coarse]
            rights = [everyone[g] for g in range(groups)]
            out = correlate(out, own, rights, left_scale, right_scale, coarse, coarse_dev, 0, pols)
    else:
        inward, across, outward = [(0, 1), (3, 2)], [(1, 2), (2, 1)], [(1, 0), (2, 3)]
        beyond_one = [(0, 2), (3, 1)]
        inner = (own_index == 1) | (own_index == 2)
        paths = (inward, across, beyond_one)
        known = [maps]
        for path in paths:
            known.append(lax.ppermute(maps, "stn", path))
        maps = jnp.stack(known)
        weights = [
            block_weights(maps, weight_table, 2 * side + step, own_count, share, pols) for step in range(2)
        ]
        steps = [(coarse, step) for coarse in range(coarse_dev) for step in range(2)]
        arrived = []
        for coarse, step in steps:
            index = len(arrived)
            near, far = sort_dishes(voltages, order, coarse, (step, 2 + step), share)
            sources = [near]
            for sent, path in zip((near, far, far), paths):
                sources.append(lax.ppermute(sent, "stn", path))
            arrived.append(sources)
        formed, ends, power = [], [], [0.0, 0.0]
        crossed = [None] * len(steps)
        for index, (coarse, step) in enumerate(steps):
            sources = arrived[index]
            if index:
                _, sources = lax.optimization_barrier((formed[-1], sources))
            own, more = form(weights[step][coarse], sources)
            formed.append(own)
            power[step] = power[step] + more
            ends.append(lax.ppermute(own, "stn", outward))
            if index == 0:
                crossed[0] = lax.ppermute(own, "stn", across)
        power = lax.psum(jnp.stack(power), "chan")
        beyond = lax.ppermute(power, "stn", across)
        beyond, *held = lax.optimization_barrier((beyond, *formed[1:]))
        for index, value in enumerate(held):
            crossed[index + 1] = lax.ppermute(value, "stn", across)
        both = jnp.stack([power, beyond])
        from_inner = lax.ppermute(both, "stn", outward)
        flag = jnp.where(inner, 0, 1)
        odd = own_index % 2 == 1
        from_inner, crossed[0] = lax.optimization_barrier((from_inner, crossed[0]))
        both = jnp.where(inner, both, from_inner)
        power = jnp.where(side == 0, both, both[::-1]).reshape((groups,) + power.shape[1:])
        left_scale, right_scale = scales(place_power(power), denominator, frames, own_index, tiles)
        far_ends, lefts = [], []

        def forward(index):
            far_ends.append(lax.ppermute(crossed[index], "stn", outward))

        def far_part(out, index):
            coarse, step = steps[index]
            far = [(crossed[index], far_ends[index], flag)]
            return correlate(
                out, lefts[coarse], far, left_scale, right_scale, coarse, coarse_dev,
                2 * (1 - side) + step, pols,
            )

        forward(0)
        sent, done = 1, 0
        for coarse in range(coarse_dev):
            low = 2 * coarse
            left = jnp.where(
                inner,
                jnp.where(odd, formed[low + 1], formed[low]),
                jnp.where(odd, ends[low + 1], ends[low]),
            )
            lefts.append(left)
            near = [(formed[low + step], ends[low + step], flag) for step in range(2)]
            out = correlate(out, left, near, left_scale, right_scale, coarse, coarse_dev, 2 * side, pols)
            if sent < len(steps):
                out, crossed[sent] = lax.optimization_barrier((out, crossed[sent]))
                forward(sent)
                sent += 1
        while done < len(steps):
            if sent < len(steps):
                out = far_part(out, done)
                done += 1
                out, crossed[sent] = lax.optimization_barrier((out, crossed[sent]))
                forward(sent)
                sent += 1
            else:
                out = far_part(out, done)
                done += 1
    out = out.reshape(2, coarse_dev, own_count, STATIONS, beams, pols, tiles, pols, LANES)
    out = jnp.swapaxes(out, -3, -2).reshape(2, coarse_dev, own_count, STATIONS, beams, pols, pols, fine)
    return out[None]


def solution(mesh):
    in_specs = (
        P(None, "chan", "stn", "tm", None, None),
        P(),
        P("stn"),
        P("stn"),
        P(None, None, "chan", None),
    )
    out_specs = P("tm", None, "chan", "stn", None, None, None, None, None)
    return jax.shard_map(
        per_device, mesh=mesh, in_specs=in_specs, out_specs=out_specs, check_vma=False
    )
```

time: 1320 us -> 664 us (0.50)
  local copies, waits for them, and re-layouts: 328 us -> 11.7 us
  matrix products: 231 us -> 3.79 us
  waiting for transfers between devices: 571 us -> 358 us
  Pallas kernels: 0 us -> 184 us
  other arithmetic: 154 us -> 16.7 us
  starting transfers between devices: 5.46 us -> 76.1 us
  between operations: 14 us -> 0.65 us
    psum x1 -> x0, waiting for transfers between devices: 564 us -> none  [per_device(): formed = lax.psum(full_sums.astype(jnp.bfloat16), 'stn')]
    ppermute x0 -> x29, waiting for transfers between devices: none -> 358 us  [the longest x1 151 us: per_device(): from_inner = lax.ppermute(both, 'stn', outward)]
    dot_general x9 -> x4, matrix products: 230 us -> 3.79 us  [block_weights(): values = jnp.dot(table, hot, preferred_element_type=jnp.float32)]
    pallas_call x0 -> x18, Pallas kernels: none -> 184 us  [the longest x6 112 us: correlate(): pl.pallas_call(body, grid_spec=pltpu.PrefetchScalarGridSpec(num_scalar_pr...]
    squeeze x6 -> x1, local copies, waits for them, and re-layouts: 136 us -> 0.01 us  [block_weights(): real, imag = (weight_table[0], weight_table[1])]
    convert_element_type x3 -> x2, other arithmetic: 122 us -> 2.48 us  [the longest x1 1.77 us: dft_tables(): jnp.sin(angles).astype(jnp.bfloat16)]
    another operation x9 -> x0, local copies, waits for them, and re-layouts: 112 us -> none  [the longest x2 69.5 us: correlate(): return jnp.stack([vis_re, vis_im]) / frames_dev]
    ppermute x0 -> x29, starting transfers between devices: none -> 69 us  [the longest x12 40.6 us: per_device(): sources.append(lax.ppermute(sent, 'stn', path))]
  transfers between devices with their start and end apart: 2 -> 33, of which waited for: 2 -> 11; matrix products, arithmetic and copies ran while one was open for 0% -> 4% of each run, Pallas kernels for 0% -> 22%
where the time goes in v1:
time: 664 us; the launch traced here: 661 us
  waiting for transfers between devices  358 us (54%)
  Pallas kernels  184 us (28%)
  starting transfers between devices  76.1 us (11%)
  other arithmetic  16.7 us (3%)
  local copies, waits for them, and re-layouts  11.7 us (2%)
  blocking collectives  10.1 us (2%)
    ppermute x1, waiting for transfers between devices, per_device(): from_inner = lax.ppermute(both, 'stn', outward)  151 us
    ppermute x12, waiting for transfers between devices, per_device(): sources.append(lax.ppermute(sent, 'stn', path))  113 us
    pallas_call x6, Pallas kernels, correlate(): pl.pallas_call(body, grid_spec=pltpu.PrefetchScalarGridSpec(num_scalar_pr...  112 us
    ppermute x4, waiting for transfers between devices, forward(): far_ends.append(lax.ppermute(crossed[index], 'stn', outward))  94.9 us
    ppermute x12, starting transfers between devices, per_device(): sources.append(lax.ppermute(sent, 'stn', path))  40.6 us
    pallas_call x4, Pallas kernels, channelize(): pl.pallas_call(body, grid=(beams,), in_specs=[pl.BlockSpec((frames, 2, ro...  37.2 us
    pallas_call x4, Pallas kernels, beam_sums(): pl.pallas_call(body, grid=(frames // frames_step,), in_specs=[pl.BlockSpe...  20.2 us
    pallas_call x4, Pallas kernels, sort_dishes(): pl.pallas_call(body, out_shape=[jax.ShapeDtypeStruct((comps, frames, tile...  14.8 us
  transfers between devices with their start and end apart: 33, of which 11 were waited for; matrix products, arithmetic and copies ran while one was open for 4% of the time, Pallas kernels for 22%

profile of v1, /device:TPU:0, one launch (start us, length us, event | category | flops | bytes accessed | tf_op | source)
XLA Modules:
  0.0 661.4 jit_solution(6225867121160468355)
XLA Ops:
  0.7 6.0 collective-permute-start.2
  10.8 3.8 sort_dishes.4
  15.3 5.8 collective-permute-start.5
  21.8 1.4 collective-permute-start.3
  25.4 40.3 %collective-permute-done.3.refs_1_ = bf16[2,16,2,64,128]{4,3,2,1,0:T(8,128)(2,1)S(1)} collective-permute-done((bf16[2,16,2,64,128]{4,3,2,1,0:T(8,128)(2,1)}, bf16[2,16,2,64,128]{4,3,2,1,0:T(8,128)(2,1)S(1)}, u32[]{:S(2)}, u32[]{:S(2)}) %collective-permute-start.3) | collective-permute-done | bytes 1048608 | tf_op jit(solution)/shard_map/ppermute | solution.py:413
  68.0 5.0 beam_sums.4
  73.0 1.5 collective-permute-start.6
  74.6 3.7 sort_dishes.5
  78.3 4.3 collective-permute-start.7
  82.6 1.6 collective-permute-start.8
  84.2 4.1 collective-permute-start.9
  88.3 1.8 sine_convert_fusion
  92.8 9.3 %channelize.4 = (bf16[8,2,16,32,128]{4,3,2,1,0:T(8,128)(2,1)}, f32[8,16,128]{2,1,0:T(8,128)}) custom-call(bf16[16,2,128,256]{3,2,1,0:T(8,128)(2,1)} %bitcast.106, bf16[16,2,128,256]{3,2,1,0:T(8,128)(2,1)} %bitcast.102, f32[16,8,256]{2,1,0:T(8,128)} %broadcast_in_dim.83.taps_ref, bf16[256,256]{1,0:T(8,128)(2,1)} %get-tuple-element.105.cos_ref, ...), custom_call_target="tpu_custom_call" | custom-call | tf_op jit(solution)/shard_map/channelize/pallas_call | solution.py:152
  102.1 4.3 collective-permute-done.7.refs_1_
  106.4 19.9 %collective-permute-done.9.refs_3_ = bf16[2,16,2,64,128]{4,3,2,1,0:T(8,128)(2,1)} collective-permute-done((bf16[2,16,2,64,128]{4,3,2,1,0:T(8,128)(2,1)}, bf16[2,16,2,64,128]{4,3,2,1,0:T(8,128)(2,1)}, u32[]{:S(2)}, u32[]{:S(2)}) %collective-permute-start.9) | collective-permute-done | bytes 1048608 | tf_op jit(solution)/shard_map/ppermute | solution.py:413
  126.3 5.0 beam_sums.5
  131.3 1.4 collective-permute-start.10
  132.7 3.7 sort_dishes.6
  136.4 5.7 collective-permute-start.11
  142.2 1.7 collective-permute-start.12
  143.9 3.9 collective-permute-start.13
  148.8 1.4 copy-done.4
  150.1 9.3 %channelize.5 = (bf16[8,2,16,32,128]{4,3,2,1,0:T(8,128)(2,1)}, f32[8,16,128]{2,1,0:T(8,128)}) custom-call(bf16[16,2,128,256]{3,2,1,0:T(8,128)(2,1)} %bitcast.108, bf16[16,2,128,256]{3,2,1,0:T(8,128)(2,1)} %bitcast.105, f32[16,8,256]{2,1,0:T(8,128)} %broadcast_in_dim.83.taps_ref, bf16[256,256]{1,0:T(8,128)(2,1)} %get-tuple-element.105.cos_ref, ...), custom_call_target="tpu_custom_call" | custom-call | tf_op jit(solution)/shard_map/channelize/pallas_call | solution.py:152
  159.4 6.5 collective-permute-done.11.refs_1_
  166.0 17.5 %collective-permute-done.13.refs_3_ = bf16[2,16,2,64,128]{4,3,2,1,0:T(8,128)(2,1)} collective-permute-done((bf16[2,16,2,64,128]{4,3,2,1,0:T(8,128)(2,1)}, bf16[2,16,2,64,128]{4,3,2,1,0:T(8,128)(2,1)}, u32[]{:S(2)}, u32[]{:S(2)}) %collective-permute-start.13) | collective-permute-done | bytes 1048608 | tf_op jit(solution)/shard_map/ppermute | solution.py:413
  183.5 5.0 beam_sums.6
  188.5 1.4 collective-permute-start.14
  189.9 3.7 sort_dishes.7
  193.6 5.7 collective-permute-start.15
  199.3 1.7 collective-permute-start.16
  201.0 4.0 collective-permute-start.17
  205.9 1.4 copy-done.3
  207.3 9.3 %channelize.6 = (bf16[8,2,16,32,128]{4,3,2,1,0:T(8,128)(2,1)}, f32[8,16,128]{2,1,0:T(8,128)}) custom-call(bf16[16,2,128,256]{3,2,1,0:T(8,128)(2,1)} %bitcast.107, bf16[16,2,128,256]{3,2,1,0:T(8,128)(2,1)} %bitcast.104, f32[16,8,256]{2,1,0:T(8,128)} %broadcast_in_dim.83.taps_ref, bf16[256,256]{1,0:T(8,128)(2,1)} %get-tuple-element.105.cos_ref, ...), custom_call_target="tpu_custom_call" | custom-call | tf_op jit(solution)/shard_map/channelize/pallas_call | solution.py:152
  216.6 6.5 collective-permute-done.15.refs_1_
  223.1 17.4 %collective-permute-done.17.refs_3_ = bf16[2,16,2,64,128]{4,3,2,1,0:T(8,128)(2,1)} collective-permute-done((bf16[2,16,2,64,128]{4,3,2,1,0:T(8,128)(2,1)}, bf16[2,16,2,64,128]{4,3,2,1,0:T(8,128)(2,1)}, u32[]{:S(2)}, u32[]{:S(2)}) %collective-permute-start.17) | collective-permute-done | bytes 1048608 | tf_op jit(solution)/shard_map/ppermute | solution.py:413
  240.6 5.2 beam_sums.7
  245.8 2.7 collective-permute-start.18
  248.4 2.1 collective-permute-start.23
  251.8 1.3 collective-permute-start.24
  253.1 1.3 collective-permute-start.20
  254.7 9.3 %channelize.7 = (bf16[8,2,16,32,128]{4,3,2,1,0:T(8,128)(2,1)}, f32[8,16,128]{2,1,0:T(8,128)}) custom-call(bf16[16,2,128,256]{3,2,1,0:T(8,128)(2,1)} %bitcast.40.prev_ref, bf16[16,2,128,256]{3,2,1,0:T(8,128)(2,1)} %bitcast.103, f32[16,8,256]{2,1,0:T(8,128)} %broadcast_in_dim.83.taps_ref, bf16[256,256]{1,0:T(8,128)(2,1)} %get-tuple-element.105.cos_ref, ...), custom_call_target="tpu_custom_call" | custom-call | tf_op jit(solution)/shard_map/channelize/pallas_call | solution.py:152
  265.0 10.1 %psum.7 = f32[2,8,16]{2,1,0:T(8,128)S(1)} all-reduce(f32[2,8,16]{2,1,0:T(8,128)S(1)} %pad_maximum_fusion.1), channel_id=1, replica_groups=mesh['tm'=2,'stn'=4,'chan'=4] {'chan'}, use_global_device_ids=true, to_apply=%region_11.12 | all-reduce | flops 256 | bytes 2048 | tf_op jit(solution)/shard_map/psum | solution.py:427
  275.7 1.3 collective-permute-start.19
  277.3 1.3 collective-permute-start.22
  279.3 150.8 %collective-permute-done.22 = f32[2,2,8,16]{3,2,1,0:T(8,128)S(1)} collective-permute-done((f32[2,2,8,16]{3,2,1,0:T(8,128)S(1)}, f32[2,2,8,16]{3,2,1,0:T(8,128)S(1)}, u32[]{:S(2)}, u32[]{:S(2)}) %collective-permute-start.22) | collective-permute-done | bytes 2080 | tf_op jit(solution)/shard_map/ppermute | solution.py:433
  430.1 2.0 collective-permute-start.27
  432.1 2.0 collective-permute-start.28
  434.1 2.0 collective-permute-start.29
  436.1 1.5 collective-permute-start.26
  438.9 4.0 select_select_fusion.refs_0_
  443.3 1.4 broadcast_in_dim.89.refs_8_.refs_6_
  445.5 25.4 %shard_map.55.refs_9_ = f32[2,2,8,32,8,8,128]{6,5,4,3,2,1,0:T(8,128)} custom-call(s32[2]{0:T(128)} %pad_add_fusion.4.scalar_ref, bf16[8,2,16,32,128]{4,3,2,1,0:T(8,128)(2,1)} %select_select_fusion.refs_0_, f32[8,8,8,128]{3,2,1,0:T(8,128)} %broadcast_in_dim.86.refs_1_, bf16[64,32]{1,0:T(8,128)(2,1)} %get-tuple-element.106.refs_2_, ...), custom_call_target="tpu_custom_call" | custom-call | tf_op jit(solution)/shard_map/pallas_call | solution.py:290
  471.0 3.3 select_select_fusion.1.refs_0_
  474.3 25.4 %shard_map.56.refs_7_ = f32[2,2,8,32,8,8,128]{6,5,4,3,2,1,0:T(8,128)} custom-call(s32[2]{0:T(128)} %pad_add_fusion.4.scalar_ref, bf16[8,2,16,32,128]{4,3,2,1,0:T(8,128)(2,1)} %select_select_fusion.1.refs_0_, f32[8,8,8,128]{3,2,1,0:T(8,128)} %broadcast_in_dim.86.refs_1_, bf16[64,32]{1,0:T(8,128)(2,1)} %get-tuple-element.106.refs_2_, ...), custom_call_target="tpu_custom_call", output_to_operand_aliasing={{}: (10, {})} | custom-call | tf_op jit(solution)/shard_map/pallas_call | solution.py:290
  499.7 1.3 collective-permute-start.32
  501.0 1.3 collective-permute-start.31
  502.3 15.3 %shard_map.57.refs_7_ = f32[2,2,8,32,8,8,128]{6,5,4,3,2,1,0:T(8,128)} custom-call(s32[2]{0:T(128)} %pad_add_fusion.3.scalar_ref, bf16[8,2,16,32,128]{4,3,2,1,0:T(8,128)(2,1)} %select_select_fusion.refs_0_, f32[8,8,8,128]{3,2,1,0:T(8,128)} %broadcast_in_dim.86.refs_1_, bf16[64,32]{1,0:T(8,128)(2,1)} %get-tuple-element.106.refs_2_, ...), custom_call_target="tpu_custom_call", output_to_operand_aliasing={{}: (8, {})} | custom-call | tf_op jit(solution)/shard_map/pallas_call | solution.py:290
  519.5 53.9 %collective-permute-done.32.refs_5_ = bf16[8,2,16,32,128]{4,3,2,1,0:T(8,128)(2,1)} collective-permute-done((bf16[8,2,16,32,128]{4,3,2,1,0:T(8,128)(2,1)}, bf16[8,2,16,32,128]{4,3,2,1,0:T(8,128)(2,1)}, u32[]{:S(2)}, u32[]{:S(2)}) %collective-permute-start.32) | collective-permute-done | bytes 2097184 | tf_op jit(solution)/shard_map/ppermute | solution.py:443
  573.4 15.2 %shard_map.58.refs_7_ = f32[2,2,8,32,8,8,128]{6,5,4,3,2,1,0:T(8,128)} custom-call(s32[2]{0:T(128)} %pad_add_fusion.2.scalar_ref, bf16[8,2,16,32,128]{4,3,2,1,0:T(8,128)(2,1)} %select_select_fusion.refs_0_, f32[8,8,8,128]{3,2,1,0:T(8,128)} %broadcast_in_dim.86.refs_1_, bf16[64,32]{1,0:T(8,128)(2,1)} %get-tuple-element.106.refs_2_, ...), custom_call_target="tpu_custom_call", output_to_operand_aliasing={{}: (8, {})} | custom-call | tf_op jit(solution)/shard_map/pallas_call | solution.py:290
  588.6 29.6 %collective-permute-done.31.refs_5_ = bf16[8,2,16,32,128]{4,3,2,1,0:T(8,128)(2,1)S(1)} collective-permute-done((bf16[8,2,16,32,128]{4,3,2,1,0:T(8,128)(2,1)}, bf16[8,2,16,32,128]{4,3,2,1,0:T(8,128)(2,1)S(1)}, u32[]{:S(2)}, u32[]{:S(2)}) %collective-permute-start.31) | collective-permute-done | bytes 2097184 | tf_op jit(solution)/shard_map/ppermute | solution.py:443
  618.2 1.3 copy-done.1
  619.5 15.3 %shard_map.59.refs_7_ = f32[2,2,8,32,8,8,128]{6,5,4,3,2,1,0:T(8,128)} custom-call(s32[2]{0:T(128)} %pad_add_fusion.3.scalar_ref, bf16[8,2,16,32,128]{4,3,2,1,0:T(8,128)(2,1)} %select_select_fusion.1.refs_0_, f32[8,8,8,128]{3,2,1,0:T(8,128)} %broadcast_in_dim.86.refs_1_, bf16[64,32]{1,0:T(8,128)(2,1)} %get-tuple-element.106.refs_2_, ...), custom_call_target="tpu_custom_call", output_to_operand_aliasing={{}: (8, {})} | custom-call | tf_op jit(solution)/shard_map/pallas_call | solution.py:290
  634.8 11.4 %collective-permute-done.30.refs_5_ = bf16[8,2,16,32,128]{4,3,2,1,0:T(8,128)(2,1)} collective-permute-done((bf16[8,2,16,32,128]{4,3,2,1,0:T(8,128)(2,1)}, bf16[8,2,16,32,128]{4,3,2,1,0:T(8,128)(2,1)}, u32[]{:S(2)}, u32[]{:S(2)}) %collective-permute-start.30) | collective-permute-done | bytes 2097184 | tf_op jit(solution)/shard_map/ppermute | solution.py:443
  646.2 15.3 %shard_map.60 = f32[2,2,8,32,8,8,128]{6,5,4,3,2,1,0:T(8,128)} custom-call(s32[2]{0:T(128)} %pad_add_fusion.2.scalar_ref, bf16[8,2,16,32,128]{4,3,2,1,0:T(8,128)(2,1)} %select_select_fusion.1.refs_0_, f32[8,8,8,128]{3,2,1,0:T(8,128)} %broadcast_in_dim.86.refs_1_, bf16[64,32]{1,0:T(8,128)(2,1)} %get-tuple-element.106.refs_2_, ...), custom_call_target="tpu_custom_call", output_to_operand_aliasing={{}: (8, {})} | custom-call | tf_op jit(solution)/shard_map/pallas_call | solution.py:290
  (123 shorter events, 23.7 us)
Async XLA Ops:
  0.7 21.1 %collective-permute-start.2 = (s32[2,128]{1,0:T(2,128)S(1)}, s32[2,128]{1,0:T(2,128)S(1)}, u32[]{:S(2)}, u32[]{:S(2)}) collective-permute-start(s32[2,128]{1,0:T(2,128)S(1)} %pad_add_fusion.1), channel_id=1, source_target_pairs={{0,8},{12,4},{1,9},{13,5},{2,10},{14,6},{3,11},{15,7},{16,24},{28,... | collective-permute-start | bytes 3080 | tf_op jit(solution)/shard_map/ppermute | solution.py:401
  6.6 16.5 %collective-permute-start = (s32[2,128]{1,0:T(2,128)S(1)}, s32[2,128]{1,0:T(2,128)S(1)}, u32[]{:S(2)}, u32[]{:S(2)}) collective-permute-start(s32[2,128]{1,0:T(2,128)S(1)} %pad_add_fusion.1), channel_id=1, source_target_pairs={{0,4},{12,8},{1,5},{13,9},{2,6},{14,10},{3,7},{15,11},{16,20},{28,... | collective-permute-start | bytes 3080 | tf_op jit(solution)/shard_map/ppermute | solution.py:401
  7.9 15.3 %collective-permute-start.1 = (s32[2,128]{1,0:T(2,128)S(1)}, s32[2,128]{1,0:T(2,128)S(1)}, u32[]{:S(2)}, u32[]{:S(2)}) collective-permute-start(s32[2,128]{1,0:T(2,128)S(1)} %pad_add_fusion.1), channel_id=1, source_target_pairs={{4,8},{8,4},{5,9},{9,5},{6,10},{10,6},{7,11},{11,7},{20,24},{24,20... | collective-permute-start | bytes 3080 | tf_op jit(solution)/shard_map/ppermute | solution.py:401
  10.8 10.4 %copy-start.14 = (bf16[2,16,2,8]{1,3,2,0:T(8,128)(2,1)S(1)}, bf16[2,16,2,8]{1,3,2,0:T(8,128)(2,1)}, u32[]{:S(2)}) copy-start(bf16[2,16,2,8]{1,3,2,0:T(8,128)(2,1)} %param.9) | copy-start | bytes 3076
  14.6 51.2 %collective-permute-start.4 = (bf16[2,16,2,64,128]{4,3,2,1,0:T(8,128)(2,1)}, bf16[2,16,2,64,128]{4,3,2,1,0:T(8,128)(2,1)S(1)}, u32[]{:S(2)}, u32[]{:S(2)}) collective-permute-start(bf16[2,16,2,64,128]{4,3,2,1,0:T(8,128)(2,1)} %bitcast.134), channel_id=1, source_target_pairs={{4,8},{8,4},{5,9},{9,5},{6,10},{10,6},{7,11},{11,7},{20,24},{24,20... | collective-permute-start | bytes 3145736 | tf_op jit(solution)/shard_map/ppermute | solution.py:413
  15.3 50.4 %collective-permute-start.5 = (bf16[2,16,2,64,128]{4,3,2,1,0:T(8,128)(2,1)}, bf16[2,16,2,64,128]{4,3,2,1,0:T(8,128)(2,1)S(1)}, u32[]{:S(2)}, u32[]{:S(2)}) collective-permute-start(bf16[2,16,2,64,128]{4,3,2,1,0:T(8,128)(2,1)} %bitcast.135), channel_id=1, source_target_pairs={{0,8},{12,4},{1,9},{13,5},{2,10},{14,6},{3,11},{15,7},{16,24},{28,... | collective-permute-start | bytes 3145736 | tf_op jit(solution)/shard_map/ppermute | solution.py:413
  21.8 44.0 %collective-permute-start.3 = (bf16[2,16,2,64,128]{4,3,2,1,0:T(8,128)(2,1)}, bf16[2,16,2,64,128]{4,3,2,1,0:T(8,128)(2,1)S(1)}, u32[]{:S(2)}, u32[]{:S(2)}) collective-permute-start(bf16[2,16,2,64,128]{4,3,2,1,0:T(8,128)(2,1)} %bitcast.109), channel_id=1, source_target_pairs={{0,4},{12,8},{1,5},{13,9},{2,6},{14,10},{3,7},{15,11},{16,20},{28,... | collective-permute-start | bytes 3145736 | tf_op jit(solution)/shard_map/ppermute | solution.py:413
  65.8 1.0 copy-start.7
  65.8 1.3 copy-start.5
  67.1 1.0 copy-start.6
  73.0 18.4 %copy-start.15 = (f32[16,256]{1,0:T(8,128)S(1)}, f32[16,256]{1,0:T(8,128)}, u32[]{:S(2)}) copy-start(f32[16,256]{1,0:T(8,128)} %param.6) | copy-start | bytes 49156
  73.0 18.4 %collective-permute-start.6 = (bf16[16,256,256]{2,1,0:T(8,128)(2,1)}, bf16[16,256,256]{2,1,0:T(8,128)(2,1)S(1)}, u32[]{:S(2)}, u32[]{:S(2)}) collective-permute-start(bf16[16,256,256]{2,1,0:T(8,128)(2,1)} %beam_sums.4), channel_id=1, source_target_pairs={{0,16},{1,17},{2,18},{3,19},{4,20},{5,21},{6,22},{7,23},{8,24},{9,... | collective-permute-start | bytes 6291464 | tf_op jit(solution)/shard_map/ppermute | solution.py:22
  78.3 28.1 %collective-permute-start.7 = (bf16[2,16,2,64,128]{4,3,2,1,0:T(8,128)(2,1)}, bf16[2,16,2,64,128]{4,3,2,1,0:T(8,128)(2,1)S(1)}, u32[]{:S(2)}, u32[]{:S(2)}) collective-permute-start(bf16[2,16,2,64,128]{4,3,2,1,0:T(8,128)(2,1)} %bitcast.111), channel_id=1, source_target_pairs={{0,4},{12,8},{1,5},{13,9},{2,6},{14,10},{3,7},{15,11},{16,20},{28,... | collective-permute-start | bytes 3145736 | tf_op jit(solution)/shard_map/ppermute | solution.py:413
  82.6 23.8 %collective-permute-start.8 = (bf16[2,16,2,64,128]{4,3,2,1,0:T(8,128)(2,1)}, bf16[2,16,2,64,128]{4,3,2,1,0:T(8,128)(2,1)}, u32[]{:S(2)}, u32[]{:S(2)}) collective-permute-start(bf16[2,16,2,64,128]{4,3,2,1,0:T(8,128)(2,1)} %bitcast.136), channel_id=1, source_target_pairs={{4,8},{8,4},{5,9},{9,5},{6,10},{10,6},{7,11},{11,7},{20,24},{24,20... | collective-permute-start | bytes 3145736 | tf_op jit(solution)/shard_map/ppermute | solution.py:413
  84.2 42.0 %collective-permute-start.9 = (bf16[2,16,2,64,128]{4,3,2,1,0:T(8,128)(2,1)}, bf16[2,16,2,64,128]{4,3,2,1,0:T(8,128)(2,1)}, u32[]{:S(2)}, u32[]{:S(2)}) collective-permute-start(bf16[2,16,2,64,128]{4,3,2,1,0:T(8,128)(2,1)} %bitcast.137), channel_id=1, source_target_pairs={{0,8},{12,4},{1,9},{13,5},{2,10},{14,6},{3,11},{15,7},{16,24},{28,... | collective-permute-start | bytes 3145736 | tf_op jit(solution)/shard_map/ppermute | solution.py:413
  91.4 1.3 copy-start.2
  106.4 19.9 %copy-start.8 = (bf16[2,16,2,64,128]{4,3,2,1,0:T(8,128)(2,1)}, bf16[2,16,2,64,128]{4,3,2,1,0:T(8,128)(2,1)S(1)}, u32[]{:S(2)}) copy-start(bf16[2,16,2,64,128]{4,3,2,1,0:T(8,128)(2,1)S(1)} %collective-permute-done.7.refs_1_) | copy-start | bytes 3145732
  131.3 17.5 %collective-permute-start.10 = (bf16[16,256,256]{2,1,0:T(8,128)(2,1)}, bf16[16,256,256]{2,1,0:T(8,128)(2,1)S(1)}, u32[]{:S(2)}, u32[]{:S(2)}) collective-permute-start(bf16[16,256,256]{2,1,0:T(8,128)(2,1)} %beam_sums.5), channel_id=1, source_target_pairs={{0,16},{1,17},{2,18},{3,19},{4,20},{5,21},{6,22},{7,23},{8,24},{9,... | collective-permute-start | bytes 6291464 | tf_op jit(solution)/shard_map/ppermute | solution.py:22
  136.4 29.5 %collective-permute-start.11 = (bf16[2,16,2,64,128]{4,3,2,1,0:T(8,128)(2,1)}, bf16[2,16,2,64,128]{4,3,2,1,0:T(8,128)(2,1)S(1)}, u32[]{:S(2)}, u32[]{:S(2)}) collective-permute-start(bf16[2,16,2,64,128]{4,3,2,1,0:T(8,128)(2,1)} %bitcast.115), channel_id=1, source_target_pairs={{0,4},{12,8},{1,5},{13,9},{2,6},{14,10},{3,7},{15,11},{16,20},{28,... | collective-permute-start | bytes 3145736 | tf_op jit(solution)/shard_map/ppermute | solution.py:413
  142.2 23.8 %collective-permute-start.12 = (bf16[2,16,2,64,128]{4,3,2,1,0:T(8,128)(2,1)}, bf16[2,16,2,64,128]{4,3,2,1,0:T(8,128)(2,1)}, u32[]{:S(2)}, u32[]{:S(2)}) collective-permute-start(bf16[2,16,2,64,128]{4,3,2,1,0:T(8,128)(2,1)} %bitcast.140), channel_id=1, source_target_pairs={{4,8},{8,4},{5,9},{9,5},{6,10},{10,6},{7,11},{11,7},{20,24},{24,20... | collective-permute-start | bytes 3145736 | tf_op jit(solution)/shard_map/ppermute | solution.py:413
  143.9 39.6 %collective-permute-start.13 = (bf16[2,16,2,64,128]{4,3,2,1,0:T(8,128)(2,1)}, bf16[2,16,2,64,128]{4,3,2,1,0:T(8,128)(2,1)}, u32[]{:S(2)}, u32[]{:S(2)}) collective-permute-start(bf16[2,16,2,64,128]{4,3,2,1,0:T(8,128)(2,1)} %bitcast.141), channel_id=1, source_target_pairs={{0,8},{12,4},{1,9},{13,5},{2,10},{14,6},{3,11},{15,7},{16,24},{28,... | collective-permute-start | bytes 3145736 | tf_op jit(solution)/shard_map/ppermute | solution.py:413
  148.8 1.4 copy-start.4
  166.0 17.5 %copy-start.10 = (bf16[2,16,2,64,128]{4,3,2,1,0:T(8,128)(2,1)}, bf16[2,16,2,64,128]{4,3,2,1,0:T(8,128)(2,1)S(1)}, u32[]{:S(2)}) copy-start(bf16[2,16,2,64,128]{4,3,2,1,0:T(8,128)(2,1)S(1)} %collective-permute-done.11.refs_1_) | copy-start | bytes 3145732
  188.5 17.4 %collective-permute-start.14 = (bf16[16,256,256]{2,1,0:T(8,128)(2,1)}, bf16[16,256,256]{2,1,0:T(8,128)(2,1)S(1)}, u32[]{:S(2)}, u32[]{:S(2)}) collective-permute-start(bf16[16,256,256]{2,1,0:T(8,128)(2,1)} %beam_sums.6), channel_id=1, source_target_pairs={{0,16},{1,17},{2,18},{3,19},{4,20},{5,21},{6,22},{7,23},{8,24},{9,... | collective-permute-start | bytes 6291464 | tf_op jit(solution)/shard_map/ppermute | solution.py:22
  193.6 29.5 %collective-permute-start.15 = (bf16[2,16,2,64,128]{4,3,2,1,0:T(8,128)(2,1)}, bf16[2,16,2,64,128]{4,3,2,1,0:T(8,128)(2,1)S(1)}, u32[]{:S(2)}, u32[]{:S(2)}) collective-permute-start(bf16[2,16,2,64,128]{4,3,2,1,0:T(8,128)(2,1)} %bitcast.113), channel_id=1, source_target_pairs={{0,4},{12,8},{1,5},{13,9},{2,6},{14,10},{3,7},{15,11},{16,20},{28,... | collective-permute-start | bytes 3145736 | tf_op jit(solution)/shard_map/ppermute | solution.py:413
  199.3 23.8 %collective-permute-start.16 = (bf16[2,16,2,64,128]{4,3,2,1,0:T(8,128)(2,1)}, bf16[2,16,2,64,128]{4,3,2,1,0:T(8,128)(2,1)}, u32[]{:S(2)}, u32[]{:S(2)}) collective-permute-start(bf16[2,16,2,64,128]{4,3,2,1,0:T(8,128)(2,1)} %bitcast.138), channel_id=1, source_target_pairs={{4,8},{8,4},{5,9},{9,5},{6,10},{10,6},{7,11},{11,7},{20,24},{24,20... | collective-permute-start | bytes 3145736 | tf_op jit(solution)/shard_map/ppermute | solution.py:413
  201.0 39.6 %collective-permute-start.17 = (bf16[2,16,2,64,128]{4,3,2,1,0:T(8,128)(2,1)}, bf16[2,16,2,64,128]{4,3,2,1,0:T(8,128)(2,1)}, u32[]{:S(2)}, u32[]{:S(2)}) collective-permute-start(bf16[2,16,2,64,128]{4,3,2,1,0:T(8,128)(2,1)} %bitcast.139), channel_id=1, source_target_pairs={{0,8},{12,4},{1,9},{13,5},{2,10},{14,6},{3,11},{15,7},{16,24},{28,... | collective-permute-start | bytes 3145736 | tf_op jit(solution)/shard_map/ppermute | solution.py:413
  205.9 1.4 copy-start.3
  223.1 17.4 %copy-start.9 = (bf16[2,16,2,64,128]{4,3,2,1,0:T(8,128)(2,1)}, bf16[2,16,2,64,128]{4,3,2,1,0:T(8,128)(2,1)S(1)}, u32[]{:S(2)}) copy-start(bf16[2,16,2,64,128]{4,3,2,1,0:T(8,128)(2,1)S(1)} %collective-permute-done.15.refs_1_) | copy-start | bytes 3145732
  240.6 12.5 %copy-start = (bf16[8,2,16,32,128]{4,3,2,1,0:T(8,128)(2,1)S(1)}, bf16[8,2,16,32,128]{4,3,2,1,0:T(8,128)(2,1)}, u32[]{:S(2)}) copy-start(bf16[8,2,16,32,128]{4,3,2,1,0:T(8,128)(2,1)} %get-tuple-element.78.refs_4_) | copy-start | bytes 6291460
  240.6 13.8 %copy-start.11 = (f32[8,16,128]{2,1,0:T(8,128)S(1)}, f32[8,16,128]{2,1,0:T(8,128)}, u32[]{:S(2)}) copy-start(f32[8,16,128]{2,1,0:T(8,128)} %get-tuple-element.69) | copy-start | bytes 196612
  240.6 13.9 %copy-start.12 = (f32[8,16,128]{2,1,0:T(8,128)S(1)}, f32[8,16,128]{2,1,0:T(8,128)}, u32[]{:S(2)}) copy-start(f32[8,16,128]{2,1,0:T(8,128)} %get-tuple-element.71) | copy-start | bytes 196612
  240.6 14.0 %copy-start.13 = (f32[8,16,128]{2,1,0:T(8,128)S(1)}, f32[8,16,128]{2,1,0:T(8,128)}, u32[]{:S(2)}) copy-start(f32[8,16,128]{2,1,0:T(8,128)} %get-tuple-element.70) | copy-start | bytes 196612
  245.8 8.9 %collective-permute-start.18 = (bf16[16,256,256]{2,1,0:T(8,128)(2,1)}, bf16[16,256,256]{2,1,0:T(8,128)(2,1)}, u32[]{:S(2)}, u32[]{:S(2)}) collective-permute-start(bf16[16,256,256]{2,1,0:T(8,128)(2,1)} %beam_sums.7), channel_id=1, source_target_pairs={{0,16},{1,17},{2,18},{3,19},{4,20},{5,21},{6,22},{7,23},{8,24},{9,... | collective-permute-start | bytes 6291464 | tf_op jit(solution)/shard_map/ppermute | solution.py:22
  248.4 28.9 %collective-permute-start.23 = (bf16[8,2,16,32,128]{4,3,2,1,0:T(8,128)(2,1)}, bf16[8,2,16,32,128]{4,3,2,1,0:T(8,128)(2,1)}, u32[]{:S(2)}, u32[]{:S(2)}) collective-permute-start(bf16[8,2,16,32,128]{4,3,2,1,0:T(8,128)(2,1)} %get-tuple-element.47.refs_4_), channel_id=1, source_target_pairs={{4,8},{8,4},{5,9},{9,5},{6,10},{10,6},{7,11},{11,7},{20,24},{24,20... | collective-permute-start | bytes 6291464 | tf_op jit(solution)/shard_map/ppermute | solution.py:426
  250.5 181.7 %collective-permute-start.25 = (bf16[8,2,16,32,128]{4,3,2,1,0:T(8,128)(2,1)}, bf16[8,2,16,32,128]{4,3,2,1,0:T(8,128)(2,1)}, u32[]{:S(2)}, u32[]{:S(2)}) collective-permute-start(bf16[8,2,16,32,128]{4,3,2,1,0:T(8,128)(2,1)} %get-tuple-element.47.refs_4_), channel_id=1, source_target_pairs={{4,0},{8,12},{5,1},{9,13},{6,2},{10,14},{7,3},{11,15},{20,16},{24,... | collective-permute-start | bytes 6291464 | tf_op jit(solution)/shard_map/ppermute | solution.py:424
  251.8 182.3 %collective-permute-start.24 = (bf16[8,2,16,32,128]{4,3,2,1,0:T(8,128)(2,1)}, bf16[8,2,16,32,128]{4,3,2,1,0:T(8,128)(2,1)}, u32[]{:S(2)}, u32[]{:S(2)}) collective-permute-start(bf16[8,2,16,32,128]{4,3,2,1,0:T(8,128)(2,1)} %get-tuple-element.76.refs_6_), channel_id=1, source_target_pairs={{4,0},{8,12},{5,1},{9,13},{6,2},{10,14},{7,3},{11,15},{20,16},{24,... | collective-permute-start | bytes 6291464 | tf_op jit(solution)/shard_map/ppermute | solution.py:424
  253.1 183.1 %collective-permute-start.20 = (bf16[8,2,16,32,128]{4,3,2,1,0:T(8,128)(2,1)S(1)}, bf16[8,2,16,32,128]{4,3,2,1,0:T(8,128)(2,1)}, u32[]{:S(2)}, u32[]{:S(2)}) collective-permute-start(bf16[8,2,16,32,128]{4,3,2,1,0:T(8,128)(2,1)S(1)} %copy-done), channel_id=1, source_target_pairs={{4,0},{8,12},{5,1},{9,13},{6,2},{10,14},{7,3},{11,15},{20,16},{24,... | collective-permute-start | bytes 6291464 | tf_op jit(solution)/shard_map/ppermute | solution.py:424
  275.1 0.7 collective-permute-start.21
  275.7 195.2 %collective-permute-start.19 = (bf16[8,2,16,32,128]{4,3,2,1,0:T(8,128)(2,1)}, bf16[8,2,16,32,128]{4,3,2,1,0:T(8,128)(2,1)}, u32[]{:S(2)}, u32[]{:S(2)}) collective-permute-start(bf16[8,2,16,32,128]{4,3,2,1,0:T(8,128)(2,1)} %get-tuple-element.80.refs_6_), channel_id=1, source_target_pairs={{4,0},{8,12},{5,1},{9,13},{6,2},{10,14},{7,3},{11,15},{20,16},{24,... | collective-permute-start | bytes 6291464 | tf_op jit(solution)/shard_map/ppermute | solution.py:424
  277.3 152.8 %collective-permute-start.22 = (f32[2,2,8,16]{3,2,1,0:T(8,128)S(1)}, f32[2,2,8,16]{3,2,1,0:T(8,128)S(1)}, u32[]{:S(2)}, u32[]{:S(2)}) collective-permute-start(f32[2,2,8,16]{3,2,1,0:T(8,128)S(1)} %pad_maximum_fusion), channel_id=1, source_target_pairs={{4,0},{8,12},{5,1},{9,13},{6,2},{10,14},{7,3},{11,15},{20,16},{24,... | collective-permute-start | bytes 6152 | tf_op jit(solution)/shard_map/ppermute | solution.py:433
  430.1 44.2 %collective-permute-start.27 = (bf16[8,2,16,32,128]{4,3,2,1,0:T(8,128)(2,1)}, bf16[8,2,16,32,128]{4,3,2,1,0:T(8,128)(2,1)}, u32[]{:S(2)}, u32[]{:S(2)}) collective-permute-start(bf16[8,2,16,32,128]{4,3,2,1,0:T(8,128)(2,1)} %get-tuple-element.76.refs_6_), channel_id=1, source_target_pairs={{4,8},{8,4},{5,9},{9,5},{6,10},{10,6},{7,11},{11,7},{20,24},{24,20... | collective-permute-start | bytes 6291464 | tf_op jit(solution)/shard_map/ppermute | solution.py:431
  432.1 67.6 %collective-permute-start.28 = (bf16[8,2,16,32,128]{4,3,2,1,0:T(8,128)(2,1)S(1)}, bf16[8,2,16,32,128]{4,3,2,1,0:T(8,128)(2,1)}, u32[]{:S(2)}, u32[]{:S(2)}) collective-permute-start(bf16[8,2,16,32,128]{4,3,2,1,0:T(8,128)(2,1)S(1)} %copy-done), channel_id=1, source_target_pairs={{4,8},{8,4},{5,9},{9,5},{6,10},{10,6},{7,11},{11,7},{20,24},{24,20... | collective-permute-start | bytes 6291464 | tf_op jit(solution)/shard_map/ppermute | solution.py:431
  434.1 83.5 %collective-permute-start.29 = (bf16[8,2,16,32,128]{4,3,2,1,0:T(8,128)(2,1)}, bf16[8,2,16,32,128]{4,3,2,1,0:T(8,128)(2,1)}, u32[]{:S(2)}, u32[]{:S(2)}) collective-permute-start(bf16[8,2,16,32,128]{4,3,2,1,0:T(8,128)(2,1)} %get-tuple-element.80.refs_6_), channel_id=1, source_target_pairs={{4,8},{8,4},{5,9},{9,5},{6,10},{10,6},{7,11},{11,7},{20,24},{24,20... | collective-permute-start | bytes 6291464 | tf_op jit(solution)/shard_map/ppermute | solution.py:431
  436.1 66.2 %collective-permute-start.26 = (bf16[8,2,16,32,128]{4,3,2,1,0:T(8,128)(2,1)}, bf16[8,2,16,32,128]{4,3,2,1,0:T(8,128)(2,1)}, u32[]{:S(2)}, u32[]{:S(2)}) collective-permute-start(bf16[8,2,16,32,128]{4,3,2,1,0:T(8,128)(2,1)} %collective-permute-done.23.refs_4_), channel_id=1, source_target_pairs={{4,0},{8,12},{5,1},{9,13},{6,2},{10,14},{7,3},{11,15},{20,16},{24,... | collective-permute-start | bytes 6291464 | tf_op jit(solution)/shard_map/ppermute | solution.py:443
  499.7 73.6 %collective-permute-start.32 = (bf16[8,2,16,32,128]{4,3,2,1,0:T(8,128)(2,1)}, bf16[8,2,16,32,128]{4,3,2,1,0:T(8,128)(2,1)}, u32[]{:S(2)}, u32[]{:S(2)}) collective-permute-start(bf16[8,2,16,32,128]{4,3,2,1,0:T(8,128)(2,1)} %collective-permute-done.27.refs_4_), channel_id=1, source_target_pairs={{4,0},{8,12},{5,1},{9,13},{6,2},{10,14},{7,3},{11,15},{20,16},{24,... | collective-permute-start | bytes 6291464 | tf_op jit(solution)/shard_map/ppermute | solution.py:443
  501.0 117.2 %collective-permute-start.31 = (bf16[8,2,16,32,128]{4,3,2,1,0:T(8,128)(2,1)}, bf16[8,2,16,32,128]{4,3,2,1,0:T(8,128)(2,1)S(1)}, u32[]{:S(2)}, u32[]{:S(2)}) collective-permute-start(bf16[8,2,16,32,128]{4,3,2,1,0:T(8,128)(2,1)} %collective-permute-done.28.refs_4_), channel_id=1, source_target_pairs={{4,0},{8,12},{5,1},{9,13},{6,2},{10,14},{7,3},{11,15},{20,16},{24,... | collective-permute-start | bytes 6291464 | tf_op jit(solution)/shard_map/ppermute | solution.py:443
  517.6 128.5 %collective-permute-start.30 = (bf16[8,2,16,32,128]{4,3,2,1,0:T(8,128)(2,1)}, bf16[8,2,16,32,128]{4,3,2,1,0:T(8,128)(2,1)}, u32[]{:S(2)}, u32[]{:S(2)}) collective-permute-start(bf16[8,2,16,32,128]{4,3,2,1,0:T(8,128)(2,1)} %collective-permute-done.29.refs_4_), channel_id=1, source_target_pairs={{4,0},{8,12},{5,1},{9,13},{6,2},{10,14},{7,3},{11,15},{20,16},{24,... | collective-permute-start | bytes 6291464 | tf_op jit(solution)/shard_map/ppermute | solution.py:443
  618.2 1.3 copy-start.1

commit v2 on v1

--- a/solution.py
+++ b/solution.py
@@ -10,6 +10,7 @@
 COARSE = 8
 LANES = 128
 UNROLL = 8
+PARTS = 2
 PREPARE = 4
 PAIRS = (2, 4)
 
@@ -183,9 +184,9 @@
     return (source[:, None] == column[None, :]).astype(jnp.bfloat16)
 
 
-def correlate(out, left, rights, left_scale, right_scale, coarse, coarse_count, block, pols):
-    beams, _, frames, rows, _ = left.shape
-    _, own, unit, _ = left_scale.shape
+def correlate(out, left, rights, left_scale, right_scale, coarse, coarse_count, block, pols, low_beam=0):
+    some_beams, _, frames, rows, _ = left.shape
+    beams, own, unit, _ = left_scale.shape
     stations = right_scale.shape[1]
     tiles = unit // (pols * pols)
     blocks = len(rights)
@@ -275,11 +276,11 @@
     operands = [left, left_scale, spread_left, spread_right, *arrays, right_scale]
     in_specs = [
         beam_spec,
-        pl.BlockSpec((1, own, unit, LANES), lambda b, s: (b, 0, 0, 0)),
+        pl.BlockSpec((1, own, unit, LANES), lambda b, s: (low_beam + b, 0, 0, 0)),
         pl.BlockSpec(spread_left.shape, lambda b, s: (0, 0)),
         pl.BlockSpec(spread_right.shape, lambda b, s: (0, 0)),
         *[beam_spec for _ in arrays],
-        pl.BlockSpec((1, others, unit, LANES), lambda b, s: (b, s[0] // blocks, 0, 0)),
+        pl.BlockSpec((1, others, unit, LANES), lambda b, s: (low_beam + b, s[0] // blocks, 0, 0)),
     ]
     aliases = {}
     if out is not None:
@@ -291,10 +292,11 @@
         body,
         grid_spec=pltpu.PrefetchScalarGridSpec(
             num_scalar_prefetch=1,
-            grid=(beams,),
+            grid=(some_beams,),
             in_specs=in_specs,
             out_specs=pl.BlockSpec(
-                (2, 1, own, others, 1, unit, LANES), lambda b, s: (0, coarse, 0, s[0] // blocks, b, 0, 0)
+                (2, 1, own, others, 1, unit, LANES),
+                lambda b, s: (0, coarse, 0, s[0] // blocks, low_beam + b, 0, 0),
             ),
             scratch_shapes=[
                 pltpu.VMEM((frames, 3, size, LANES), jnp.float32),
@@ -365,7 +367,7 @@
     order = jnp.sum(jnp.where(ranks[None, :] == places[:, None], places[None, :], 0), axis=1)
     maps = jnp.stack([station_map, beam_index])
 
-    def form(weights, sources):
+    def form(weights, sources, beams):
         sums = beam_sums(weights, sources)
         earlier = shifted(sums, "tm", 1)
         formed, lane_power = channelize(earlier, sums, fir_taps, cosine, sine, beams)
@@ -382,7 +384,7 @@
         for coarse in range(coarse_dev):
             blocks = jnp.stack(sort_dishes(voltages, order, coarse, range(groups), share))
             arrived = lax.all_to_all(blocks, "stn", 0, 0, tiled=True)
-            own, more = form(weights[coarse], [arrived[g] for g in range(groups)])
+            own, more = form(weights[coarse], [arrived[g] for g in range(groups)], beams)
             power = power + more
             formed.append((own, lax.all_gather(own, "stn")))
         power = place_power(lax.psum(lax.all_gather(power, "stn"), "chan"))
@@ -400,8 +402,15 @@
         for path in paths:
             known.append(lax.ppermute(maps, "stn", path))
         maps = jnp.stack(known)
+        some = beams // PARTS
         weights = [
-            block_weights(maps, weight_table, 2 * side + step, own_count, share, pols) for step in range(2)
+            [
+                block_weights(
+                    maps, weight_table[..., part * some : (part + 1) * some], 2 * side + step, own_count, share, pols
+                )
+                for part in range(PARTS)
+            ]
+            for step in range(2)
         ]
         steps = [(coarse, step) for coarse in range(coarse_dev) for step in range(2)]
         arrived = []
@@ -412,70 +421,70 @@
             for sent, path in zip((near, far, far), paths):
                 sources.append(lax.ppermute(sent, "stn", path))
             arrived.append(sources)
-        formed, ends, power = [], [], [0.0, 0.0]
-        crossed = [None] * len(steps)
-        for index, (coarse, step) in enumerate(steps):
-            sources = arrived[index]
+        formed, ends, power = {}, {}, [[0.0] * PARTS for _ in range(2)]
+        keys = [(*key, part) for key in steps for part in range(PARTS)]
+        crossed = {}
+        for index, (coarse, step, part) in enumerate(keys):
+            sources = arrived[index // PARTS]
             if index:
-                _, sources = lax.optimization_barrier((formed[-1], sources))
-            own, more = form(weights[step][coarse], sources)
-            formed.append(own)
-            power[step] = power[step] + more
-            ends.append(lax.ppermute(own, "stn", outward))
-            if index == 0:
-                crossed[0] = lax.ppermute(own, "stn", across)
-        power = lax.psum(jnp.stack(power), "chan")
+                _, sources = lax.optimization_barrier((formed[keys[index - 1]], sources))
+            own, more = form(weights[step][part][coarse], sources, some)
+            formed[coarse, step, part] = own
+            power[step][part] = power[step][part] + more
+            ends[coarse, step, part] = lax.ppermute(own, "stn", outward)
+            if index < PARTS:
+                crossed[coarse, step, part] = lax.ppermute(own, "stn", across)
+        power = jnp.stack([jnp.concatenate(parts) for parts in power])
+        power = lax.psum(power, "chan")
         beyond = lax.ppermute(power, "stn", across)
-        beyond, *held = lax.optimization_barrier((beyond, *formed[1:]))
-        for index, value in enumerate(held):
-            crossed[index + 1] = lax.ppermute(value, "stn", across)
+        beyond, *held = lax.optimization_barrier((beyond, *[formed[key] for key in keys[PARTS:]]))
+        for index, value in enumerate(held, PARTS):
+            crossed[keys[index]] = lax.ppermute(value, "stn", across)
         both = jnp.stack([power, beyond])
         from_inner = lax.ppermute(both, "stn", outward)
         flag = jnp.where(inner, 0, 1)
         odd = own_index % 2 == 1
-        from_inner, crossed[0] = lax.optimization_barrier((from_inner, crossed[0]))
+        held = [crossed[key] for key in keys[:PARTS]] + [ends[key] for key in keys]
+        from_inner, *held = lax.optimization_barrier((from_inner, *held))
+        crossed.update(zip(keys[:PARTS], held))
+        ends = dict(zip(keys, held[PARTS:]))
         both = jnp.where(inner, both, from_inner)
         power = jnp.where(side == 0, both, both[::-1]).reshape((groups,) + power.shape[1:])
         left_scale, right_scale = scales(place_power(power), denominator, frames, own_index, tiles)
-        far_ends, lefts = [], []
+        far_ends, lefts = {}, {}
 
         def forward(index):
-            far_ends.append(lax.ppermute(crossed[index], "stn", outward))
-
-        def far_part(out, index):
-            coarse, step = steps[index]
-            far = [(crossed[index], far_ends[index], flag)]
+            far_ends[keys[index]] = lax.ppermute(crossed[keys[index]], "stn", outward)
+
+        def near_work(out, coarse, part):
+            lefts[coarse, part] = jnp.where(
+                inner,
+                jnp.where(odd, formed[coarse, 1, part], formed[coarse, 0, part]),
+                jnp.where(odd, ends[coarse, 1, part], ends[coarse, 0, part]),
+            )
+            near = [(formed[coarse, step, part], ends[coarse, step, part], flag) for step in range(2)]
             return correlate(
-                out, lefts[coarse], far, left_scale, right_scale, coarse, coarse_dev,
-                2 * (1 - side) + step, pols,
+                out, lefts[coarse, part], near, left_scale, right_scale, coarse, coarse_dev,
+                2 * side, pols, part * some,
             )
 
-        forward(0)
-        sent, done = 1, 0
-        for coarse in range(coarse_dev):
-            low = 2 * coarse
-            left = jnp.where(
-                inner,
-                jnp.where(odd, formed[low + 1], formed[low]),
-                jnp.where(odd, ends[low + 1], ends[low]),
+        def far_work(out, coarse, step, part):
+            far = [(crossed[coarse, step, part], far_ends[coarse, step, part], flag)]
+            return correlate(
+                out, lefts[coarse, part], far, left_scale, right_scale, coarse, coarse_dev,
+                2 * (1 - side) + step, pols, part * some,
             )
-            lefts.append(left)
-            near = [(formed[low + step], ends[low + step], flag) for step in range(2)]
-            out = correlate(out, left, near, left_scale, right_scale, coarse, coarse_dev, 2 * side, pols)
-            if sent < len(steps):
-                out, crossed[sent] = lax.optimization_barrier((out, crossed[sent]))
+
+        work = [(near_work, (coarse, part)) for coarse in range(coarse_dev) for part in range(PARTS)]
+        work += [(far_work, key) for key in keys]
+        for index in range(PARTS):
+            forward(index)
+        for index, (make, which) in enumerate(work):
+            out = make(out, *which)
+            sent = index + PARTS
+            if sent < len(keys):
+                out, crossed[keys[sent]] = lax.optimization_barrier((out, crossed[keys[sent]]))
                 forward(sent)
-                sent += 1
-        while done < len(steps):
-            if sent < len(steps):
-                out = far_part(out, done)
-                done += 1
-                out, crossed[sent] = lax.optimization_barrier((out, crossed[sent]))
-                forward(sent)
-                sent += 1
-            else:
-                out = far_part(out, done)
-                done += 1
     out = out.reshape(2, coarse_dev, own_count, STATIONS, beams, pols, tiles, pols, LANES)
     out = jnp.swapaxes(out, -3, -2).reshape(2, coarse_dev, own_count, STATIONS, beams, pols, pols, fine)
     return out[None]

time: 664 us -> 716 us (1.078)
  Pallas kernels: 184 us -> 223 us
  waiting for transfers between devices: 358 us -> 335 us
  starting transfers between devices: 76.1 us -> 96.8 us
    ppermute x1, waiting for transfers between devices: 151 us -> 18.6 us  [per_device(): from_inner = lax.ppermute(both, 'stn', outward)]
    ppermute x12 -> x24, waiting for transfers between devices: 94.9 us -> 183 us  [the longest x8 126 us: per_device(): ends[coarse, step, part] = lax.ppermute(own, 'stn', outward)]
    ppermute x12, waiting for transfers between devices: 113 us -> 134 us  [per_device(): sources.append(lax.ppermute(sent, 'stn', path))]
    pallas_call x6 -> x12, Pallas kernels: 112 us -> 129 us  [correlate(): pl.pallas_call(body, grid_spec=pltpu.PrefetchScalarGridSpec(num_scalar_pr...]
    pallas_call x4 -> x8, Pallas kernels: 20.2 us -> 36.5 us  [beam_sums(): pl.pallas_call(body, grid=(frames // frames_step,), in_specs=[pl.BlockSpe...]
    ppermute x12 -> x24, starting transfers between devices: 18.6 us -> 34.1 us  [the longest x8 10.5 us: forward(): far_ends[keys[index]] = lax.ppermute(crossed[keys[index]], 'stn', outward)]
    ppermute x4 -> x8, starting transfers between devices: 7.03 us -> 14.7 us  [shifted(): lax.ppermute(value, axis, [(source, source + steps) for source in range(f...]
    pallas_call x4 -> x8, Pallas kernels: 37.2 us -> 43.3 us  [channelize(): pl.pallas_call(body, grid=(beams,), in_specs=[pl.BlockSpec((frames, 2, ro...]
  transfers between devices with their start and end apart: 33 -> 49, of which waited for: 11 -> 21; matrix products, arithmetic and copies ran while one was open for 4% -> 5% of each run, Pallas kernels for 22% -> 22%
where the time goes in v2:
time: 716 us; the launch traced here: 712 us
  waiting for transfers between devices  335 us (47%)
  Pallas kernels  223 us (31%)
  starting transfers between devices  96.8 us (14%)
  other arithmetic  22.9 us (3%)
  local copies, waits for them, and re-layouts  16.5 us (2%)
  blocking collectives  10.1 us (1%)
    ppermute x12, waiting for transfers between devices, per_device(): sources.append(lax.ppermute(sent, 'stn', path))  134 us
    pallas_call x12, Pallas kernels, correlate(): pl.pallas_call(body, grid_spec=pltpu.PrefetchScalarGridSpec(num_scalar_pr...  129 us
    ppermute x8, waiting for transfers between devices, per_device(): ends[coarse, step, part] = lax.ppermute(own, 'stn', outward)  126 us
    ppermute x8, waiting for transfers between devices, forward(): far_ends[keys[index]] = lax.ppermute(crossed[keys[index]], 'stn', outward)  56.5 us
    pallas_call x8, Pallas kernels, channelize(): pl.pallas_call(body, grid=(beams,), in_specs=[pl.BlockSpec((frames, 2, ro...  43.3 us
    ppermute x12, starting transfers between devices, per_device(): sources.append(lax.ppermute(sent, 'stn', path))  38.2 us
    pallas_call x8, Pallas kernels, beam_sums(): pl.pallas_call(body, grid=(frames // frames_step,), in_specs=[pl.BlockSpe...  36.5 us
    ppermute x1, waiting for transfers between devices, per_device(): from_inner = lax.ppermute(both, 'stn', outward)  18.6 us
  transfers between devices with their start and end apart: 49, of which 21 were waited for; matrix products, arithmetic and copies ran while one was open for 5% of the time, Pallas kernels for 22%

profile of v2, /device:TPU:0, one launch (start us, length us, event | category | flops | bytes accessed | tf_op | source)
XLA Modules:
  0.0 712.0 jit_solution(6305609634311328488)
XLA Ops:
  0.7 6.0 collective-permute-start.2
  10.8 3.6 sort_dishes.4
  15.1 5.8 collective-permute-start.5
  26.6 39.0 %collective-permute-done.3.refs_1_ = bf16[2,16,2,64,128]{4,3,2,1,0:T(8,128)(2,1)S(1)} collective-permute-done((bf16[2,16,2,64,128]{4,3,2,1,0:T(8,128)(2,1)}, bf16[2,16,2,64,128]{4,3,2,1,0:T(8,128)(2,1)S(1)}, u32[]{:S(2)}, u32[]{:S(2)}) %collective-permute-start.3) | collective-permute-done | bytes 1048608 | tf_op jit(solution)/shard_map/ppermute | solution.py:422
  67.9 4.5 beam_sums.8
  73.8 3.6 sort_dishes.5
  81.5 5.4 channelize.8
  86.9 4.6 beam_sums.9
  93.0 4.3 collective-permute-start.8
  102.5 5.4 channelize.9
  108.0 13.1 %collective-permute-done.8.refs_1_ = bf16[2,16,2,64,128]{4,3,2,1,0:T(8,128)(2,1)S(1)} collective-permute-done((bf16[2,16,2,64,128]{4,3,2,1,0:T(8,128)(2,1)}, bf16[2,16,2,64,128]{4,3,2,1,0:T(8,128)(2,1)S(1)}, u32[]{:S(2)}, u32[]{:S(2)}) %collective-permute-start.8) | collective-permute-done | bytes 1048608 | tf_op jit(solution)/shard_map/ppermute | solution.py:422
  121.1 19.9 %collective-permute-done.10.refs_3_ = bf16[2,16,2,64,128]{4,3,2,1,0:T(8,128)(2,1)S(1)} collective-permute-done((bf16[2,16,2,64,128]{4,3,2,1,0:T(8,128)(2,1)}, bf16[2,16,2,64,128]{4,3,2,1,0:T(8,128)(2,1)S(1)}, u32[]{:S(2)}, u32[]{:S(2)}) %collective-permute-start.10) | collective-permute-done | bytes 1048608 | tf_op jit(solution)/shard_map/ppermute | solution.py:422
  142.0 4.5 beam_sums.10
  147.9 3.6 sort_dishes.6
  153.3 5.4 channelize.10
  158.8 4.6 beam_sums.11
  164.7 6.0 collective-permute-start.13
  172.4 3.9 collective-permute-start.15
  178.1 5.4 channelize.11
  183.6 10.9 %collective-permute-done.13.refs_1_ = bf16[2,16,2,64,128]{4,3,2,1,0:T(8,128)(2,1)S(1)} collective-permute-done((bf16[2,16,2,64,128]{4,3,2,1,0:T(8,128)(2,1)}, bf16[2,16,2,64,128]{4,3,2,1,0:T(8,128)(2,1)S(1)}, u32[]{:S(2)}, u32[]{:S(2)}) %collective-permute-start.13) | collective-permute-done | bytes 1048608 | tf_op jit(solution)/shard_map/ppermute | solution.py:422
  194.5 19.8 %collective-permute-done.15.refs_3_ = bf16[2,16,2,64,128]{4,3,2,1,0:T(8,128)(2,1)} collective-permute-done((bf16[2,16,2,64,128]{4,3,2,1,0:T(8,128)(2,1)}, bf16[2,16,2,64,128]{4,3,2,1,0:T(8,128)(2,1)}, u32[]{:S(2)}, u32[]{:S(2)}) %collective-permute-start.15) | collective-permute-done | bytes 1048608 | tf_op jit(solution)/shard_map/ppermute | solution.py:422
  214.3 4.5 beam_sums.12
  220.2 3.6 sort_dishes.7
  225.7 5.4 channelize.12
  231.1 4.6 beam_sums.13
  237.9 5.7 collective-permute-start.18
  245.4 3.9 collective-permute-start.20
  250.1 5.4 channelize.13
  255.5 11.9 %collective-permute-done.18.refs_1_ = bf16[2,16,2,64,128]{4,3,2,1,0:T(8,128)(2,1)S(1)} collective-permute-done((bf16[2,16,2,64,128]{4,3,2,1,0:T(8,128)(2,1)}, bf16[2,16,2,64,128]{4,3,2,1,0:T(8,128)(2,1)S(1)}, u32[]{:S(2)}, u32[]{:S(2)}) %collective-permute-start.18) | collective-permute-done | bytes 1048608 | tf_op jit(solution)/shard_map/ppermute | solution.py:422
  267.4 18.9 %collective-permute-done.20.refs_3_ = bf16[2,16,2,64,128]{4,3,2,1,0:T(8,128)(2,1)} collective-permute-done((bf16[2,16,2,64,128]{4,3,2,1,0:T(8,128)(2,1)}, bf16[2,16,2,64,128]{4,3,2,1,0:T(8,128)(2,1)}, u32[]{:S(2)}, u32[]{:S(2)}) %collective-permute-start.20) | collective-permute-done | bytes 1048608 | tf_op jit(solution)/shard_map/ppermute | solution.py:422
  286.3 4.6 beam_sums.14
  294.9 5.4 channelize.14
  300.2 4.6 beam_sums.15
  304.8 3.2 collective-permute-start.22
  318.3 5.4 channelize.15
  325.9 10.1 %psum.7 = f32[2,8,16]{2,1,0:T(8,128)S(1)} all-reduce(f32[2,8,16]{2,1,0:T(8,128)S(1)} %pad_maximum_fusion.1), channel_id=1, replica_groups=mesh['tm'=2,'stn'=4,'chan'=4] {'chan'}, use_global_device_ids=true, to_apply=%region_15.16 | all-reduce | flops 256 | bytes 2048 | tf_op jit(solution)/shard_map/psum | solution.py:438
  335.9 3.8 collective-permute-done.27.refs_5_
  341.7 20.5 %collective-permute-done.28.refs_5_ = bf16[4,2,16,32,128]{4,3,2,1,0:T(8,128)(2,1)} collective-permute-done((bf16[4,2,16,32,128]{4,3,2,1,0:T(8,128)(2,1)S(1)}, bf16[4,2,16,32,128]{4,3,2,1,0:T(8,128)(2,1)}, u32[]{:S(2)}, u32[]{:S(2)}) %collective-permute-start.28) | collective-permute-done | bytes 1048608 | tf_op jit(solution)/shard_map/ppermute | solution.py:434
  363.5 21.2 %collective-permute-done.29.refs_7_ = bf16[4,2,16,32,128]{4,3,2,1,0:T(8,128)(2,1)} collective-permute-done((bf16[4,2,16,32,128]{4,3,2,1,0:T(8,128)(2,1)}, bf16[4,2,16,32,128]{4,3,2,1,0:T(8,128)(2,1)}, u32[]{:S(2)}, u32[]{:S(2)}) %collective-permute-start.29) | collective-permute-done | bytes 1048608 | tf_op jit(solution)/shard_map/ppermute | solution.py:434
  389.0 18.2 %collective-permute-done.30.refs_7_ = bf16[4,2,16,32,128]{4,3,2,1,0:T(8,128)(2,1)} collective-permute-done((bf16[4,2,16,32,128]{4,3,2,1,0:T(8,128)(2,1)S(1)}, bf16[4,2,16,32,128]{4,3,2,1,0:T(8,128)(2,1)}, u32[]{:S(2)}, u32[]{:S(2)}) %collective-permute-start.30) | collective-permute-done | bytes 1048608 | tf_op jit(solution)/shard_map/ppermute | solution.py:434
  409.1 20.6 %collective-permute-done.31.refs_5_ = bf16[4,2,16,32,128]{4,3,2,1,0:T(8,128)(2,1)} collective-permute-done((bf16[4,2,16,32,128]{4,3,2,1,0:T(8,128)(2,1)}, bf16[4,2,16,32,128]{4,3,2,1,0:T(8,128)(2,1)}, u32[]{:S(2)}, u32[]{:S(2)}) %collective-permute-start.31) | collective-permute-done | bytes 1048608 | tf_op jit(solution)/shard_map/ppermute | solution.py:434
  431.3 20.8 %collective-permute-done.32.refs_5_ = bf16[4,2,16,32,128]{4,3,2,1,0:T(8,128)(2,1)} collective-permute-done((bf16[4,2,16,32,128]{4,3,2,1,0:T(8,128)(2,1)}, bf16[4,2,16,32,128]{4,3,2,1,0:T(8,128)(2,1)}, u32[]{:S(2)}, u32[]{:S(2)}) %collective-permute-start.32) | collective-permute-done | bytes 1048608 | tf_op jit(solution)/shard_map/ppermute | solution.py:434
  453.7 20.8 %collective-permute-done.33.refs_7_ = bf16[4,2,16,32,128]{4,3,2,1,0:T(8,128)(2,1)} collective-permute-done((bf16[4,2,16,32,128]{4,3,2,1,0:T(8,128)(2,1)}, bf16[4,2,16,32,128]{4,3,2,1,0:T(8,128)(2,1)}, u32[]{:S(2)}, u32[]{:S(2)}) %collective-permute-start.33) | collective-permute-done | bytes 1048608 | tf_op jit(solution)/shard_map/ppermute | solution.py:434
  476.2 18.6 %collective-permute-done.24 = f32[2,2,8,16]{3,2,1,0:T(8,128)S(1)} collective-permute-done((f32[2,2,8,16]{3,2,1,0:T(8,128)S(1)}, f32[2,2,8,16]{3,2,1,0:T(8,128)S(1)}, u32[]{:S(2)}, u32[]{:S(2)}) %collective-permute-start.24) | collective-permute-done | bytes 2080 | tf_op jit(solution)/shard_map/ppermute | solution.py:444
  498.6 2.7 select_select_fusion.1.refs_0_
  503.4 14.2 %shard_map.55.refs_9_ = f32[2,2,8,32,8,8,128]{6,5,4,3,2,1,0:T(8,128)} custom-call(s32[2]{0:T(128)} %pad_add_fusion.4.scalar_ref, bf16[4,2,16,32,128]{4,3,2,1,0:T(8,128)(2,1)} %select_select_fusion.1.refs_0_, f32[8,8,8,128]{3,2,1,0:T(8,128)} %broadcast_in_dim.112.refs_1_, bf16[64,32]{1,0:T(8,128)(2,1)} %get-tuple-element.200.refs_2_, ...), custom_call_target="tpu_custom_call" | custom-call | tf_op jit(solution)/shard_map/pallas_call | solution.py:291
  523.2 2.4 select_select_fusion.2.refs_0_
  528.0 2.7 select_select_fusion.3.refs_0_
  530.7 14.3 %shard_map.56.refs_9_ = f32[2,2,8,32,8,8,128]{6,5,4,3,2,1,0:T(8,128)} custom-call(s32[2]{0:T(128)} %pad_add_fusion.4.scalar_ref, bf16[4,2,16,32,128]{4,3,2,1,0:T(8,128)(2,1)} %select_select_fusion.2.refs_0_, f32[8,8,8,128]{3,2,1,0:T(8,128)} %broadcast_in_dim.112.refs_1_, bf16[64,32]{1,0:T(8,128)(2,1)} %get-tuple-element.200.refs_2_, ...), custom_call_target="tpu_custom_call", output_to_operand_aliasing={{}: (10, {})} | custom-call | tf_op jit(solution)/shard_map/pallas_call | solution.py:291
  545.0 14.2 %shard_map.57.refs_9_ = f32[2,2,8,32,8,8,128]{6,5,4,3,2,1,0:T(8,128)} custom-call(s32[2]{0:T(128)} %pad_add_fusion.4.scalar_ref, bf16[4,2,16,32,128]{4,3,2,1,0:T(8,128)(2,1)} %select_select_fusion.refs_0_, f32[8,8,8,128]{3,2,1,0:T(8,128)} %broadcast_in_dim.112.refs_1_, bf16[64,32]{1,0:T(8,128)(2,1)} %get-tuple-element.200.refs_2_, ...), custom_call_target="tpu_custom_call", output_to_operand_aliasing={{}: (10, {})} | custom-call | tf_op jit(solution)/shard_map/pallas_call | solution.py:291
  559.2 14.4 %shard_map.58.refs_7_ = f32[2,2,8,32,8,8,128]{6,5,4,3,2,1,0:T(8,128)} custom-call(s32[2]{0:T(128)} %pad_add_fusion.4.scalar_ref, bf16[4,2,16,32,128]{4,3,2,1,0:T(8,128)(2,1)} %select_select_fusion.3.refs_0_, f32[8,8,8,128]{3,2,1,0:T(8,128)} %broadcast_in_dim.112.refs_1_, bf16[64,32]{1,0:T(8,128)(2,1)} %get-tuple-element.200.refs_2_, ...), custom_call_target="tpu_custom_call", output_to_operand_aliasing={{}: (10, {})} | custom-call | tf_op jit(solution)/shard_map/pallas_call | solution.py:291
  574.9 8.9 %shard_map.59.refs_7_ = f32[2,2,8,32,8,8,128]{6,5,4,3,2,1,0:T(8,128)} custom-call(s32[2]{0:T(128)} %pad_add_fusion.3.scalar_ref, bf16[4,2,16,32,128]{4,3,2,1,0:T(8,128)(2,1)} %select_select_fusion.1.refs_0_, f32[8,8,8,128]{3,2,1,0:T(8,128)} %broadcast_in_dim.112.refs_1_, bf16[64,32]{1,0:T(8,128)(2,1)} %get-tuple-element.200.refs_2_, ...), custom_call_target="tpu_custom_call", output_to_operand_aliasing={{}: (8, {})} | custom-call | tf_op jit(solution)/shard_map/pallas_call | solution.py:291
  586.4 9.0 %shard_map.60.refs_7_ = f32[2,2,8,32,8,8,128]{6,5,4,3,2,1,0:T(8,128)} custom-call(s32[2]{0:T(128)} %pad_add_fusion.3.scalar_ref, bf16[4,2,16,32,128]{4,3,2,1,0:T(8,128)(2,1)} %select_select_fusion.2.refs_0_, f32[8,8,8,128]{3,2,1,0:T(8,128)} %broadcast_in_dim.112.refs_1_, bf16[64,32]{1,0:T(8,128)(2,1)} %get-tuple-element.200.refs_2_, ...), custom_call_target="tpu_custom_call", output_to_operand_aliasing={{}: (8, {})} | custom-call | tf_op jit(solution)/shard_map/pallas_call | solution.py:291
  598.8 8.9 %shard_map.61.refs_7_ = f32[2,2,8,32,8,8,128]{6,5,4,3,2,1,0:T(8,128)} custom-call(s32[2]{0:T(128)} %pad_add_fusion.2.scalar_ref, bf16[4,2,16,32,128]{4,3,2,1,0:T(8,128)(2,1)} %select_select_fusion.1.refs_0_, f32[8,8,8,128]{3,2,1,0:T(8,128)} %broadcast_in_dim.112.refs_1_, bf16[64,32]{1,0:T(8,128)(2,1)} %get-tuple-element.200.refs_2_, ...), custom_call_target="tpu_custom_call", output_to_operand_aliasing={{}: (8, {})} | custom-call | tf_op jit(solution)/shard_map/pallas_call | solution.py:291
  607.8 8.4 %collective-permute-done.47.refs_5_ = bf16[4,2,16,32,128]{4,3,2,1,0:T(8,128)(2,1)S(1)} collective-permute-done((bf16[4,2,16,32,128]{4,3,2,1,0:T(8,128)(2,1)}, bf16[4,2,16,32,128]{4,3,2,1,0:T(8,128)(2,1)S(1)}, u32[]{:S(2)}, u32[]{:S(2)}) %collective-permute-start.47) | collective-permute-done | bytes 1048608 | tf_op jit(solution)/shard_map/ppermute | solution.py:457
  617.1 9.0 %shard_map.62.refs_7_ = f32[2,2,8,32,8,8,128]{6,5,4,3,2,1,0:T(8,128)} custom-call(s32[2]{0:T(128)} %pad_add_fusion.2.scalar_ref, bf16[4,2,16,32,128]{4,3,2,1,0:T(8,128)(2,1)} %select_select_fusion.2.refs_0_, f32[8,8,8,128]{3,2,1,0:T(8,128)} %broadcast_in_dim.112.refs_1_, bf16[64,32]{1,0:T(8,128)(2,1)} %get-tuple-element.200.refs_2_, ...), custom_call_target="tpu_custom_call", output_to_operand_aliasing={{}: (8, {})} | custom-call | tf_op jit(solution)/shard_map/pallas_call | solution.py:291
  626.1 12.6 %collective-permute-done.46.refs_5_ = bf16[4,2,16,32,128]{4,3,2,1,0:T(8,128)(2,1)} collective-permute-done((bf16[4,2,16,32,128]{4,3,2,1,0:T(8,128)(2,1)}, bf16[4,2,16,32,128]{4,3,2,1,0:T(8,128)(2,1)}, u32[]{:S(2)}, u32[]{:S(2)}) %collective-permute-start.46) | collective-permute-done | bytes 1048608 | tf_op jit(solution)/shard_map/ppermute | solution.py:457
  638.7 8.9 %shard_map.63.refs_7_ = f32[2,2,8,32,8,8,128]{6,5,4,3,2,1,0:T(8,128)} custom-call(s32[2]{0:T(128)} %pad_add_fusion.3.scalar_ref, bf16[4,2,16,32,128]{4,3,2,1,0:T(8,128)(2,1)} %select_select_fusion.refs_0_, f32[8,8,8,128]{3,2,1,0:T(8,128)} %broadcast_in_dim.112.refs_1_, bf16[64,32]{1,0:T(8,128)(2,1)} %get-tuple-element.200.refs_2_, ...), custom_call_target="tpu_custom_call", output_to_operand_aliasing={{}: (8, {})} | custom-call | tf_op jit(solution)/shard_map/pallas_call | solution.py:291
  647.6 13.5 %collective-permute-done.45.refs_5_ = bf16[4,2,16,32,128]{4,3,2,1,0:T(8,128)(2,1)S(1)} collective-permute-done((bf16[4,2,16,32,128]{4,3,2,1,0:T(8,128)(2,1)}, bf16[4,2,16,32,128]{4,3,2,1,0:T(8,128)(2,1)S(1)}, u32[]{:S(2)}, u32[]{:S(2)}) %collective-permute-start.45) | collective-permute-done | bytes 1048608 | tf_op jit(solution)/shard_map/ppermute | solution.py:457
  662.0 9.0 %shard_map.64.refs_7_ = f32[2,2,8,32,8,8,128]{6,5,4,3,2,1,0:T(8,128)} custom-call(s32[2]{0:T(128)} %pad_add_fusion.3.scalar_ref, bf16[4,2,16,32,128]{4,3,2,1,0:T(8,128)(2,1)} %select_select_fusion.3.refs_0_, f32[8,8,8,128]{3,2,1,0:T(8,128)} %broadcast_in_dim.112.refs_1_, bf16[64,32]{1,0:T(8,128)(2,1)} %get-tuple-element.200.refs_2_, ...), custom_call_target="tpu_custom_call", output_to_operand_aliasing={{}: (8, {})} | custom-call | tf_op jit(solution)/shard_map/pallas_call | solution.py:291
  671.0 12.6 %collective-permute-done.44.refs_5_ = bf16[4,2,16,32,128]{4,3,2,1,0:T(8,128)(2,1)} collective-permute-done((bf16[4,2,16,32,128]{4,3,2,1,0:T(8,128)(2,1)}, bf16[4,2,16,32,128]{4,3,2,1,0:T(8,128)(2,1)}, u32[]{:S(2)}, u32[]{:S(2)}) %collective-permute-start.44) | collective-permute-done | bytes 1048608 | tf_op jit(solution)/shard_map/ppermute | solution.py:457
  683.6 8.9 %shard_map.65.refs_7_ = f32[2,2,8,32,8,8,128]{6,5,4,3,2,1,0:T(8,128)} custom-call(s32[2]{0:T(128)} %pad_add_fusion.2.scalar_ref, bf16[4,2,16,32,128]{4,3,2,1,0:T(8,128)(2,1)} %select_select_fusion.refs_0_, f32[8,8,8,128]{3,2,1,0:T(8,128)} %broadcast_in_dim.112.refs_1_, bf16[64,32]{1,0:T(8,128)(2,1)} %get-tuple-element.200.refs_2_, ...), custom_call_target="tpu_custom_call", output_to_operand_aliasing={{}: (8, {})} | custom-call | tf_op jit(solution)/shard_map/pallas_call | solution.py:291
  692.5 9.5 %collective-permute-done.43.refs_5_ = bf16[4,2,16,32,128]{4,3,2,1,0:T(8,128)(2,1)S(1)} collective-permute-done((bf16[4,2,16,32,128]{4,3,2,1,0:T(8,128)(2,1)}, bf16[4,2,16,32,128]{4,3,2,1,0:T(8,128)(2,1)S(1)}, u32[]{:S(2)}, u32[]{:S(2)}) %collective-permute-start.43) | collective-permute-done | bytes 1048608 | tf_op jit(solution)/shard_map/ppermute | solution.py:457
  703.0 9.0 %shard_map.66 = f32[2,2,8,32,8,8,128]{6,5,4,3,2,1,0:T(8,128)} custom-call(s32[2]{0:T(128)} %pad_add_fusion.2.scalar_ref, bf16[4,2,16,32,128]{4,3,2,1,0:T(8,128)(2,1)} %select_select_fusion.3.refs_0_, f32[8,8,8,128]{3,2,1,0:T(8,128)} %broadcast_in_dim.112.refs_1_, bf16[64,32]{1,0:T(8,128)(2,1)} %get-tuple-element.200.refs_2_, ...), custom_call_target="tpu_custom_call", output_to_operand_aliasing={{}: (8, {})} | custom-call | tf_op jit(solution)/shard_map/pallas_call | solution.py:291
  (198 shorter events, 97.0 us)
Async XLA Ops:
  0.7 22.4 %collective-permute-start.2 = (s32[2,128]{1,0:T(2,128)S(1)}, s32[2,128]{1,0:T(2,128)S(1)}, u32[]{:S(2)}, u32[]{:S(2)}) collective-permute-start(s32[2,128]{1,0:T(2,128)S(1)} %pad_add_fusion.1), channel_id=1, source_target_pairs={{0,8},{12,4},{1,9},{13,5},{2,10},{14,6},{3,11},{15,7},{16,24},{28,... | collective-permute-start | bytes 3080 | tf_op jit(solution)/shard_map/ppermute | solution.py:403
  6.6 17.8 %collective-permute-start = (s32[2,128]{1,0:T(2,128)S(1)}, s32[2,128]{1,0:T(2,128)S(1)}, u32[]{:S(2)}, u32[]{:S(2)}) collective-permute-start(s32[2,128]{1,0:T(2,128)S(1)} %pad_add_fusion.1), channel_id=1, source_target_pairs={{0,4},{12,8},{1,5},{13,9},{2,6},{14,10},{3,7},{15,11},{16,20},{28,... | collective-permute-start | bytes 3080 | tf_op jit(solution)/shard_map/ppermute | solution.py:403
  7.9 16.6 %collective-permute-start.1 = (s32[2,128]{1,0:T(2,128)S(1)}, s32[2,128]{1,0:T(2,128)S(1)}, u32[]{:S(2)}, u32[]{:S(2)}) collective-permute-start(s32[2,128]{1,0:T(2,128)S(1)} %pad_add_fusion.1), channel_id=1, source_target_pairs={{4,8},{8,4},{5,9},{9,5},{6,10},{10,6},{7,11},{11,7},{20,24},{24,20... | collective-permute-start | bytes 3080 | tf_op jit(solution)/shard_map/ppermute | solution.py:403
  14.4 51.2 %collective-permute-start.4 = (bf16[2,16,2,64,128]{4,3,2,1,0:T(8,128)(2,1)}, bf16[2,16,2,64,128]{4,3,2,1,0:T(8,128)(2,1)S(1)}, u32[]{:S(2)}, u32[]{:S(2)}) collective-permute-start(bf16[2,16,2,64,128]{4,3,2,1,0:T(8,128)(2,1)} %bitcast.180), channel_id=1, source_target_pairs={{4,8},{8,4},{5,9},{9,5},{6,10},{10,6},{7,11},{11,7},{20,24},{24,20... | collective-permute-start | bytes 3145736 | tf_op jit(solution)/shard_map/ppermute | solution.py:422
  15.1 50.4 %collective-permute-start.5 = (bf16[2,16,2,64,128]{4,3,2,1,0:T(8,128)(2,1)}, bf16[2,16,2,64,128]{4,3,2,1,0:T(8,128)(2,1)S(1)}, u32[]{:S(2)}, u32[]{:S(2)}) collective-permute-start(bf16[2,16,2,64,128]{4,3,2,1,0:T(8,128)(2,1)} %bitcast.181), channel_id=1, source_target_pairs={{0,8},{12,4},{1,9},{13,5},{2,10},{14,6},{3,11},{15,7},{16,24},{28,... | collective-permute-start | bytes 3145736 | tf_op jit(solution)/shard_map/ppermute | solution.py:422
  23.1 42.4 %collective-permute-start.3 = (bf16[2,16,2,64,128]{4,3,2,1,0:T(8,128)(2,1)}, bf16[2,16,2,64,128]{4,3,2,1,0:T(8,128)(2,1)S(1)}, u32[]{:S(2)}, u32[]{:S(2)}) collective-permute-start(bf16[2,16,2,64,128]{4,3,2,1,0:T(8,128)(2,1)} %bitcast.142), channel_id=1, source_target_pairs={{0,4},{12,8},{1,5},{13,9},{2,6},{14,10},{3,7},{15,11},{16,20},{28,... | collective-permute-start | bytes 3145736 | tf_op jit(solution)/shard_map/ppermute | solution.py:422
  65.6 1.4 copy-start.3
  72.5 7.6 %collective-permute-start.6 = (bf16[16,128,256]{2,1,0:T(8,128)(2,1)}, bf16[16,128,256]{2,1,0:T(8,128)(2,1)S(1)}, u32[]{:S(2)}, u32[]{:S(2)}) collective-permute-start(bf16[16,128,256]{2,1,0:T(8,128)(2,1)} %beam_sums.8), channel_id=1, source_target_pairs={{0,16},{1,17},{2,18},{3,19},{4,20},{5,21},{6,22},{7,23},{8,24},{9,... | collective-permute-start | bytes 3145736 | tf_op jit(solution)/shard_map/ppermute | solution.py:23
  80.1 1.4 copy-start.14
  91.5 223.8 %copy-start.18 = (f32[4,16,128]{2,1,0:T(8,128)S(1)}, f32[4,16,128]{2,1,0:T(8,128)}, u32[]{:S(2)}) copy-start(f32[4,16,128]{2,1,0:T(8,128)} %get-tuple-element.131) | copy-start | bytes 98308
  91.5 10.1 %collective-permute-start.7 = (bf16[16,128,256]{2,1,0:T(8,128)(2,1)}, bf16[16,128,256]{2,1,0:T(8,128)(2,1)S(1)}, u32[]{:S(2)}, u32[]{:S(2)}) collective-permute-start(bf16[16,128,256]{2,1,0:T(8,128)(2,1)} %beam_sums.9), channel_id=1, source_target_pairs={{0,16},{1,17},{2,18},{3,19},{4,20},{5,21},{6,22},{7,23},{8,24},{9,... | collective-permute-start | bytes 3145736 | tf_op jit(solution)/shard_map/ppermute | solution.py:23
  93.0 28.1 %collective-permute-start.8 = (bf16[2,16,2,64,128]{4,3,2,1,0:T(8,128)(2,1)}, bf16[2,16,2,64,128]{4,3,2,1,0:T(8,128)(2,1)S(1)}, u32[]{:S(2)}, u32[]{:S(2)}) collective-permute-start(bf16[2,16,2,64,128]{4,3,2,1,0:T(8,128)(2,1)} %bitcast.145), channel_id=1, source_target_pairs={{0,4},{12,8},{1,5},{13,9},{2,6},{14,10},{3,7},{15,11},{16,20},{28,... | collective-permute-start | bytes 3145736 | tf_op jit(solution)/shard_map/ppermute | solution.py:422
  97.3 43.7 %collective-permute-start.10 = (bf16[2,16,2,64,128]{4,3,2,1,0:T(8,128)(2,1)}, bf16[2,16,2,64,128]{4,3,2,1,0:T(8,128)(2,1)S(1)}, u32[]{:S(2)}, u32[]{:S(2)}) collective-permute-start(bf16[2,16,2,64,128]{4,3,2,1,0:T(8,128)(2,1)} %bitcast.182), channel_id=1, source_target_pairs={{0,8},{12,4},{1,9},{13,5},{2,10},{14,6},{3,11},{15,7},{16,24},{28,... | collective-permute-start | bytes 3145736 | tf_op jit(solution)/shard_map/ppermute | solution.py:422
  98.7 42.3 %collective-permute-start.9 = (bf16[2,16,2,64,128]{4,3,2,1,0:T(8,128)(2,1)}, bf16[2,16,2,64,128]{4,3,2,1,0:T(8,128)(2,1)}, u32[]{:S(2)}, u32[]{:S(2)}) collective-permute-start(bf16[2,16,2,64,128]{4,3,2,1,0:T(8,128)(2,1)} %bitcast.183), channel_id=1, source_target_pairs={{4,8},{8,4},{5,9},{9,5},{6,10},{10,6},{7,11},{11,7},{20,24},{24,20... | collective-permute-start | bytes 3145736 | tf_op jit(solution)/shard_map/ppermute | solution.py:422
  108.0 203.0 %copy-start = (bf16[4,2,16,32,128]{4,3,2,1,0:T(8,128)(2,1)S(1)}, bf16[4,2,16,32,128]{4,3,2,1,0:T(8,128)(2,1)}, u32[]{:S(2)}) copy-start(bf16[4,2,16,32,128]{4,3,2,1,0:T(8,128)(2,1)} %get-tuple-element.94.refs_4_) | copy-start | bytes 3145732
  108.0 207.4 %copy-start.19 = (f32[4,16,128]{2,1,0:T(8,128)S(1)}, f32[4,16,128]{2,1,0:T(8,128)}, u32[]{:S(2)}) copy-start(f32[4,16,128]{2,1,0:T(8,128)} %get-tuple-element.133) | copy-start | bytes 98308
  121.1 19.9 %copy-start.6 = (bf16[2,16,2,64,128]{4,3,2,1,0:T(8,128)(2,1)}, bf16[2,16,2,64,128]{4,3,2,1,0:T(8,128)(2,1)S(1)}, u32[]{:S(2)}) copy-start(bf16[2,16,2,64,128]{4,3,2,1,0:T(8,128)(2,1)S(1)} %collective-permute-done.8.refs_1_) | copy-start | bytes 3145732
  141.0 1.0 copy-start.8
  146.6 5.8 collective-permute-start.11
  158.8 156.7 %copy-start.20 = (f32[4,16,128]{2,1,0:T(8,128)S(1)}, f32[4,16,128]{2,1,0:T(8,128)}, u32[]{:S(2)}) copy-start(f32[4,16,128]{2,1,0:T(8,128)} %get-tuple-element.135) | copy-start | bytes 98308
  163.3 13.8 %collective-permute-start.12 = (bf16[16,128,256]{2,1,0:T(8,128)(2,1)}, bf16[16,128,256]{2,1,0:T(8,128)(2,1)S(1)}, u32[]{:S(2)}, u32[]{:S(2)}) collective-permute-start(bf16[16,128,256]{2,1,0:T(8,128)(2,1)} %beam_sums.11), channel_id=1, source_target_pairs={{0,16},{1,17},{2,18},{3,19},{4,20},{5,21},{6,22},{7,23},{8,24},{9,... | collective-permute-start | bytes 3145736 | tf_op jit(solution)/shard_map/ppermute | solution.py:23
  164.7 29.8 %collective-permute-start.13 = (bf16[2,16,2,64,128]{4,3,2,1,0:T(8,128)(2,1)}, bf16[2,16,2,64,128]{4,3,2,1,0:T(8,128)(2,1)S(1)}, u32[]{:S(2)}, u32[]{:S(2)}) collective-permute-start(bf16[2,16,2,64,128]{4,3,2,1,0:T(8,128)(2,1)} %bitcast.148), channel_id=1, source_target_pairs={{0,4},{12,8},{1,5},{13,9},{2,6},{14,10},{3,7},{15,11},{16,20},{28,... | collective-permute-start | bytes 3145736 | tf_op jit(solution)/shard_map/ppermute | solution.py:422
  170.7 23.8 %collective-permute-start.14 = (bf16[2,16,2,64,128]{4,3,2,1,0:T(8,128)(2,1)}, bf16[2,16,2,64,128]{4,3,2,1,0:T(8,128)(2,1)}, u32[]{:S(2)}, u32[]{:S(2)}) collective-permute-start(bf16[2,16,2,64,128]{4,3,2,1,0:T(8,128)(2,1)} %bitcast.186), channel_id=1, source_target_pairs={{4,8},{8,4},{5,9},{9,5},{6,10},{10,6},{7,11},{11,7},{20,24},{24,20... | collective-permute-start | bytes 3145736 | tf_op jit(solution)/shard_map/ppermute | solution.py:422
  172.4 41.9 %collective-permute-start.15 = (bf16[2,16,2,64,128]{4,3,2,1,0:T(8,128)(2,1)}, bf16[2,16,2,64,128]{4,3,2,1,0:T(8,128)(2,1)}, u32[]{:S(2)}, u32[]{:S(2)}) collective-permute-start(bf16[2,16,2,64,128]{4,3,2,1,0:T(8,128)(2,1)} %bitcast.187), channel_id=1, source_target_pairs={{0,8},{12,4},{1,9},{13,5},{2,10},{14,6},{3,11},{15,7},{16,24},{28,... | collective-permute-start | bytes 3145736 | tf_op jit(solution)/shard_map/ppermute | solution.py:422
  177.1 1.0 copy-start.15
  183.6 132.0 %copy-start.21 = (f32[4,16,128]{2,1,0:T(8,128)S(1)}, f32[4,16,128]{2,1,0:T(8,128)}, u32[]{:S(2)}) copy-start(f32[4,16,128]{2,1,0:T(8,128)} %get-tuple-element.137) | copy-start | bytes 98308
  183.6 141.0 %copy-start.1 = (bf16[4,2,16,32,128]{4,3,2,1,0:T(8,128)(2,1)S(1)}, bf16[4,2,16,32,128]{4,3,2,1,0:T(8,128)(2,1)}, u32[]{:S(2)}) copy-start(bf16[4,2,16,32,128]{4,3,2,1,0:T(8,128)(2,1)} %get-tuple-element.153.refs_6_) | copy-start | bytes 3145732
  194.5 19.8 %copy-start.7 = (bf16[2,16,2,64,128]{4,3,2,1,0:T(8,128)(2,1)}, bf16[2,16,2,64,128]{4,3,2,1,0:T(8,128)(2,1)S(1)}, u32[]{:S(2)}) copy-start(bf16[2,16,2,64,128]{4,3,2,1,0:T(8,128)(2,1)S(1)} %collective-permute-done.13.refs_1_) | copy-start | bytes 3145732
  218.8 5.9 collective-permute-start.16
  224.7 1.0 copy-start.16
  235.7 14.4 %collective-permute-start.17 = (bf16[16,128,256]{2,1,0:T(8,128)(2,1)}, bf16[16,128,256]{2,1,0:T(8,128)(2,1)}, u32[]{:S(2)}, u32[]{:S(2)}) collective-permute-start(bf16[16,128,256]{2,1,0:T(8,128)(2,1)} %beam_sums.13), channel_id=1, source_target_pairs={{0,16},{1,17},{2,18},{3,19},{4,20},{5,21},{6,22},{7,23},{8,24},{9,... | collective-permute-start | bytes 3145736 | tf_op jit(solution)/shard_map/ppermute | solution.py:23
  237.9 29.5 %collective-permute-start.18 = (bf16[2,16,2,64,128]{4,3,2,1,0:T(8,128)(2,1)}, bf16[2,16,2,64,128]{4,3,2,1,0:T(8,128)(2,1)S(1)}, u32[]{:S(2)}, u32[]{:S(2)}) collective-permute-start(bf16[2,16,2,64,128]{4,3,2,1,0:T(8,128)(2,1)} %bitcast.151), channel_id=1, source_target_pairs={{0,4},{12,8},{1,5},{13,9},{2,6},{14,10},{3,7},{15,11},{16,20},{28,... | collective-permute-start | bytes 3145736 | tf_op jit(solution)/shard_map/ppermute | solution.py:422
  243.6 23.8 %collective-permute-start.19 = (bf16[2,16,2,64,128]{4,3,2,1,0:T(8,128)(2,1)}, bf16[2,16,2,64,128]{4,3,2,1,0:T(8,128)(2,1)}, u32[]{:S(2)}, u32[]{:S(2)}) collective-permute-start(bf16[2,16,2,64,128]{4,3,2,1,0:T(8,128)(2,1)} %bitcast.184), channel_id=1, source_target_pairs={{4,8},{8,4},{5,9},{9,5},{6,10},{10,6},{7,11},{11,7},{20,24},{24,20... | collective-permute-start | bytes 3145736 | tf_op jit(solution)/shard_map/ppermute | solution.py:422
  245.4 41.0 %collective-permute-start.20 = (bf16[2,16,2,64,128]{4,3,2,1,0:T(8,128)(2,1)}, bf16[2,16,2,64,128]{4,3,2,1,0:T(8,128)(2,1)}, u32[]{:S(2)}, u32[]{:S(2)}) collective-permute-start(bf16[2,16,2,64,128]{4,3,2,1,0:T(8,128)(2,1)} %bitcast.185), channel_id=1, source_target_pairs={{0,8},{12,4},{1,9},{13,5},{2,10},{14,6},{3,11},{15,7},{16,24},{28,... | collective-permute-start | bytes 3145736 | tf_op jit(solution)/shard_map/ppermute | solution.py:422
  267.4 18.9 %copy-start.9 = (bf16[2,16,2,64,128]{4,3,2,1,0:T(8,128)(2,1)}, bf16[2,16,2,64,128]{4,3,2,1,0:T(8,128)(2,1)S(1)}, u32[]{:S(2)}) copy-start(bf16[2,16,2,64,128]{4,3,2,1,0:T(8,128)(2,1)S(1)} %collective-permute-done.18.refs_1_) | copy-start | bytes 3145732
  286.3 239.3 %copy-start.2 = (bf16[4,2,16,32,128]{4,3,2,1,0:T(8,128)(2,1)S(1)}, bf16[4,2,16,32,128]{4,3,2,1,0:T(8,128)(2,1)}, u32[]{:S(2)}) copy-start(bf16[4,2,16,32,128]{4,3,2,1,0:T(8,128)(2,1)} %get-tuple-element.155.refs_4_) | copy-start | bytes 3145732
  291.0 3.9 collective-permute-start.21
  304.8 9.2 %collective-permute-start.22 = (bf16[16,128,256]{2,1,0:T(8,128)(2,1)}, bf16[16,128,256]{2,1,0:T(8,128)(2,1)}, u32[]{:S(2)}, u32[]{:S(2)}) collective-permute-start(bf16[16,128,256]{2,1,0:T(8,128)(2,1)} %beam_sums.15), channel_id=1, source_target_pairs={{0,16},{1,17},{2,18},{3,19},{4,20},{5,21},{6,22},{7,23},{8,24},{9,... | collective-permute-start | bytes 3145736 | tf_op jit(solution)/shard_map/ppermute | solution.py:23
  308.1 16.5 %collective-permute-start.25 = (bf16[4,2,16,32,128]{4,3,2,1,0:T(8,128)(2,1)}, bf16[4,2,16,32,128]{4,3,2,1,0:T(8,128)(2,1)}, u32[]{:S(2)}, u32[]{:S(2)}) collective-permute-start(bf16[4,2,16,32,128]{4,3,2,1,0:T(8,128)(2,1)} %get-tuple-element.89.refs_4_), channel_id=1, source_target_pairs={{4,8},{8,4},{5,9},{9,5},{6,10},{10,6},{7,11},{11,7},{20,24},{24,20... | collective-permute-start | bytes 3145736 | tf_op jit(solution)/shard_map/ppermute | solution.py:436
  309.7 30.1 %collective-permute-start.27 = (bf16[4,2,16,32,128]{4,3,2,1,0:T(8,128)(2,1)}, bf16[4,2,16,32,128]{4,3,2,1,0:T(8,128)(2,1)}, u32[]{:S(2)}, u32[]{:S(2)}) collective-permute-start(bf16[4,2,16,32,128]{4,3,2,1,0:T(8,128)(2,1)} %get-tuple-element.89.refs_4_), channel_id=1, source_target_pairs={{4,0},{8,12},{5,1},{9,13},{6,2},{10,14},{7,3},{11,15},{20,16},{24,... | collective-permute-start | bytes 3145736 | tf_op jit(solution)/shard_map/ppermute | solution.py:434
  311.0 29.4 %collective-permute-start.26 = (bf16[4,2,16,32,128]{4,3,2,1,0:T(8,128)(2,1)S(1)}, bf16[4,2,16,32,128]{4,3,2,1,0:T(8,128)(2,1)}, u32[]{:S(2)}, u32[]{:S(2)}) collective-permute-start(bf16[4,2,16,32,128]{4,3,2,1,0:T(8,128)(2,1)S(1)} %copy-done), channel_id=1, source_target_pairs={{4,8},{8,4},{5,9},{9,5},{6,10},{10,6},{7,11},{11,7},{20,24},{24,20... | collective-permute-start | bytes 3145736 | tf_op jit(solution)/shard_map/ppermute | solution.py:436
  312.7 49.5 %collective-permute-start.28 = (bf16[4,2,16,32,128]{4,3,2,1,0:T(8,128)(2,1)S(1)}, bf16[4,2,16,32,128]{4,3,2,1,0:T(8,128)(2,1)}, u32[]{:S(2)}, u32[]{:S(2)}) collective-permute-start(bf16[4,2,16,32,128]{4,3,2,1,0:T(8,128)(2,1)S(1)} %copy-done), channel_id=1, source_target_pairs={{4,0},{8,12},{5,1},{9,13},{6,2},{10,14},{7,3},{11,15},{20,16},{24,... | collective-permute-start | bytes 3145736 | tf_op jit(solution)/shard_map/ppermute | solution.py:434
  314.0 70.7 %collective-permute-start.29 = (bf16[4,2,16,32,128]{4,3,2,1,0:T(8,128)(2,1)}, bf16[4,2,16,32,128]{4,3,2,1,0:T(8,128)(2,1)}, u32[]{:S(2)}, u32[]{:S(2)}) collective-permute-start(bf16[4,2,16,32,128]{4,3,2,1,0:T(8,128)(2,1)} %get-tuple-element.151.refs_6_), channel_id=1, source_target_pairs={{4,0},{8,12},{5,1},{9,13},{6,2},{10,14},{7,3},{11,15},{20,16},{24,... | collective-permute-start | bytes 3145736 | tf_op jit(solution)/shard_map/ppermute | solution.py:434
  324.6 82.6 %collective-permute-start.30 = (bf16[4,2,16,32,128]{4,3,2,1,0:T(8,128)(2,1)S(1)}, bf16[4,2,16,32,128]{4,3,2,1,0:T(8,128)(2,1)}, u32[]{:S(2)}, u32[]{:S(2)}) collective-permute-start(bf16[4,2,16,32,128]{4,3,2,1,0:T(8,128)(2,1)S(1)} %copy-done.1), channel_id=1, source_target_pairs={{4,0},{8,12},{5,1},{9,13},{6,2},{10,14},{7,3},{11,15},{20,16},{24,... | collective-permute-start | bytes 3145736 | tf_op jit(solution)/shard_map/ppermute | solution.py:434
  339.8 46.2 %collective-permute-start.23 = (f32[2,8,16]{2,1,0:T(8,128)S(1)}, f32[2,8,16]{2,1,0:T(8,128)S(1)}, u32[]{:S(2)}, u32[]{:S(2)}) collective-permute-start(f32[2,8,16]{2,1,0:T(8,128)S(1)} %psum.7), channel_id=1, source_target_pairs={{4,8},{8,4},{5,9},{9,5},{6,10},{10,6},{7,11},{11,7},{20,24},{24,20... | collective-permute-start | bytes 3080 | tf_op jit(solution)/shard_map/ppermute | solution.py:439
  340.4 89.2 %collective-permute-start.31 = (bf16[4,2,16,32,128]{4,3,2,1,0:T(8,128)(2,1)}, bf16[4,2,16,32,128]{4,3,2,1,0:T(8,128)(2,1)}, u32[]{:S(2)}, u32[]{:S(2)}) collective-permute-start(bf16[4,2,16,32,128]{4,3,2,1,0:T(8,128)(2,1)} %get-tuple-element.155.refs_4_), channel_id=1, source_target_pairs={{4,0},{8,12},{5,1},{9,13},{6,2},{10,14},{7,3},{11,15},{20,16},{24,... | collective-permute-start | bytes 3145736 | tf_op jit(solution)/shard_map/ppermute | solution.py:434
  362.2 89.9 %collective-permute-start.32 = (bf16[4,2,16,32,128]{4,3,2,1,0:T(8,128)(2,1)}, bf16[4,2,16,32,128]{4,3,2,1,0:T(8,128)(2,1)}, u32[]{:S(2)}, u32[]{:S(2)}) collective-permute-start(bf16[4,2,16,32,128]{4,3,2,1,0:T(8,128)(2,1)} %get-tuple-element.157.refs_4_), channel_id=1, source_target_pairs={{4,0},{8,12},{5,1},{9,13},{6,2},{10,14},{7,3},{11,15},{20,16},{24,... | collective-permute-start | bytes 3145736 | tf_op jit(solution)/shard_map/ppermute | solution.py:434
  384.7 89.9 %collective-permute-start.33 = (bf16[4,2,16,32,128]{4,3,2,1,0:T(8,128)(2,1)}, bf16[4,2,16,32,128]{4,3,2,1,0:T(8,128)(2,1)}, u32[]{:S(2)}, u32[]{:S(2)}) collective-permute-start(bf16[4,2,16,32,128]{4,3,2,1,0:T(8,128)(2,1)} %get-tuple-element.159.refs_6_), channel_id=1, source_target_pairs={{4,0},{8,12},{5,1},{9,13},{6,2},{10,14},{7,3},{11,15},{20,16},{24,... | collective-permute-start | bytes 3145736 | tf_op jit(solution)/shard_map/ppermute | solution.py:434
  386.0 110.4 %collective-permute-start.34 = (bf16[4,2,16,32,128]{4,3,2,1,0:T(8,128)(2,1)}, bf16[4,2,16,32,128]{4,3,2,1,0:T(8,128)(2,1)}, u32[]{:S(2)}, u32[]{:S(2)}) collective-permute-start(bf16[4,2,16,32,128]{4,3,2,1,0:T(8,128)(2,1)} %get-tuple-element.161.refs_6_), channel_id=1, source_target_pairs={{4,0},{8,12},{5,1},{9,13},{6,2},{10,14},{7,3},{11,15},{20,16},{24,... | collective-permute-start | bytes 3145736 | tf_op jit(solution)/shard_map/ppermute | solution.py:434
  407.2 87.6 %collective-permute-start.24 = (f32[2,2,8,16]{3,2,1,0:T(8,128)S(1)}, f32[2,2,8,16]{3,2,1,0:T(8,128)S(1)}, u32[]{:S(2)}, u32[]{:S(2)}) collective-permute-start(f32[2,2,8,16]{3,2,1,0:T(8,128)S(1)} %pad_maximum_fusion), channel_id=1, source_target_pairs={{4,0},{8,12},{5,1},{9,13},{6,2},{10,14},{7,3},{11,15},{20,16},{24,... | collective-permute-start | bytes 6152 | tf_op jit(solution)/shard_map/ppermute | solution.py:444
  429.6 88.0 %collective-permute-start.37 = (bf16[4,2,16,32,128]{4,3,2,1,0:T(8,128)(2,1)}, bf16[4,2,16,32,128]{4,3,2,1,0:T(8,128)(2,1)}, u32[]{:S(2)}, u32[]{:S(2)}) collective-permute-start(bf16[4,2,16,32,128]{4,3,2,1,0:T(8,128)(2,1)} %get-tuple-element.151.refs_6_), channel_id=1, source_target_pairs={{4,8},{8,4},{5,9},{9,5},{6,10},{10,6},{7,11},{11,7},{20,24},{24,20... | collective-permute-start | bytes 3145736 | tf_op jit(solution)/shard_map/ppermute | solution.py:442
  452.1 67.2 %collective-permute-start.38 = (bf16[4,2,16,32,128]{4,3,2,1,0:T(8,128)(2,1)S(1)}, bf16[4,2,16,32,128]{4,3,2,1,0:T(8,128)(2,1)}, u32[]{:S(2)}, u32[]{:S(2)}) collective-permute-start(bf16[4,2,16,32,128]{4,3,2,1,0:T(8,128)(2,1)S(1)} %copy-done.1), channel_id=1, source_target_pairs={{4,8},{8,4},{5,9},{9,5},{6,10},{10,6},{7,11},{11,7},{20,24},{24,20... | collective-permute-start | bytes 3145736 | tf_op jit(solution)/shard_map/ppermute | solution.py:442
  474.6 46.0 %collective-permute-start.39 = (bf16[4,2,16,32,128]{4,3,2,1,0:T(8,128)(2,1)}, bf16[4,2,16,32,128]{4,3,2,1,0:T(8,128)(2,1)}, u32[]{:S(2)}, u32[]{:S(2)}) collective-permute-start(bf16[4,2,16,32,128]{4,3,2,1,0:T(8,128)(2,1)} %get-tuple-element.155.refs_4_), channel_id=1, source_target_pairs={{4,8},{8,4},{5,9},{9,5},{6,10},{10,6},{7,11},{11,7},{20,24},{24,20... | collective-permute-start | bytes 3145736 | tf_op jit(solution)/shard_map/ppermute | solution.py:442
  494.8 27.1 %collective-permute-start.40 = (bf16[4,2,16,32,128]{4,3,2,1,0:T(8,128)(2,1)}, bf16[4,2,16,32,128]{4,3,2,1,0:T(8,128)(2,1)}, u32[]{:S(2)}, u32[]{:S(2)}) collective-permute-start(bf16[4,2,16,32,128]{4,3,2,1,0:T(8,128)(2,1)} %get-tuple-element.157.refs_4_), channel_id=1, source_target_pairs={{4,8},{8,4},{5,9},{9,5},{6,10},{10,6},{7,11},{11,7},{20,24},{24,20... | collective-permute-start | bytes 3145736 | tf_op jit(solution)/shard_map/ppermute | solution.py:442
  496.4 87.4 %collective-permute-start.41 = (bf16[4,2,16,32,128]{4,3,2,1,0:T(8,128)(2,1)}, bf16[4,2,16,32,128]{4,3,2,1,0:T(8,128)(2,1)}, u32[]{:S(2)}, u32[]{:S(2)}) collective-permute-start(bf16[4,2,16,32,128]{4,3,2,1,0:T(8,128)(2,1)} %get-tuple-element.159.refs_6_), channel_id=1, source_target_pairs={{4,8},{8,4},{5,9},{9,5},{6,10},{10,6},{7,11},{11,7},{20,24},{24,20... | collective-permute-start | bytes 3145736 | tf_op jit(solution)/shard_map/ppermute | solution.py:442
  517.6 77.8 %collective-permute-start.42 = (bf16[4,2,16,32,128]{4,3,2,1,0:T(8,128)(2,1)}, bf16[4,2,16,32,128]{4,3,2,1,0:T(8,128)(2,1)}, u32[]{:S(2)}, u32[]{:S(2)}) collective-permute-start(bf16[4,2,16,32,128]{4,3,2,1,0:T(8,128)(2,1)} %get-tuple-element.161.refs_6_), channel_id=1, source_target_pairs={{4,8},{8,4},{5,9},{9,5},{6,10},{10,6},{7,11},{11,7},{20,24},{24,20... | collective-permute-start | bytes 3145736 | tf_op jit(solution)/shard_map/ppermute | solution.py:442
  519.3 54.2 %collective-permute-start.36 = (bf16[4,2,16,32,128]{4,3,2,1,0:T(8,128)(2,1)}, bf16[4,2,16,32,128]{4,3,2,1,0:T(8,128)(2,1)}, u32[]{:S(2)}, u32[]{:S(2)}) collective-permute-start(bf16[4,2,16,32,128]{4,3,2,1,0:T(8,128)(2,1)} %collective-permute-done.25.refs_4_), channel_id=1, source_target_pairs={{4,0},{8,12},{5,1},{9,13},{6,2},{10,14},{7,3},{11,15},{20,16},{24,... | collective-permute-start | bytes 3145736 | tf_op jit(solution)/shard_map/ppermute | solution.py:457
  520.6 64.5 %collective-permute-start.35 = (bf16[4,2,16,32,128]{4,3,2,1,0:T(8,128)(2,1)}, bf16[4,2,16,32,128]{4,3,2,1,0:T(8,128)(2,1)}, u32[]{:S(2)}, u32[]{:S(2)}) collective-permute-start(bf16[4,2,16,32,128]{4,3,2,1,0:T(8,128)(2,1)} %collective-permute-done.26.refs_4_), channel_id=1, source_target_pairs={{4,0},{8,12},{5,1},{9,13},{6,2},{10,14},{7,3},{11,15},{20,16},{24,... | collective-permute-start | bytes 3145736 | tf_op jit(solution)/shard_map/ppermute | solution.py:457
  521.9 74.8 %collective-permute-start.48 = (bf16[4,2,16,32,128]{4,3,2,1,0:T(8,128)(2,1)}, bf16[4,2,16,32,128]{4,3,2,1,0:T(8,128)(2,1)}, u32[]{:S(2)}, u32[]{:S(2)}) collective-permute-start(bf16[4,2,16,32,128]{4,3,2,1,0:T(8,128)(2,1)} %collective-permute-done.37.refs_4_), channel_id=1, source_target_pairs={{4,0},{8,12},{5,1},{9,13},{6,2},{10,14},{7,3},{11,15},{20,16},{24,... | collective-permute-start | bytes 3145736 | tf_op jit(solution)/shard_map/ppermute | solution.py:457
  573.6 42.6 %collective-permute-start.47 = (bf16[4,2,16,32,128]{4,3,2,1,0:T(8,128)(2,1)}, bf16[4,2,16,32,128]{4,3,2,1,0:T(8,128)(2,1)S(1)}, u32[]{:S(2)}, u32[]{:S(2)}) collective-permute-start(bf16[4,2,16,32,128]{4,3,2,1,0:T(8,128)(2,1)} %collective-permute-done.38.refs_4_), channel_id=1, source_target_pairs={{4,0},{8,12},{5,1},{9,13},{6,2},{10,14},{7,3},{11,15},{20,16},{24,... | collective-permute-start | bytes 3145736 | tf_op jit(solution)/shard_map/ppermute | solution.py:457
  583.8 54.9 %collective-permute-start.46 = (bf16[4,2,16,32,128]{4,3,2,1,0:T(8,128)(2,1)}, bf16[4,2,16,32,128]{4,3,2,1,0:T(8,128)(2,1)}, u32[]{:S(2)}, u32[]{:S(2)}) collective-permute-start(bf16[4,2,16,32,128]{4,3,2,1,0:T(8,128)(2,1)} %collective-permute-done.39.refs_4_), channel_id=1, source_target_pairs={{4,0},{8,12},{5,1},{9,13},{6,2},{10,14},{7,3},{11,15},{20,16},{24,... | collective-permute-start | bytes 3145736 | tf_op jit(solution)/shard_map/ppermute | solution.py:457
  585.1 76.0 %collective-permute-start.45 = (bf16[4,2,16,32,128]{4,3,2,1,0:T(8,128)(2,1)}, bf16[4,2,16,32,128]{4,3,2,1,0:T(8,128)(2,1)S(1)}, u32[]{:S(2)}, u32[]{:S(2)}) collective-permute-start(bf16[4,2,16,32,128]{4,3,2,1,0:T(8,128)(2,1)} %collective-permute-done.40.refs_4_), channel_id=1, source_target_pairs={{4,0},{8,12},{5,1},{9,13},{6,2},{10,14},{7,3},{11,15},{20,16},{24,... | collective-permute-start | bytes 3145736 | tf_op jit(solution)/shard_map/ppermute | solution.py:457
  595.4 88.2 %collective-permute-start.44 = (bf16[4,2,16,32,128]{4,3,2,1,0:T(8,128)(2,1)}, bf16[4,2,16,32,128]{4,3,2,1,0:T(8,128)(2,1)}, u32[]{:S(2)}, u32[]{:S(2)}) collective-permute-start(bf16[4,2,16,32,128]{4,3,2,1,0:T(8,128)(2,1)} %collective-permute-done.41.refs_4_), channel_id=1, source_target_pairs={{4,0},{8,12},{5,1},{9,13},{6,2},{10,14},{7,3},{11,15},{20,16},{24,... | collective-permute-start | bytes 3145736 | tf_op jit(solution)/shard_map/ppermute | solution.py:457
  596.7 105.4 %collective-permute-start.43 = (bf16[4,2,16,32,128]{4,3,2,1,0:T(8,128)(2,1)}, bf16[4,2,16,32,128]{4,3,2,1,0:T(8,128)(2,1)S(1)}, u32[]{:S(2)}, u32[]{:S(2)}) collective-permute-start(bf16[4,2,16,32,128]{4,3,2,1,0:T(8,128)(2,1)} %collective-permute-done.42.refs_4_), channel_id=1, source_target_pairs={{4,0},{8,12},{5,1},{9,13},{6,2},{10,14},{7,3},{11,15},{20,16},{24,... | collective-permute-start | bytes 3145736 | tf_op jit(solution)/shard_map/ppermute | solution.py:457
  (7 other events, 6.8 us)

commit v3 on v2

--- a/solution.py
+++ b/solution.py
@@ -10,7 +10,6 @@
 COARSE = 8
 LANES = 128
 UNROLL = 8
-PARTS = 2
 PREPARE = 4
 PAIRS = (2, 4)
 
@@ -113,21 +112,25 @@
             wide_ref[frame] = prev_ref[frames - history + frame].astype(jnp.float32)
         for frame in range(frames):
             wide_ref[history + frame] = cur_ref[frame].astype(jnp.float32)
-        for comp in range(2):
+        groups = rows // 8
+
+        def filter_rows(index, carry):
+            comp = index // groups
+            low = pl.multiple_of(index % groups * 8, 8)
             for tile in range(tiles):
                 lanes = slice(tile * LANES, (tile + 1) * LANES)
-                for low in range(0, rows, 8):
-                    for frame in range(frames):
-                        terms = [
-                            taps_ref[tap, :, lanes]
-                            * wide_ref[history + frame - tap, comp, low : low + 8, lanes]
-                            for tap in range(taps_count)
-                        ]
-                        while len(terms) > 1:
-                            terms = [
-                                a + b for a, b in zip(terms[::2], terms[1::2])
-                            ] + terms[len(terms) // 2 * 2 :]
-                        filt_ref[comp, frame * rows + low : frame * rows + low + 8, lanes] = terms[0]
+                for frame in range(frames):
+                    terms = [
+                        taps_ref[tap, :, lanes] * wide_ref[history + frame - tap, comp, pl.ds(low, 8), lanes]
+                        for tap in range(taps_count)
+                    ]
+                    while len(terms) > 1:
+                        odd = terms[len(terms) // 2 * 2 :]
+                        terms = [a + b for a, b in zip(terms[::2], terms[1::2])] + odd
+                    filt_ref[comp, pl.ds(frame * rows + low, 8), lanes] = terms[0]
+            return carry
+
+        lax.fori_loop(0, 2 * groups, filter_rows, 0)
         real_part = filt_ref[0].astype(jnp.bfloat16)
         imag_part = filt_ref[1].astype(jnp.bfloat16)
 
@@ -349,6 +352,13 @@
     return left.reshape(beams, own_count, unit, LANES), right.reshape(beams, blocks * own_count, unit, LANES)
 
 
+def beam_parts(beams, last):
+    half = beams // 2
+    if not last:
+        return [(0, half), (half, half)]
+    return [(0, half), (half, half // 2), (half + half // 2, half - half // 2)]
+
+
 def per_device(voltages, fir_taps, station_map, beam_index, weight_table):
     _, coarse_dev, dishes_dev, frames, pols, fine = voltages.shape
     groups = lax.axis_size("stn")
@@ -402,16 +412,7 @@
         for path in paths:
             known.append(lax.ppermute(maps, "stn", path))
         maps = jnp.stack(known)
-        some = beams // PARTS
-        weights = [
-            [
-                block_weights(
-                    maps, weight_table[..., part * some : (part + 1) * some], 2 * side + step, own_count, share, pols
-                )
-                for part in range(PARTS)
-            ]
-            for step in range(2)
-        ]
+        parts = [beam_parts(beams, coarse == coarse_dev - 1) for coarse in range(coarse_dev)]
         steps = [(coarse, step) for coarse in range(coarse_dev) for step in range(2)]
         arrived = []
         for coarse, step in steps:
@@ -421,33 +422,39 @@
             for sent, path in zip((near, far, far), paths):
                 sources.append(lax.ppermute(sent, "stn", path))
             arrived.append(sources)
-        formed, ends, power = {}, {}, [[0.0] * PARTS for _ in range(2)]
-        keys = [(*key, part) for key in steps for part in range(PARTS)]
+        formed, ends, powers = {}, {}, {}
+        keys = [(coarse, step, part) for coarse, step in steps for part in parts[coarse]]
+        early = len(parts[0])
+        weights = {}
+        for step in range(2):
+            for part in {part: None for some in parts for part in some}:
+                table = weight_table[..., part[0] : sum(part)]
+                weights[step, part] = block_weights(maps, table, 2 * side + step, own_count, share, pols)
         crossed = {}
         for index, (coarse, step, part) in enumerate(keys):
-            sources = arrived[index // PARTS]
+            sources = arrived[steps.index((coarse, step))]
             if index:
                 _, sources = lax.optimization_barrier((formed[keys[index - 1]], sources))
-            own, more = form(weights[step][part][coarse], sources, some)
+            own, powers[coarse, step, part] = form(weights[step, part][coarse], sources, part[1])
             formed[coarse, step, part] = own
-            power[step][part] = power[step][part] + more
             ends[coarse, step, part] = lax.ppermute(own, "stn", outward)
-            if index < PARTS:
+            if index < early:
                 crossed[coarse, step, part] = lax.ppermute(own, "stn", across)
-        power = jnp.stack([jnp.concatenate(parts) for parts in power])
+        power = sum(
+            jnp.stack([jnp.concatenate([powers[coarse, step, part] for part in parts[coarse]]) for step in range(2)])
+            for coarse in range(coarse_dev)
+        )
         power = lax.psum(power, "chan")
         beyond = lax.ppermute(power, "stn", across)
-        beyond, *held = lax.optimization_barrier((beyond, *[formed[key] for key in keys[PARTS:]]))
-        for index, value in enumerate(held, PARTS):
+        beyond, *held = lax.optimization_barrier((beyond, *[formed[key] for key in keys[early:]]))
+        for index, value in enumerate(held, early):
             crossed[keys[index]] = lax.ppermute(value, "stn", across)
         both = jnp.stack([power, beyond])
         from_inner = lax.ppermute(both, "stn", outward)
         flag = jnp.where(inner, 0, 1)
         odd = own_index % 2 == 1
-        held = [crossed[key] for key in keys[:PARTS]] + [ends[key] for key in keys]
-        from_inner, *held = lax.optimization_barrier((from_inner, *held))
-        crossed.update(zip(keys[:PARTS], held))
-        ends = dict(zip(keys, held[PARTS:]))
+        from_inner, *held = lax.optimization_barrier((from_inner, *[ends[key] for key in keys]))
+        ends = dict(zip(keys, held))
         both = jnp.where(inner, both, from_inner)
         power = jnp.where(side == 0, both, both[::-1]).reshape((groups,) + power.shape[1:])
         left_scale, right_scale = scales(place_power(power), denominator, frames, own_index, tiles)
@@ -465,23 +472,23 @@
             near = [(formed[coarse, step, part], ends[coarse, step, part], flag) for step in range(2)]
             return correlate(
                 out, lefts[coarse, part], near, left_scale, right_scale, coarse, coarse_dev,
-                2 * side, pols, part * some,
+                2 * side, pols, part[0],
             )
 
         def far_work(out, coarse, step, part):
             far = [(crossed[coarse, step, part], far_ends[coarse, step, part], flag)]
             return correlate(
                 out, lefts[coarse, part], far, left_scale, right_scale, coarse, coarse_dev,
-                2 * (1 - side) + step, pols, part * some,
+                2 * (1 - side) + step, pols, part[0],
             )
 
-        work = [(near_work, (coarse, part)) for coarse in range(coarse_dev) for part in range(PARTS)]
+        work = [(near_work, (coarse, part)) for coarse in range(coarse_dev) for part in parts[coarse]]
         work += [(far_work, key) for key in keys]
-        for index in range(PARTS):
+        for index in range(early):
             forward(index)
         for index, (make, which) in enumerate(work):
             out = make(out, *which)
-            sent = index + PARTS
+            sent = index + early
             if sent < len(keys):
                 out, crossed[keys[sent]] = lax.optimization_barrier((out, crossed[keys[sent]]))
                 forward(sent)

time: 716 us -> 745 us (1.041)
  Pallas kernels: 223 us -> 248 us
  waiting for transfers between devices: 335 us -> 325 us
  starting transfers between devices: 96.8 us -> 106 us
    ppermute x8 -> x10, waiting for transfers between devices: 56.5 us -> 80.7 us  [forward(): far_ends[keys[index]] = lax.ppermute(crossed[keys[index]], 'stn', outward)]
    ppermute x8 -> x10, waiting for transfers between devices: 126 us -> 107 us  [per_device(): ends[coarse, step, part] = lax.ppermute(own, 'stn', outward)]
    ppermute x1, waiting for transfers between devices: 18.6 us -> 9.82 us  [per_device(): from_inner = lax.ppermute(both, 'stn', outward)]
    pallas_call x12 -> x15, Pallas kernels: 129 us -> 137 us  [correlate(): pl.pallas_call(body, grid_spec=pltpu.PrefetchScalarGridSpec(num_scalar_pr...]
    pallas_call x8 -> x10, Pallas kernels: 36.5 us -> 44.9 us  [beam_sums(): pl.pallas_call(body, grid=(frames // frames_step,), in_specs=[pl.BlockSpe...]
    pallas_call x8 -> x10, Pallas kernels: 43.3 us -> 51.4 us  [channelize(): pl.pallas_call(body, grid=(beams,), in_specs=[pl.BlockSpec((frames, 2, ro...]
    ppermute x8 -> x10, starting transfers between devices: 14.7 us -> 19.5 us  [shifted(): lax.ppermute(value, axis, [(source, source + steps) for source in range(f...]
  transfers between devices with their start and end apart: 49 -> 57, of which waited for: 21 -> 21; matrix products, arithmetic and copies ran while one was open for 5% -> 5% of each run, Pallas kernels for 22% -> 26%
where the time goes in v3:
time: 745 us; the launch traced here: 741 us
  waiting for transfers between devices  325 us (44%)
  Pallas kernels  248 us (33%)
  starting transfers between devices  106 us (14%)
  other arithmetic  25.1 us (3%)
  local copies, waits for them, and re-layouts  16.8 us (2%)
  blocking collectives  10.1 us (1%)
  matrix products  8.16 us (1%)
    pallas_call x15, Pallas kernels, correlate(): pl.pallas_call(body, grid_spec=pltpu.PrefetchScalarGridSpec(num_scalar_pr...  137 us
    ppermute x12, waiting for transfers between devices, per_device(): sources.append(lax.ppermute(sent, 'stn', path))  127 us
    ppermute x10, waiting for transfers between devices, per_device(): ends[coarse, step, part] = lax.ppermute(own, 'stn', outward)  107 us
    ppermute x10, waiting for transfers between devices, forward(): far_ends[keys[index]] = lax.ppermute(crossed[keys[index]], 'stn', outward)  80.7 us
    pallas_call x10, Pallas kernels, channelize(): pl.pallas_call(body, grid=(beams,), in_specs=[pl.BlockSpec((frames, 2, ro...  51.4 us
    pallas_call x10, Pallas kernels, beam_sums(): pl.pallas_call(body, grid=(frames // frames_step,), in_specs=[pl.BlockSpe...  44.9 us
    ppermute x12, starting transfers between devices, per_device(): sources.append(lax.ppermute(sent, 'stn', path))  36.1 us
    ppermute x10, starting transfers between devices, shifted(): lax.ppermute(value, axis, [(source, source + steps) for source in range(f...  19.5 us
  transfers between devices with their start and end apart: 57, of which 21 were waited for; matrix products, arithmetic and copies ran while one was open for 5% of the time, Pallas kernels for 26%

profile of v3, /device:TPU:0, one launch (start us, length us, event | category | flops | bytes accessed | tf_op | source)
XLA Modules:
  0.0 740.7 jit_solution(9377981361191179716)
XLA Ops:
  0.7 6.0 collective-permute-start.2
  10.8 3.6 sort_dishes.4
  15.2 5.8 collective-permute-start.5
  26.7 39.0 %collective-permute-done.3.refs_1_ = bf16[2,16,2,64,128]{4,3,2,1,0:T(8,128)(2,1)S(1)} collective-permute-done((bf16[2,16,2,64,128]{4,3,2,1,0:T(8,128)(2,1)}, bf16[2,16,2,64,128]{4,3,2,1,0:T(8,128)(2,1)S(1)}, u32[]{:S(2)}, u32[]{:S(2)}) %collective-permute-start.3) | collective-permute-done | bytes 1048608 | tf_op jit(solution)/shard_map/ppermute | solution.py:423
  68.0 4.5 beam_sums.10
  73.8 3.6 sort_dishes.5
  81.5 6.0 channelize.10
  87.5 4.6 beam_sums.11
  94.3 4.3 collective-permute-start.8
  102.0 6.0 channelize.11
  108.0 14.4 %collective-permute-done.8.refs_1_ = bf16[2,16,2,64,128]{4,3,2,1,0:T(8,128)(2,1)S(1)} collective-permute-done((bf16[2,16,2,64,128]{4,3,2,1,0:T(8,128)(2,1)}, bf16[2,16,2,64,128]{4,3,2,1,0:T(8,128)(2,1)S(1)}, u32[]{:S(2)}, u32[]{:S(2)}) %collective-permute-start.8) | collective-permute-done | bytes 1048608 | tf_op jit(solution)/shard_map/ppermute | solution.py:423
  122.5 19.0 %collective-permute-done.10.refs_3_ = bf16[2,16,2,64,128]{4,3,2,1,0:T(8,128)(2,1)S(1)} collective-permute-done((bf16[2,16,2,64,128]{4,3,2,1,0:T(8,128)(2,1)}, bf16[2,16,2,64,128]{4,3,2,1,0:T(8,128)(2,1)S(1)}, u32[]{:S(2)}, u32[]{:S(2)}) %collective-permute-start.10) | collective-permute-done | bytes 1048608 | tf_op jit(solution)/shard_map/ppermute | solution.py:423
  142.8 4.5 beam_sums.12
  148.8 3.6 sort_dishes.6
  154.2 6.0 channelize.12
  160.2 4.6 beam_sums.13
  167.1 6.5 collective-permute-start.13
  174.4 3.9 collective-permute-start.15
  179.2 6.0 channelize.13
  185.2 12.2 %collective-permute-done.13.refs_1_ = bf16[2,16,2,64,128]{4,3,2,1,0:T(8,128)(2,1)S(1)} collective-permute-done((bf16[2,16,2,64,128]{4,3,2,1,0:T(8,128)(2,1)}, bf16[2,16,2,64,128]{4,3,2,1,0:T(8,128)(2,1)S(1)}, u32[]{:S(2)}, u32[]{:S(2)}) %collective-permute-start.13) | collective-permute-done | bytes 1048608 | tf_op jit(solution)/shard_map/ppermute | solution.py:423
  197.4 18.9 %collective-permute-done.15.refs_3_ = bf16[2,16,2,64,128]{4,3,2,1,0:T(8,128)(2,1)S(1)} collective-permute-done((bf16[2,16,2,64,128]{4,3,2,1,0:T(8,128)(2,1)}, bf16[2,16,2,64,128]{4,3,2,1,0:T(8,128)(2,1)S(1)}, u32[]{:S(2)}, u32[]{:S(2)}) %collective-permute-start.15) | collective-permute-done | bytes 1048608 | tf_op jit(solution)/shard_map/ppermute | solution.py:423
  217.3 4.5 beam_sums.14
  226.5 6.0 channelize.14
  232.5 4.4 beam_sums.15
  236.9 3.1 collective-permute-start.17
  240.0 3.6 sort_dishes.7
  243.6 5.9 collective-permute-start.19
  250.3 3.9 collective-permute-start.21
  255.1 3.9 channelize.15
  259.0 4.4 beam_sums.16
  266.5 3.8 channelize.16
  273.4 20.1 %collective-permute-done.21.refs_3_ = bf16[2,16,2,64,128]{4,3,2,1,0:T(8,128)(2,1)S(1)} collective-permute-done((bf16[2,16,2,64,128]{4,3,2,1,0:T(8,128)(2,1)}, bf16[2,16,2,64,128]{4,3,2,1,0:T(8,128)(2,1)S(1)}, u32[]{:S(2)}, u32[]{:S(2)}) %collective-permute-start.21) | collective-permute-done | bytes 1048608 | tf_op jit(solution)/shard_map/ppermute | solution.py:423
  294.5 4.5 beam_sums.17
  305.1 6.0 channelize.17
  311.1 4.5 beam_sums.18
  322.8 3.8 channelize.18
  326.7 4.4 beam_sums.19
  334.6 15.9 %collective-permute-done.28.refs_5_ = bf16[4,2,16,32,128]{4,3,2,1,0:T(8,128)(2,1)S(1)} collective-permute-done((bf16[4,2,16,32,128]{4,3,2,1,0:T(8,128)(2,1)}, bf16[4,2,16,32,128]{4,3,2,1,0:T(8,128)(2,1)S(1)}, u32[]{:S(2)}, u32[]{:S(2)}) %collective-permute-start.28) | collective-permute-done | bytes 1048608 | tf_op jit(solution)/shard_map/ppermute | solution.py:440
  358.0 3.9 channelize.19
  362.7 10.1 %psum.7 = f32[2,8,16]{2,1,0:T(8,128)S(1)} all-reduce(f32[2,8,16]{2,1,0:T(8,128)S(1)} %maximum_add_fusion), channel_id=1, replica_groups=mesh['tm'=2,'stn'=4,'chan'=4] {'chan'}, use_global_device_ids=true, to_apply=%region_17.18 | all-reduce | flops 256 | bytes 2048 | tf_op jit(solution)/shard_map/psum | solution.py:447
  374.0 21.5 %collective-permute-done.30.refs_7_ = bf16[4,2,16,32,128]{4,3,2,1,0:T(8,128)(2,1)} collective-permute-done((bf16[4,2,16,32,128]{4,3,2,1,0:T(8,128)(2,1)}, bf16[4,2,16,32,128]{4,3,2,1,0:T(8,128)(2,1)}, u32[]{:S(2)}, u32[]{:S(2)}) %collective-permute-start.30) | collective-permute-done | bytes 1048608 | tf_op jit(solution)/shard_map/ppermute | solution.py:440
  396.9 32.4 %collective-permute-done.32.refs_5_ = bf16[2,2,16,32,128]{4,3,2,1,0:T(8,128)(2,1)} collective-permute-done((bf16[2,2,16,32,128]{4,3,2,1,0:T(8,128)(2,1)}, bf16[2,2,16,32,128]{4,3,2,1,0:T(8,128)(2,1)}, u32[]{:S(2)}, u32[]{:S(2)}) %collective-permute-start.32) | collective-permute-done | bytes 524320 | tf_op jit(solution)/shard_map/ppermute | solution.py:440
  435.2 27.8 %collective-permute-done.33.refs_5_ = bf16[2,2,16,32,128]{4,3,2,1,0:T(8,128)(2,1)} collective-permute-done((bf16[2,2,16,32,128]{4,3,2,1,0:T(8,128)(2,1)}, bf16[2,2,16,32,128]{4,3,2,1,0:T(8,128)(2,1)}, u32[]{:S(2)}, u32[]{:S(2)}) %collective-permute-start.33) | collective-permute-done | bytes 524320 | tf_op jit(solution)/shard_map/ppermute | solution.py:440
  465.6 8.6 %collective-permute-done.35.refs_7_ = bf16[2,2,16,32,128]{4,3,2,1,0:T(8,128)(2,1)} collective-permute-done((bf16[2,2,16,32,128]{4,3,2,1,0:T(8,128)(2,1)}, bf16[2,2,16,32,128]{4,3,2,1,0:T(8,128)(2,1)}, u32[]{:S(2)}, u32[]{:S(2)}) %collective-permute-start.35) | collective-permute-done | bytes 524320 | tf_op jit(solution)/shard_map/ppermute | solution.py:440
  475.9 9.8 %collective-permute-done.26 = f32[2,2,8,16]{3,2,1,0:T(8,128)S(1)} collective-permute-done((f32[2,2,8,16]{3,2,1,0:T(8,128)S(1)}, f32[2,2,8,16]{3,2,1,0:T(8,128)S(1)}, u32[]{:S(2)}, u32[]{:S(2)}) %collective-permute-start.26) | collective-permute-done | bytes 2080 | tf_op jit(solution)/shard_map/ppermute | solution.py:453
  501.3 14.3 %shard_map.55.refs_9_ = f32[2,2,8,32,8,8,128]{6,5,4,3,2,1,0:T(8,128)} custom-call(s32[2]{0:T(128)} %pad_add_fusion.3.scalar_ref, bf16[4,2,16,32,128]{4,3,2,1,0:T(8,128)(2,1)} %select_select_fusion.2.refs_0_, f32[8,8,8,128]{3,2,1,0:T(8,128)} %broadcast_in_dim.153.refs_1_, bf16[64,32]{1,0:T(8,128)(2,1)} %get-tuple-element.246.refs_2_, ...), custom_call_target="tpu_custom_call" | custom-call | tf_op jit(solution)/shard_map/pallas_call | solution.py:294
  518.1 14.3 %shard_map.56.refs_9_ = f32[2,2,8,32,8,8,128]{6,5,4,3,2,1,0:T(8,128)} custom-call(s32[2]{0:T(128)} %pad_add_fusion.3.scalar_ref, bf16[4,2,16,32,128]{4,3,2,1,0:T(8,128)(2,1)} %select_select_fusion.1.refs_0_, f32[8,8,8,128]{3,2,1,0:T(8,128)} %broadcast_in_dim.153.refs_1_, bf16[64,32]{1,0:T(8,128)(2,1)} %get-tuple-element.246.refs_2_, ...), custom_call_target="tpu_custom_call", output_to_operand_aliasing={{}: (10, {})} | custom-call | tf_op jit(solution)/shard_map/pallas_call | solution.py:294
  532.4 14.3 %shard_map.57.refs_9_ = f32[2,2,8,32,8,8,128]{6,5,4,3,2,1,0:T(8,128)} custom-call(s32[2]{0:T(128)} %pad_add_fusion.3.scalar_ref, bf16[4,2,16,32,128]{4,3,2,1,0:T(8,128)(2,1)} %select_select_fusion.refs_0_, f32[8,8,8,128]{3,2,1,0:T(8,128)} %broadcast_in_dim.153.refs_1_, bf16[64,32]{1,0:T(8,128)(2,1)} %get-tuple-element.246.refs_2_, ...), custom_call_target="tpu_custom_call", output_to_operand_aliasing={{}: (10, {})} | custom-call | tf_op jit(solution)/shard_map/pallas_call | solution.py:294
  556.0 8.7 %shard_map.58.refs_9_ = f32[2,2,8,32,8,8,128]{6,5,4,3,2,1,0:T(8,128)} custom-call(s32[2]{0:T(128)} %pad_add_fusion.3.scalar_ref, bf16[2,2,16,32,128]{4,3,2,1,0:T(8,128)(2,1)} %select_select_fusion.3.refs_0_, f32[8,8,8,128]{3,2,1,0:T(8,128)} %broadcast_in_dim.153.refs_1_, bf16[64,32]{1,0:T(8,128)(2,1)} %get-tuple-element.246.refs_2_, ...), custom_call_target="tpu_custom_call", output_to_operand_aliasing={{}: (10, {})} | custom-call | tf_op jit(solution)/shard_map/pallas_call | solution.py:294
  564.7 8.8 %shard_map.59.refs_7_ = f32[2,2,8,32,8,8,128]{6,5,4,3,2,1,0:T(8,128)} custom-call(s32[2]{0:T(128)} %pad_add_fusion.3.scalar_ref, bf16[2,2,16,32,128]{4,3,2,1,0:T(8,128)(2,1)} %select_select_fusion.4.refs_0_, f32[8,8,8,128]{3,2,1,0:T(8,128)} %broadcast_in_dim.153.refs_1_, bf16[64,32]{1,0:T(8,128)(2,1)} %get-tuple-element.246.refs_2_, ...), custom_call_target="tpu_custom_call", output_to_operand_aliasing={{}: (10, {})} | custom-call | tf_op jit(solution)/shard_map/pallas_call | solution.py:294
  574.2 8.9 %shard_map.60.refs_7_ = f32[2,2,8,32,8,8,128]{6,5,4,3,2,1,0:T(8,128)} custom-call(s32[2]{0:T(128)} %pad_add_fusion.4.scalar_ref, bf16[4,2,16,32,128]{4,3,2,1,0:T(8,128)(2,1)} %select_select_fusion.2.refs_0_, f32[8,8,8,128]{3,2,1,0:T(8,128)} %broadcast_in_dim.153.refs_1_, bf16[64,32]{1,0:T(8,128)(2,1)} %get-tuple-element.246.refs_2_, ...), custom_call_target="tpu_custom_call", output_to_operand_aliasing={{}: (8, {})} | custom-call | tf_op jit(solution)/shard_map/pallas_call | solution.py:294
  585.2 9.1 %shard_map.61.refs_7_ = f32[2,2,8,32,8,8,128]{6,5,4,3,2,1,0:T(8,128)} custom-call(s32[2]{0:T(128)} %pad_add_fusion.4.scalar_ref, bf16[4,2,16,32,128]{4,3,2,1,0:T(8,128)(2,1)} %select_select_fusion.1.refs_0_, f32[8,8,8,128]{3,2,1,0:T(8,128)} %broadcast_in_dim.153.refs_1_, bf16[64,32]{1,0:T(8,128)(2,1)} %get-tuple-element.246.refs_2_, ...), custom_call_target="tpu_custom_call", output_to_operand_aliasing={{}: (8, {})} | custom-call | tf_op jit(solution)/shard_map/pallas_call | solution.py:294
  594.3 32.1 %collective-permute-done.38.refs_5_ = bf16[4,2,16,32,128]{4,3,2,1,0:T(8,128)(2,1)} collective-permute-done((bf16[4,2,16,32,128]{4,3,2,1,0:T(8,128)(2,1)}, bf16[4,2,16,32,128]{4,3,2,1,0:T(8,128)(2,1)}, u32[]{:S(2)}, u32[]{:S(2)}) %collective-permute-start.38) | collective-permute-done | bytes 1048608 | tf_op jit(solution)/shard_map/ppermute | solution.py:464
  627.7 8.9 %shard_map.62.refs_7_ = f32[2,2,8,32,8,8,128]{6,5,4,3,2,1,0:T(8,128)} custom-call(s32[2]{0:T(128)} %pad_add_fusion.2.scalar_ref, bf16[4,2,16,32,128]{4,3,2,1,0:T(8,128)(2,1)} %select_select_fusion.2.refs_0_, f32[8,8,8,128]{3,2,1,0:T(8,128)} %broadcast_in_dim.153.refs_1_, bf16[64,32]{1,0:T(8,128)(2,1)} %get-tuple-element.246.refs_2_, ...), custom_call_target="tpu_custom_call", output_to_operand_aliasing={{}: (8, {})} | custom-call | tf_op jit(solution)/shard_map/pallas_call | solution.py:294
  637.9 10.9 %collective-permute-done.56.refs_5_ = bf16[4,2,16,32,128]{4,3,2,1,0:T(8,128)(2,1)S(1)} collective-permute-done((bf16[4,2,16,32,128]{4,3,2,1,0:T(8,128)(2,1)}, bf16[4,2,16,32,128]{4,3,2,1,0:T(8,128)(2,1)S(1)}, u32[]{:S(2)}, u32[]{:S(2)}) %collective-permute-start.56) | collective-permute-done | bytes 1048608 | tf_op jit(solution)/shard_map/ppermute | solution.py:464
  650.0 21.3 %collective-permute-done.55.refs_5_ = bf16[4,2,16,32,128]{4,3,2,1,0:T(8,128)(2,1)} collective-permute-done((bf16[4,2,16,32,128]{4,3,2,1,0:T(8,128)(2,1)}, bf16[4,2,16,32,128]{4,3,2,1,0:T(8,128)(2,1)}, u32[]{:S(2)}, u32[]{:S(2)}) %collective-permute-start.55) | collective-permute-done | bytes 1048608 | tf_op jit(solution)/shard_map/ppermute | solution.py:464
  672.6 9.0 %shard_map.63.refs_7_ = f32[2,2,8,32,8,8,128]{6,5,4,3,2,1,0:T(8,128)} custom-call(s32[2]{0:T(128)} %pad_add_fusion.2.scalar_ref, bf16[4,2,16,32,128]{4,3,2,1,0:T(8,128)(2,1)} %select_select_fusion.1.refs_0_, f32[8,8,8,128]{3,2,1,0:T(8,128)} %broadcast_in_dim.153.refs_1_, bf16[64,32]{1,0:T(8,128)(2,1)} %get-tuple-element.246.refs_2_, ...), custom_call_target="tpu_custom_call", output_to_operand_aliasing={{}: (8, {})} | custom-call | tf_op jit(solution)/shard_map/pallas_call | solution.py:294
  681.6 8.9 %shard_map.64.refs_7_ = f32[2,2,8,32,8,8,128]{6,5,4,3,2,1,0:T(8,128)} custom-call(s32[2]{0:T(128)} %pad_add_fusion.4.scalar_ref, bf16[4,2,16,32,128]{4,3,2,1,0:T(8,128)(2,1)} %select_select_fusion.refs_0_, f32[8,8,8,128]{3,2,1,0:T(8,128)} %broadcast_in_dim.153.refs_1_, bf16[64,32]{1,0:T(8,128)(2,1)} %get-tuple-element.246.refs_2_, ...), custom_call_target="tpu_custom_call", output_to_operand_aliasing={{}: (8, {})} | custom-call | tf_op jit(solution)/shard_map/pallas_call | solution.py:294
  690.5 14.5 %collective-permute-done.54.refs_5_ = bf16[2,2,16,32,128]{4,3,2,1,0:T(8,128)(2,1)} collective-permute-done((bf16[2,2,16,32,128]{4,3,2,1,0:T(8,128)(2,1)}, bf16[2,2,16,32,128]{4,3,2,1,0:T(8,128)(2,1)}, u32[]{:S(2)}, u32[]{:S(2)}) %collective-permute-start.54) | collective-permute-done | bytes 524320 | tf_op jit(solution)/shard_map/ppermute | solution.py:464
  705.0 5.7 shard_map.65.refs_7_
  712.7 5.7 shard_map.66.refs_7_
  719.5 8.9 %shard_map.67.refs_7_ = f32[2,2,8,32,8,8,128]{6,5,4,3,2,1,0:T(8,128)} custom-call(s32[2]{0:T(128)} %pad_add_fusion.2.scalar_ref, bf16[4,2,16,32,128]{4,3,2,1,0:T(8,128)(2,1)} %select_select_fusion.refs_0_, f32[8,8,8,128]{3,2,1,0:T(8,128)} %broadcast_in_dim.153.refs_1_, bf16[64,32]{1,0:T(8,128)(2,1)} %get-tuple-element.246.refs_2_, ...), custom_call_target="tpu_custom_call", output_to_operand_aliasing={{}: (8, {})} | custom-call | tf_op jit(solution)/shard_map/pallas_call | solution.py:294
  728.4 5.7 shard_map.68.refs_7_
  734.9 5.7 shard_map.69
  (258 shorter events, 123.7 us)
Async XLA Ops:
  0.0 223.4 %copy-start.28 = (bf16[2,16,2,8]{1,3,2,0:T(8,128)(2,1)S(1)}, bf16[2,16,2,8]{1,3,2,0:T(8,128)(2,1)}, u32[]{:S(2)}) copy-start(bf16[2,16,2,8]{1,3,2,0:T(8,128)(2,1)} %param.9) | copy-start | bytes 3076
  0.7 22.5 %collective-permute-start.2 = (s32[2,128]{1,0:T(2,128)S(1)}, s32[2,128]{1,0:T(2,128)S(1)}, u32[]{:S(2)}, u32[]{:S(2)}) collective-permute-start(s32[2,128]{1,0:T(2,128)S(1)} %pad_add_fusion.1), channel_id=1, source_target_pairs={{0,8},{12,4},{1,9},{13,5},{2,10},{14,6},{3,11},{15,7},{16,24},{28,... | collective-permute-start | bytes 3080 | tf_op jit(solution)/shard_map/ppermute | solution.py:413
  6.7 17.9 %collective-permute-start = (s32[2,128]{1,0:T(2,128)S(1)}, s32[2,128]{1,0:T(2,128)S(1)}, u32[]{:S(2)}, u32[]{:S(2)}) collective-permute-start(s32[2,128]{1,0:T(2,128)S(1)} %pad_add_fusion.1), channel_id=1, source_target_pairs={{0,4},{12,8},{1,5},{13,9},{2,6},{14,10},{3,7},{15,11},{16,20},{28,... | collective-permute-start | bytes 3080 | tf_op jit(solution)/shard_map/ppermute | solution.py:413
  8.0 16.6 %collective-permute-start.1 = (s32[2,128]{1,0:T(2,128)S(1)}, s32[2,128]{1,0:T(2,128)S(1)}, u32[]{:S(2)}, u32[]{:S(2)}) collective-permute-start(s32[2,128]{1,0:T(2,128)S(1)} %pad_add_fusion.1), channel_id=1, source_target_pairs={{4,8},{8,4},{5,9},{9,5},{6,10},{10,6},{7,11},{11,7},{20,24},{24,20... | collective-permute-start | bytes 3080 | tf_op jit(solution)/shard_map/ppermute | solution.py:413
  14.5 51.2 %collective-permute-start.4 = (bf16[2,16,2,64,128]{4,3,2,1,0:T(8,128)(2,1)}, bf16[2,16,2,64,128]{4,3,2,1,0:T(8,128)(2,1)S(1)}, u32[]{:S(2)}, u32[]{:S(2)}) collective-permute-start(bf16[2,16,2,64,128]{4,3,2,1,0:T(8,128)(2,1)} %bitcast.224), channel_id=1, source_target_pairs={{4,8},{8,4},{5,9},{9,5},{6,10},{10,6},{7,11},{11,7},{20,24},{24,20... | collective-permute-start | bytes 3145736 | tf_op jit(solution)/shard_map/ppermute | solution.py:423
  15.2 50.4 %collective-permute-start.5 = (bf16[2,16,2,64,128]{4,3,2,1,0:T(8,128)(2,1)}, bf16[2,16,2,64,128]{4,3,2,1,0:T(8,128)(2,1)S(1)}, u32[]{:S(2)}, u32[]{:S(2)}) collective-permute-start(bf16[2,16,2,64,128]{4,3,2,1,0:T(8,128)(2,1)} %bitcast.225), channel_id=1, source_target_pairs={{0,8},{12,4},{1,9},{13,5},{2,10},{14,6},{3,11},{15,7},{16,24},{28,... | collective-permute-start | bytes 3145736 | tf_op jit(solution)/shard_map/ppermute | solution.py:423
  23.2 42.4 %collective-permute-start.3 = (bf16[2,16,2,64,128]{4,3,2,1,0:T(8,128)(2,1)}, bf16[2,16,2,64,128]{4,3,2,1,0:T(8,128)(2,1)S(1)}, u32[]{:S(2)}, u32[]{:S(2)}) collective-permute-start(bf16[2,16,2,64,128]{4,3,2,1,0:T(8,128)(2,1)} %bitcast.187), channel_id=1, source_target_pairs={{0,4},{12,8},{1,5},{13,9},{2,6},{14,10},{3,7},{15,11},{16,20},{28,... | collective-permute-start | bytes 3145736 | tf_op jit(solution)/shard_map/ppermute | solution.py:423
  72.5 7.6 %collective-permute-start.6 = (bf16[16,128,256]{2,1,0:T(8,128)(2,1)}, bf16[16,128,256]{2,1,0:T(8,128)(2,1)S(1)}, u32[]{:S(2)}, u32[]{:S(2)}) collective-permute-start(bf16[16,128,256]{2,1,0:T(8,128)(2,1)} %beam_sums.10), channel_id=1, source_target_pairs={{0,16},{1,17},{2,18},{3,19},{4,20},{5,21},{6,22},{7,23},{8,24},{9,... | collective-permute-start | bytes 3145736 | tf_op jit(solution)/shard_map/ppermute | solution.py:22
  92.1 9.9 %collective-permute-start.7 = (bf16[16,128,256]{2,1,0:T(8,128)(2,1)}, bf16[16,128,256]{2,1,0:T(8,128)(2,1)}, u32[]{:S(2)}, u32[]{:S(2)}) collective-permute-start(bf16[16,128,256]{2,1,0:T(8,128)(2,1)} %beam_sums.11), channel_id=1, source_target_pairs={{0,16},{1,17},{2,18},{3,19},{4,20},{5,21},{6,22},{7,23},{8,24},{9,... | collective-permute-start | bytes 3145736 | tf_op jit(solution)/shard_map/ppermute | solution.py:22
  94.3 28.1 %collective-permute-start.8 = (bf16[2,16,2,64,128]{4,3,2,1,0:T(8,128)(2,1)}, bf16[2,16,2,64,128]{4,3,2,1,0:T(8,128)(2,1)S(1)}, u32[]{:S(2)}, u32[]{:S(2)}) collective-permute-start(bf16[2,16,2,64,128]{4,3,2,1,0:T(8,128)(2,1)} %bitcast.190), channel_id=1, source_target_pairs={{0,4},{12,8},{1,5},{13,9},{2,6},{14,10},{3,7},{15,11},{16,20},{28,... | collective-permute-start | bytes 3145736 | tf_op jit(solution)/shard_map/ppermute | solution.py:423
  98.7 42.8 %collective-permute-start.10 = (bf16[2,16,2,64,128]{4,3,2,1,0:T(8,128)(2,1)}, bf16[2,16,2,64,128]{4,3,2,1,0:T(8,128)(2,1)S(1)}, u32[]{:S(2)}, u32[]{:S(2)}) collective-permute-start(bf16[2,16,2,64,128]{4,3,2,1,0:T(8,128)(2,1)} %bitcast.226), channel_id=1, source_target_pairs={{0,8},{12,4},{1,9},{13,5},{2,10},{14,6},{3,11},{15,7},{16,24},{28,... | collective-permute-start | bytes 3145736 | tf_op jit(solution)/shard_map/ppermute | solution.py:423
  100.0 41.4 %collective-permute-start.9 = (bf16[2,16,2,64,128]{4,3,2,1,0:T(8,128)(2,1)}, bf16[2,16,2,64,128]{4,3,2,1,0:T(8,128)(2,1)S(1)}, u32[]{:S(2)}, u32[]{:S(2)}) collective-permute-start(bf16[2,16,2,64,128]{4,3,2,1,0:T(8,128)(2,1)} %bitcast.227), channel_id=1, source_target_pairs={{4,8},{8,4},{5,9},{9,5},{6,10},{10,6},{7,11},{11,7},{20,24},{24,20... | collective-permute-start | bytes 3145736 | tf_op jit(solution)/shard_map/ppermute | solution.py:423
  147.3 187.1 %copy-start.29 = (f32[4,16,128]{2,1,0:T(8,128)S(1)}, f32[4,16,128]{2,1,0:T(8,128)}, u32[]{:S(2)}) copy-start(f32[4,16,128]{2,1,0:T(8,128)} %get-tuple-element.159) | copy-start | bytes 98308
  147.3 187.2 %copy-start.30 = (f32[4,16,128]{2,1,0:T(8,128)S(1)}, f32[4,16,128]{2,1,0:T(8,128)}, u32[]{:S(2)}) copy-start(f32[4,16,128]{2,1,0:T(8,128)} %get-tuple-element.160) | copy-start | bytes 98308
  147.3 6.0 collective-permute-start.11
  160.2 191.6 %copy-start.31 = (f32[4,16,128]{2,1,0:T(8,128)S(1)}, f32[4,16,128]{2,1,0:T(8,128)}, u32[]{:S(2)}) copy-start(f32[4,16,128]{2,1,0:T(8,128)} %get-tuple-element.161) | copy-start | bytes 98308
  164.8 14.4 %collective-permute-start.12 = (bf16[16,128,256]{2,1,0:T(8,128)(2,1)}, bf16[16,128,256]{2,1,0:T(8,128)(2,1)}, u32[]{:S(2)}, u32[]{:S(2)}) collective-permute-start(bf16[16,128,256]{2,1,0:T(8,128)(2,1)} %beam_sums.13), channel_id=1, source_target_pairs={{0,16},{1,17},{2,18},{3,19},{4,20},{5,21},{6,22},{7,23},{8,24},{9,... | collective-permute-start | bytes 3145736 | tf_op jit(solution)/shard_map/ppermute | solution.py:22
  167.1 30.3 %collective-permute-start.13 = (bf16[2,16,2,64,128]{4,3,2,1,0:T(8,128)(2,1)}, bf16[2,16,2,64,128]{4,3,2,1,0:T(8,128)(2,1)S(1)}, u32[]{:S(2)}, u32[]{:S(2)}) collective-permute-start(bf16[2,16,2,64,128]{4,3,2,1,0:T(8,128)(2,1)} %bitcast.173), channel_id=1, source_target_pairs={{0,4},{12,8},{1,5},{13,9},{2,6},{14,10},{3,7},{15,11},{16,20},{28,... | collective-permute-start | bytes 3145736 | tf_op jit(solution)/shard_map/ppermute | solution.py:423
  173.6 23.8 %collective-permute-start.14 = (bf16[2,16,2,64,128]{4,3,2,1,0:T(8,128)(2,1)}, bf16[2,16,2,64,128]{4,3,2,1,0:T(8,128)(2,1)S(1)}, u32[]{:S(2)}, u32[]{:S(2)}) collective-permute-start(bf16[2,16,2,64,128]{4,3,2,1,0:T(8,128)(2,1)} %bitcast.230), channel_id=1, source_target_pairs={{4,8},{8,4},{5,9},{9,5},{6,10},{10,6},{7,11},{11,7},{20,24},{24,20... | collective-permute-start | bytes 3145736 | tf_op jit(solution)/shard_map/ppermute | solution.py:423
  174.4 41.9 %collective-permute-start.15 = (bf16[2,16,2,64,128]{4,3,2,1,0:T(8,128)(2,1)}, bf16[2,16,2,64,128]{4,3,2,1,0:T(8,128)(2,1)S(1)}, u32[]{:S(2)}, u32[]{:S(2)}) collective-permute-start(bf16[2,16,2,64,128]{4,3,2,1,0:T(8,128)(2,1)} %bitcast.231), channel_id=1, source_target_pairs={{0,8},{12,4},{1,9},{13,5},{2,10},{14,6},{3,11},{15,7},{16,24},{28,... | collective-permute-start | bytes 3145736 | tf_op jit(solution)/shard_map/ppermute | solution.py:423
  221.8 3.8 collective-permute-start.16
  236.9 18.2 %collective-permute-start.17 = (bf16[16,64,256]{2,1,0:T(8,128)(2,1)}, bf16[16,64,256]{2,1,0:T(8,128)(2,1)}, u32[]{:S(2)}, u32[]{:S(2)}) collective-permute-start(bf16[16,64,256]{2,1,0:T(8,128)(2,1)} %beam_sums.15), channel_id=1, source_target_pairs={{0,16},{1,17},{2,18},{3,19},{4,20},{5,21},{6,22},{7,23},{8,24},{9,... | collective-permute-start | bytes 1572872 | tf_op jit(solution)/shard_map/ppermute | solution.py:22
  243.6 29.7 %collective-permute-start.19 = (bf16[2,16,2,64,128]{4,3,2,1,0:T(8,128)(2,1)}, bf16[2,16,2,64,128]{4,3,2,1,0:T(8,128)(2,1)S(1)}, u32[]{:S(2)}, u32[]{:S(2)}) collective-permute-start(bf16[2,16,2,64,128]{4,3,2,1,0:T(8,128)(2,1)} %bitcast.177), channel_id=1, source_target_pairs={{0,4},{12,8},{1,5},{13,9},{2,6},{14,10},{3,7},{15,11},{16,20},{28,... | collective-permute-start | bytes 3145736 | tf_op jit(solution)/shard_map/ppermute | solution.py:423
  249.6 23.8 %collective-permute-start.20 = (bf16[2,16,2,64,128]{4,3,2,1,0:T(8,128)(2,1)}, bf16[2,16,2,64,128]{4,3,2,1,0:T(8,128)(2,1)S(1)}, u32[]{:S(2)}, u32[]{:S(2)}) collective-permute-start(bf16[2,16,2,64,128]{4,3,2,1,0:T(8,128)(2,1)} %bitcast.228), channel_id=1, source_target_pairs={{4,8},{8,4},{5,9},{9,5},{6,10},{10,6},{7,11},{11,7},{20,24},{24,20... | collective-permute-start | bytes 3145736 | tf_op jit(solution)/shard_map/ppermute | solution.py:423
  250.3 43.2 %collective-permute-start.21 = (bf16[2,16,2,64,128]{4,3,2,1,0:T(8,128)(2,1)}, bf16[2,16,2,64,128]{4,3,2,1,0:T(8,128)(2,1)S(1)}, u32[]{:S(2)}, u32[]{:S(2)}) collective-permute-start(bf16[2,16,2,64,128]{4,3,2,1,0:T(8,128)(2,1)} %bitcast.229), channel_id=1, source_target_pairs={{0,8},{12,4},{1,9},{13,5},{2,10},{14,6},{3,11},{15,7},{16,24},{28,... | collective-permute-start | bytes 3145736 | tf_op jit(solution)/shard_map/ppermute | solution.py:423
  263.3 3.1 collective-permute-start.18
  299.0 5.1 collective-permute-start.22
  300.4 30.7 %collective-permute-start.27 = (bf16[4,2,16,32,128]{4,3,2,1,0:T(8,128)(2,1)}, bf16[4,2,16,32,128]{4,3,2,1,0:T(8,128)(2,1)}, u32[]{:S(2)}, u32[]{:S(2)}) collective-permute-start(bf16[4,2,16,32,128]{4,3,2,1,0:T(8,128)(2,1)} %get-tuple-element.107.refs_4_), channel_id=1, source_target_pairs={{4,0},{8,12},{5,1},{9,13},{6,2},{10,14},{7,3},{11,15},{20,16},{24,... | collective-permute-start | bytes 3145736 | tf_op jit(solution)/shard_map/ppermute | solution.py:440
  301.7 31.5 %collective-permute-start.41 = (bf16[4,2,16,32,128]{4,3,2,1,0:T(8,128)(2,1)}, bf16[4,2,16,32,128]{4,3,2,1,0:T(8,128)(2,1)}, u32[]{:S(2)}, u32[]{:S(2)}) collective-permute-start(bf16[4,2,16,32,128]{4,3,2,1,0:T(8,128)(2,1)} %get-tuple-element.107.refs_4_), channel_id=1, source_target_pairs={{4,8},{8,4},{5,9},{9,5},{6,10},{10,6},{7,11},{11,7},{20,24},{24,20... | collective-permute-start | bytes 3145736 | tf_op jit(solution)/shard_map/ppermute | solution.py:442
  311.1 204.5 %copy-start.6 = (bf16[4,2,16,32,128]{4,3,2,1,0:T(8,128)(2,1)S(1)}, bf16[4,2,16,32,128]{4,3,2,1,0:T(8,128)(2,1)}, u32[]{:S(2)}) copy-start(bf16[4,2,16,32,128]{4,3,2,1,0:T(8,128)(2,1)} %get-tuple-element.186.refs_4_) | copy-start | bytes 3145732
  311.1 204.5 %copy-start.7 = (bf16[4,2,16,32,128]{4,3,2,1,0:T(8,128)(2,1)S(1)}, bf16[4,2,16,32,128]{4,3,2,1,0:T(8,128)(2,1)}, u32[]{:S(2)}) copy-start(bf16[4,2,16,32,128]{4,3,2,1,0:T(8,128)(2,1)} %get-tuple-element.192.refs_6_) | copy-start | bytes 3145732
  315.7 5.1 collective-permute-start.23
  317.8 32.8 %collective-permute-start.28 = (bf16[4,2,16,32,128]{4,3,2,1,0:T(8,128)(2,1)}, bf16[4,2,16,32,128]{4,3,2,1,0:T(8,128)(2,1)S(1)}, u32[]{:S(2)}, u32[]{:S(2)}) collective-permute-start(bf16[4,2,16,32,128]{4,3,2,1,0:T(8,128)(2,1)} %get-tuple-element.112.refs_4_), channel_id=1, source_target_pairs={{4,0},{8,12},{5,1},{9,13},{6,2},{10,14},{7,3},{11,15},{20,16},{24,... | collective-permute-start | bytes 3145736 | tf_op jit(solution)/shard_map/ppermute | solution.py:440
  319.1 33.0 %collective-permute-start.39 = (bf16[4,2,16,32,128]{4,3,2,1,0:T(8,128)(2,1)}, bf16[4,2,16,32,128]{4,3,2,1,0:T(8,128)(2,1)}, u32[]{:S(2)}, u32[]{:S(2)}) collective-permute-start(bf16[4,2,16,32,128]{4,3,2,1,0:T(8,128)(2,1)} %get-tuple-element.112.refs_4_), channel_id=1, source_target_pairs={{4,8},{8,4},{5,9},{9,5},{6,10},{10,6},{7,11},{11,7},{20,24},{24,20... | collective-permute-start | bytes 3145736 | tf_op jit(solution)/shard_map/ppermute | solution.py:442
  320.7 52.4 %collective-permute-start.29 = (bf16[4,2,16,32,128]{4,3,2,1,0:T(8,128)(2,1)}, bf16[4,2,16,32,128]{4,3,2,1,0:T(8,128)(2,1)}, u32[]{:S(2)}, u32[]{:S(2)}) collective-permute-start(bf16[4,2,16,32,128]{4,3,2,1,0:T(8,128)(2,1)} %get-tuple-element.175.refs_6_), channel_id=1, source_target_pairs={{4,0},{8,12},{5,1},{9,13},{6,2},{10,14},{7,3},{11,15},{20,16},{24,... | collective-permute-start | bytes 3145736 | tf_op jit(solution)/shard_map/ppermute | solution.py:440
  331.0 22.3 %collective-permute-start.24 = (bf16[16,64,256]{2,1,0:T(8,128)(2,1)}, bf16[16,64,256]{2,1,0:T(8,128)(2,1)}, u32[]{:S(2)}, u32[]{:S(2)}) collective-permute-start(bf16[16,64,256]{2,1,0:T(8,128)(2,1)} %beam_sums.19), channel_id=1, source_target_pairs={{0,16},{1,17},{2,18},{3,19},{4,20},{5,21},{6,22},{7,23},{8,24},{9,... | collective-permute-start | bytes 1572872 | tf_op jit(solution)/shard_map/ppermute | solution.py:22
  333.1 62.5 %collective-permute-start.30 = (bf16[4,2,16,32,128]{4,3,2,1,0:T(8,128)(2,1)}, bf16[4,2,16,32,128]{4,3,2,1,0:T(8,128)(2,1)}, u32[]{:S(2)}, u32[]{:S(2)}) collective-permute-start(bf16[4,2,16,32,128]{4,3,2,1,0:T(8,128)(2,1)} %get-tuple-element.184.refs_6_), channel_id=1, source_target_pairs={{4,0},{8,12},{5,1},{9,13},{6,2},{10,14},{7,3},{11,15},{20,16},{24,... | collective-permute-start | bytes 3145736 | tf_op jit(solution)/shard_map/ppermute | solution.py:440
  350.5 167.5 %copy-start.8 = (bf16[4,2,16,32,128]{4,3,2,1,0:T(8,128)(2,1)}, bf16[4,2,16,32,128]{4,3,2,1,0:T(8,128)(2,1)S(1)}, u32[]{:S(2)}) copy-start(bf16[4,2,16,32,128]{4,3,2,1,0:T(8,128)(2,1)S(1)} %collective-permute-done.28.refs_5_) | copy-start | bytes 3145732
  350.5 82.7 %collective-permute-start.31 = (bf16[4,2,16,32,128]{4,3,2,1,0:T(8,128)(2,1)}, bf16[4,2,16,32,128]{4,3,2,1,0:T(8,128)(2,1)}, u32[]{:S(2)}, u32[]{:S(2)}) collective-permute-start(bf16[4,2,16,32,128]{4,3,2,1,0:T(8,128)(2,1)} %get-tuple-element.186.refs_4_), channel_id=1, source_target_pairs={{4,0},{8,12},{5,1},{9,13},{6,2},{10,14},{7,3},{11,15},{20,16},{24,... | collective-permute-start | bytes 3145736 | tf_op jit(solution)/shard_map/ppermute | solution.py:440
  352.0 77.3 %collective-permute-start.32 = (bf16[2,2,16,32,128]{4,3,2,1,0:T(8,128)(2,1)}, bf16[2,2,16,32,128]{4,3,2,1,0:T(8,128)(2,1)}, u32[]{:S(2)}, u32[]{:S(2)}) collective-permute-start(bf16[2,2,16,32,128]{4,3,2,1,0:T(8,128)(2,1)} %get-tuple-element.188.refs_4_), channel_id=1, source_target_pairs={{4,0},{8,12},{5,1},{9,13},{6,2},{10,14},{7,3},{11,15},{20,16},{24,... | collective-permute-start | bytes 1572872 | tf_op jit(solution)/shard_map/ppermute | solution.py:440
  353.4 110.9 %collective-permute-start.34 = (bf16[4,2,16,32,128]{4,3,2,1,0:T(8,128)(2,1)}, bf16[4,2,16,32,128]{4,3,2,1,0:T(8,128)(2,1)}, u32[]{:S(2)}, u32[]{:S(2)}) collective-permute-start(bf16[4,2,16,32,128]{4,3,2,1,0:T(8,128)(2,1)} %get-tuple-element.192.refs_6_), channel_id=1, source_target_pairs={{4,0},{8,12},{5,1},{9,13},{6,2},{10,14},{7,3},{11,15},{20,16},{24,... | collective-permute-start | bytes 3145736 | tf_op jit(solution)/shard_map/ppermute | solution.py:440
  373.1 57.5 %collective-permute-start.25 = (f32[2,8,16]{2,1,0:T(8,128)S(1)}, f32[2,8,16]{2,1,0:T(8,128)S(1)}, u32[]{:S(2)}, u32[]{:S(2)}) collective-permute-start(f32[2,8,16]{2,1,0:T(8,128)S(1)} %psum.7), channel_id=1, source_target_pairs={{4,8},{8,4},{5,9},{9,5},{6,10},{10,6},{7,11},{11,7},{20,24},{24,20... | collective-permute-start | bytes 3080 | tf_op jit(solution)/shard_map/ppermute | solution.py:448
  395.6 67.4 %collective-permute-start.33 = (bf16[2,2,16,32,128]{4,3,2,1,0:T(8,128)(2,1)}, bf16[2,2,16,32,128]{4,3,2,1,0:T(8,128)(2,1)}, u32[]{:S(2)}, u32[]{:S(2)}) collective-permute-start(bf16[2,2,16,32,128]{4,3,2,1,0:T(8,128)(2,1)} %get-tuple-element.190.refs_4_), channel_id=1, source_target_pairs={{4,0},{8,12},{5,1},{9,13},{6,2},{10,14},{7,3},{11,15},{20,16},{24,... | collective-permute-start | bytes 1572872 | tf_op jit(solution)/shard_map/ppermute | solution.py:440
  429.3 44.9 %collective-permute-start.35 = (bf16[2,2,16,32,128]{4,3,2,1,0:T(8,128)(2,1)}, bf16[2,2,16,32,128]{4,3,2,1,0:T(8,128)(2,1)}, u32[]{:S(2)}, u32[]{:S(2)}) collective-permute-start(bf16[2,2,16,32,128]{4,3,2,1,0:T(8,128)(2,1)} %get-tuple-element.194.refs_6_), channel_id=1, source_target_pairs={{4,0},{8,12},{5,1},{9,13},{6,2},{10,14},{7,3},{11,15},{20,16},{24,... | collective-permute-start | bytes 1572872 | tf_op jit(solution)/shard_map/ppermute | solution.py:440
  430.6 56.8 %collective-permute-start.36 = (bf16[2,2,16,32,128]{4,3,2,1,0:T(8,128)(2,1)}, bf16[2,2,16,32,128]{4,3,2,1,0:T(8,128)(2,1)}, u32[]{:S(2)}, u32[]{:S(2)}) collective-permute-start(bf16[2,2,16,32,128]{4,3,2,1,0:T(8,128)(2,1)} %get-tuple-element.196.refs_6_), channel_id=1, source_target_pairs={{4,0},{8,12},{5,1},{9,13},{6,2},{10,14},{7,3},{11,15},{20,16},{24,... | collective-permute-start | bytes 1572872 | tf_op jit(solution)/shard_map/ppermute | solution.py:440
  433.3 52.5 %collective-permute-start.26 = (f32[2,2,8,16]{3,2,1,0:T(8,128)S(1)}, f32[2,2,8,16]{3,2,1,0:T(8,128)S(1)}, u32[]{:S(2)}, u32[]{:S(2)}) collective-permute-start(f32[2,2,8,16]{3,2,1,0:T(8,128)S(1)} %pad_maximum_fusion), channel_id=1, source_target_pairs={{4,0},{8,12},{5,1},{9,13},{6,2},{10,14},{7,3},{11,15},{20,16},{24,... | collective-permute-start | bytes 6152 | tf_op jit(solution)/shard_map/ppermute | solution.py:453
  463.0 83.7 %collective-permute-start.42 = (bf16[4,2,16,32,128]{4,3,2,1,0:T(8,128)(2,1)}, bf16[4,2,16,32,128]{4,3,2,1,0:T(8,128)(2,1)}, u32[]{:S(2)}, u32[]{:S(2)}) collective-permute-start(bf16[4,2,16,32,128]{4,3,2,1,0:T(8,128)(2,1)} %collective-permute-done.41.refs_4_), channel_id=1, source_target_pairs={{4,0},{8,12},{5,1},{9,13},{6,2},{10,14},{7,3},{11,15},{20,16},{24,... | collective-permute-start | bytes 3145736 | tf_op jit(solution)/shard_map/ppermute | solution.py:464
  464.3 83.9 %collective-permute-start.40 = (bf16[4,2,16,32,128]{4,3,2,1,0:T(8,128)(2,1)}, bf16[4,2,16,32,128]{4,3,2,1,0:T(8,128)(2,1)}, u32[]{:S(2)}, u32[]{:S(2)}) collective-permute-start(bf16[4,2,16,32,128]{4,3,2,1,0:T(8,128)(2,1)} %collective-permute-done.39.refs_4_), channel_id=1, source_target_pairs={{4,0},{8,12},{5,1},{9,13},{6,2},{10,14},{7,3},{11,15},{20,16},{24,... | collective-permute-start | bytes 3145736 | tf_op jit(solution)/shard_map/ppermute | solution.py:464
  474.2 20.1 %collective-permute-start.37 = (bf16[4,2,16,32,128]{4,3,2,1,0:T(8,128)(2,1)}, bf16[4,2,16,32,128]{4,3,2,1,0:T(8,128)(2,1)}, u32[]{:S(2)}, u32[]{:S(2)}) collective-permute-start(bf16[4,2,16,32,128]{4,3,2,1,0:T(8,128)(2,1)} %get-tuple-element.175.refs_6_), channel_id=1, source_target_pairs={{4,8},{8,4},{5,9},{9,5},{6,10},{10,6},{7,11},{11,7},{20,24},{24,20... | collective-permute-start | bytes 3145736 | tf_op jit(solution)/shard_map/ppermute | solution.py:451
  485.7 10.0 %collective-permute-start.43 = (bf16[4,2,16,32,128]{4,3,2,1,0:T(8,128)(2,1)}, bf16[4,2,16,32,128]{4,3,2,1,0:T(8,128)(2,1)}, u32[]{:S(2)}, u32[]{:S(2)}) collective-permute-start(bf16[4,2,16,32,128]{4,3,2,1,0:T(8,128)(2,1)} %get-tuple-element.184.refs_6_), channel_id=1, source_target_pairs={{4,8},{8,4},{5,9},{9,5},{6,10},{10,6},{7,11},{11,7},{20,24},{24,20... | collective-permute-start | bytes 3145736 | tf_op jit(solution)/shard_map/ppermute | solution.py:451
  487.4 9.9 %collective-permute-start.44 = (bf16[4,2,16,32,128]{4,3,2,1,0:T(8,128)(2,1)}, bf16[4,2,16,32,128]{4,3,2,1,0:T(8,128)(2,1)}, u32[]{:S(2)}, u32[]{:S(2)}) collective-permute-start(bf16[4,2,16,32,128]{4,3,2,1,0:T(8,128)(2,1)} %get-tuple-element.186.refs_4_), channel_id=1, source_target_pairs={{4,8},{8,4},{5,9},{9,5},{6,10},{10,6},{7,11},{11,7},{20,24},{24,20... | collective-permute-start | bytes 3145736 | tf_op jit(solution)/shard_map/ppermute | solution.py:451
  494.3 55.2 %collective-permute-start.45 = (bf16[2,2,16,32,128]{4,3,2,1,0:T(8,128)(2,1)}, bf16[2,2,16,32,128]{4,3,2,1,0:T(8,128)(2,1)}, u32[]{:S(2)}, u32[]{:S(2)}) collective-permute-start(bf16[2,2,16,32,128]{4,3,2,1,0:T(8,128)(2,1)} %get-tuple-element.188.refs_4_), channel_id=1, source_target_pairs={{4,8},{8,4},{5,9},{9,5},{6,10},{10,6},{7,11},{11,7},{20,24},{24,20... | collective-permute-start | bytes 1572872 | tf_op jit(solution)/shard_map/ppermute | solution.py:451
  495.8 55.1 %collective-permute-start.46 = (bf16[2,2,16,32,128]{4,3,2,1,0:T(8,128)(2,1)}, bf16[2,2,16,32,128]{4,3,2,1,0:T(8,128)(2,1)}, u32[]{:S(2)}, u32[]{:S(2)}) collective-permute-start(bf16[2,2,16,32,128]{4,3,2,1,0:T(8,128)(2,1)} %get-tuple-element.190.refs_4_), channel_id=1, source_target_pairs={{4,8},{8,4},{5,9},{9,5},{6,10},{10,6},{7,11},{11,7},{20,24},{24,20... | collective-permute-start | bytes 1572872 | tf_op jit(solution)/shard_map/ppermute | solution.py:451
  497.3 76.1 %collective-permute-start.47 = (bf16[4,2,16,32,128]{4,3,2,1,0:T(8,128)(2,1)}, bf16[4,2,16,32,128]{4,3,2,1,0:T(8,128)(2,1)}, u32[]{:S(2)}, u32[]{:S(2)}) collective-permute-start(bf16[4,2,16,32,128]{4,3,2,1,0:T(8,128)(2,1)} %get-tuple-element.192.refs_6_), channel_id=1, source_target_pairs={{4,8},{8,4},{5,9},{9,5},{6,10},{10,6},{7,11},{11,7},{20,24},{24,20... | collective-permute-start | bytes 3145736 | tf_op jit(solution)/shard_map/ppermute | solution.py:451
  546.7 36.3 %collective-permute-start.48 = (bf16[2,2,16,32,128]{4,3,2,1,0:T(8,128)(2,1)S(1)}, bf16[2,2,16,32,128]{4,3,2,1,0:T(8,128)(2,1)}, u32[]{:S(2)}, u32[]{:S(2)}) collective-permute-start(bf16[2,2,16,32,128]{4,3,2,1,0:T(8,128)(2,1)S(1)} %copy-done.17), channel_id=1, source_target_pairs={{4,8},{8,4},{5,9},{9,5},{6,10},{10,6},{7,11},{11,7},{20,24},{24,20... | collective-permute-start | bytes 1572872 | tf_op jit(solution)/shard_map/ppermute | solution.py:451
  548.2 78.1 %collective-permute-start.38 = (bf16[4,2,16,32,128]{4,3,2,1,0:T(8,128)(2,1)}, bf16[4,2,16,32,128]{4,3,2,1,0:T(8,128)(2,1)}, u32[]{:S(2)}, u32[]{:S(2)}) collective-permute-start(bf16[4,2,16,32,128]{4,3,2,1,0:T(8,128)(2,1)} %collective-permute-done.37.refs_4_), channel_id=1, source_target_pairs={{4,0},{8,12},{5,1},{9,13},{6,2},{10,14},{7,3},{11,15},{20,16},{24,... | collective-permute-start | bytes 3145736 | tf_op jit(solution)/shard_map/ppermute | solution.py:464
  549.5 99.2 %collective-permute-start.56 = (bf16[4,2,16,32,128]{4,3,2,1,0:T(8,128)(2,1)}, bf16[4,2,16,32,128]{4,3,2,1,0:T(8,128)(2,1)S(1)}, u32[]{:S(2)}, u32[]{:S(2)}) collective-permute-start(bf16[4,2,16,32,128]{4,3,2,1,0:T(8,128)(2,1)} %collective-permute-done.43.refs_4_), channel_id=1, source_target_pairs={{4,0},{8,12},{5,1},{9,13},{6,2},{10,14},{7,3},{11,15},{20,16},{24,... | collective-permute-start | bytes 3145736 | tf_op jit(solution)/shard_map/ppermute | solution.py:464
  550.8 120.5 %collective-permute-start.55 = (bf16[4,2,16,32,128]{4,3,2,1,0:T(8,128)(2,1)}, bf16[4,2,16,32,128]{4,3,2,1,0:T(8,128)(2,1)}, u32[]{:S(2)}, u32[]{:S(2)}) collective-permute-start(bf16[4,2,16,32,128]{4,3,2,1,0:T(8,128)(2,1)} %collective-permute-done.44.refs_4_), channel_id=1, source_target_pairs={{4,0},{8,12},{5,1},{9,13},{6,2},{10,14},{7,3},{11,15},{20,16},{24,... | collective-permute-start | bytes 3145736 | tf_op jit(solution)/shard_map/ppermute | solution.py:464
  573.5 63.1 %collective-permute-start.49 = (bf16[2,2,16,32,128]{4,3,2,1,0:T(8,128)(2,1)S(1)}, bf16[2,2,16,32,128]{4,3,2,1,0:T(8,128)(2,1)S(1)}, u32[]{:S(2)}, u32[]{:S(2)}) collective-permute-start(bf16[2,2,16,32,128]{4,3,2,1,0:T(8,128)(2,1)S(1)} %copy-done.19), channel_id=1, source_target_pairs={{4,8},{8,4},{5,9},{9,5},{6,10},{10,6},{7,11},{11,7},{20,24},{24,20... | collective-permute-start | bytes 1572872 | tf_op jit(solution)/shard_map/ppermute | solution.py:451
  583.1 135.4 %collective-permute-start.52 = (bf16[4,2,16,32,128]{4,3,2,1,0:T(8,128)(2,1)}, bf16[4,2,16,32,128]{4,3,2,1,0:T(8,128)(2,1)S(1)}, u32[]{:S(2)}, u32[]{:S(2)}) collective-permute-start(bf16[4,2,16,32,128]{4,3,2,1,0:T(8,128)(2,1)} %collective-permute-done.47.refs_4_), channel_id=1, source_target_pairs={{4,0},{8,12},{5,1},{9,13},{6,2},{10,14},{7,3},{11,15},{20,16},{24,... | collective-permute-start | bytes 3145736 | tf_op jit(solution)/shard_map/ppermute | solution.py:464
  626.4 78.6 %collective-permute-start.54 = (bf16[2,2,16,32,128]{4,3,2,1,0:T(8,128)(2,1)}, bf16[2,2,16,32,128]{4,3,2,1,0:T(8,128)(2,1)}, u32[]{:S(2)}, u32[]{:S(2)}) collective-permute-start(bf16[2,2,16,32,128]{4,3,2,1,0:T(8,128)(2,1)} %collective-permute-done.45.refs_4_), channel_id=1, source_target_pairs={{4,0},{8,12},{5,1},{9,13},{6,2},{10,14},{7,3},{11,15},{20,16},{24,... | collective-permute-start | bytes 1572872 | tf_op jit(solution)/shard_map/ppermute | solution.py:464
  636.6 76.1 %collective-permute-start.53 = (bf16[2,2,16,32,128]{4,3,2,1,0:T(8,128)(2,1)}, bf16[2,2,16,32,128]{4,3,2,1,0:T(8,128)(2,1)}, u32[]{:S(2)}, u32[]{:S(2)}) collective-permute-start(bf16[2,2,16,32,128]{4,3,2,1,0:T(8,128)(2,1)} %collective-permute-done.46.refs_4_), channel_id=1, source_target_pairs={{4,0},{8,12},{5,1},{9,13},{6,2},{10,14},{7,3},{11,15},{20,16},{24,... | collective-permute-start | bytes 1572872 | tf_op jit(solution)/shard_map/ppermute | solution.py:464
  648.7 79.6 %collective-permute-start.51 = (bf16[2,2,16,32,128]{4,3,2,1,0:T(8,128)(2,1)}, bf16[2,2,16,32,128]{4,3,2,1,0:T(8,128)(2,1)}, u32[]{:S(2)}, u32[]{:S(2)}) collective-permute-start(bf16[2,2,16,32,128]{4,3,2,1,0:T(8,128)(2,1)} %collective-permute-done.48.refs_4_), channel_id=1, source_target_pairs={{4,0},{8,12},{5,1},{9,13},{6,2},{10,14},{7,3},{11,15},{20,16},{24,... | collective-permute-start | bytes 1572872 | tf_op jit(solution)/shard_map/ppermute | solution.py:464
  671.3 62.8 %collective-permute-start.50 = (bf16[2,2,16,32,128]{4,3,2,1,0:T(8,128)(2,1)S(1)}, bf16[2,2,16,32,128]{4,3,2,1,0:T(8,128)(2,1)S(1)}, u32[]{:S(2)}, u32[]{:S(2)}) collective-permute-start(bf16[2,2,16,32,128]{4,3,2,1,0:T(8,128)(2,1)S(1)} %collective-permute-done.49.refs_4_), channel_id=1, source_target_pairs={{4,0},{8,12},{5,1},{9,13},{6,2},{10,14},{7,3},{11,15},{20,16},{24,... | collective-permute-start | bytes 1572872 | tf_op jit(solution)/shard_map/ppermute | solution.py:464
  (27 other events, 584.1 us)

commit v4 on v3

--- a/solution.py
+++ b/solution.py
@@ -112,25 +112,21 @@
             wide_ref[frame] = prev_ref[frames - history + frame].astype(jnp.float32)
         for frame in range(frames):
             wide_ref[history + frame] = cur_ref[frame].astype(jnp.float32)
-        groups = rows // 8
-
-        def filter_rows(index, carry):
-            comp = index // groups
-            low = pl.multiple_of(index % groups * 8, 8)
+        for comp in range(2):
             for tile in range(tiles):
                 lanes = slice(tile * LANES, (tile + 1) * LANES)
-                for frame in range(frames):
-                    terms = [
-                        taps_ref[tap, :, lanes] * wide_ref[history + frame - tap, comp, pl.ds(low, 8), lanes]
-                        for tap in range(taps_count)
-                    ]
-                    while len(terms) > 1:
-                        odd = terms[len(terms) // 2 * 2 :]
-                        terms = [a + b for a, b in zip(terms[::2], terms[1::2])] + odd
-                    filt_ref[comp, pl.ds(frame * rows + low, 8), lanes] = terms[0]
-            return carry
-
-        lax.fori_loop(0, 2 * groups, filter_rows, 0)
+                for low in range(0, rows, 8):
+                    for frame in range(frames):
+                        terms = [
+                            taps_ref[tap, :, lanes]
+                            * wide_ref[history + frame - tap, comp, low : low + 8, lanes]
+                            for tap in range(taps_count)
+                        ]
+                        while len(terms) > 1:
+                            terms = [
+                                a + b for a, b in zip(terms[::2], terms[1::2])
+                            ] + terms[len(terms) // 2 * 2 :]
+                        filt_ref[comp, frame * rows + low : frame * rows + low + 8, lanes] = terms[0]
         real_part = filt_ref[0].astype(jnp.bfloat16)
         imag_part = filt_ref[1].astype(jnp.bfloat16)
 
@@ -352,11 +348,9 @@
     return left.reshape(beams, own_count, unit, LANES), right.reshape(beams, blocks * own_count, unit, LANES)
 
 
-def beam_parts(beams, last):
+def beam_parts(beams):
     half = beams // 2
-    if not last:
-        return [(0, half), (half, half)]
-    return [(0, half), (half, half // 2), (half + half // 2, half - half // 2)]
+    return [(0, half), (half, beams - half)]
 
 
 def per_device(voltages, fir_taps, station_map, beam_index, weight_table):
@@ -412,7 +406,7 @@
         for path in paths:
             known.append(lax.ppermute(maps, "stn", path))
         maps = jnp.stack(known)
-        parts = [beam_parts(beams, coarse == coarse_dev - 1) for coarse in range(coarse_dev)]
+        parts = [beam_parts(beams) for _ in range(coarse_dev)]
         steps = [(coarse, step) for coarse in range(coarse_dev) for step in range(2)]
         arrived = []
         for coarse, step in steps:

time: 745 us -> 758 us (1.017)
  waiting for transfers between devices: 325 us -> 378 us
  Pallas kernels: 248 us -> 223 us
  starting transfers between devices: 106 us -> 96.8 us
    ppermute x10 -> x8, waiting for transfers between devices: 107 us -> 127 us  [per_device(): ends[coarse, step, part] = lax.ppermute(own, 'stn', outward)]
    ppermute x10 -> x8, waiting for transfers between devices: 80.7 us -> 97.9 us  [forward(): far_ends[keys[index]] = lax.ppermute(crossed[keys[index]], 'stn', outward)]
    ppermute x1, waiting for transfers between devices: 9.82 us -> 18.8 us  [per_device(): from_inner = lax.ppermute(both, 'stn', outward)]
    pallas_call x10 -> x8, Pallas kernels: 44.9 us -> 36.5 us  [beam_sums(): pl.pallas_call(body, grid=(frames // frames_step,), in_specs=[pl.BlockSpe...]
    pallas_call x15 -> x12, Pallas kernels: 137 us -> 129 us  [correlate(): pl.pallas_call(body, grid_spec=pltpu.PrefetchScalarGridSpec(num_scalar_pr...]
    pallas_call x10 -> x8, Pallas kernels: 51.4 us -> 43.3 us  [channelize(): pl.pallas_call(body, grid=(beams,), in_specs=[pl.BlockSpec((frames, 2, ro...]
    ppermute x10 -> x8, starting transfers between devices: 19.5 us -> 14.7 us  [shifted(): lax.ppermute(value, axis, [(source, source + steps) for source in range(f...]
  transfers between devices with their start and end apart: 57 -> 49, of which waited for: 21 -> 21; matrix products, arithmetic and copies ran while one was open for 5% -> 4% of each run, Pallas kernels for 26% -> 21%
where the time goes in v4:
time: 758 us; the launch traced here: 755 us
  waiting for transfers between devices  378 us (50%)
  Pallas kernels  223 us (29%)
  starting transfers between devices  96.8 us (13%)
  other arithmetic  22.9 us (3%)
  local copies, waits for them, and re-layouts  16.6 us (2%)
  blocking collectives  10.1 us (1%)
    ppermute x12, waiting for transfers between devices, per_device(): sources.append(lax.ppermute(sent, 'stn', path))  133 us
    pallas_call x12, Pallas kernels, correlate(): pl.pallas_call(body, grid_spec=pltpu.PrefetchScalarGridSpec(num_scalar_pr...  129 us
    ppermute x8, waiting for transfers between devices, per_device(): ends[coarse, step, part] = lax.ppermute(own, 'stn', outward)  127 us
    ppermute x8, waiting for transfers between devices, forward(): far_ends[keys[index]] = lax.ppermute(crossed[keys[index]], 'stn', outward)  97.9 us
    pallas_call x8, Pallas kernels, channelize(): pl.pallas_call(body, grid=(beams,), in_specs=[pl.BlockSpec((frames, 2, ro...  43.3 us
    ppermute x12, starting transfers between devices, per_device(): sources.append(lax.ppermute(sent, 'stn', path))  38.2 us
    pallas_call x8, Pallas kernels, beam_sums(): pl.pallas_call(body, grid=(frames // frames_step,), in_specs=[pl.BlockSpe...  36.5 us
    ppermute x1, waiting for transfers between devices, per_device(): from_inner = lax.ppermute(both, 'stn', outward)  18.8 us
  transfers between devices with their start and end apart: 49, of which 21 were waited for; matrix products, arithmetic and copies ran while one was open for 4% of the time, Pallas kernels for 21%

profile of v4, /device:TPU:0, one launch (start us, length us, event | category | flops | bytes accessed | tf_op | source)
XLA Modules:
  0.0 754.6 jit_solution(9779041300781383801)
XLA Ops:
  0.7 6.0 collective-permute-start.2
  10.8 3.6 sort_dishes.4
  15.1 5.8 collective-permute-start.5
  26.6 39.0 %collective-permute-done.3.refs_1_ = bf16[2,16,2,64,128]{4,3,2,1,0:T(8,128)(2,1)S(1)} collective-permute-done((bf16[2,16,2,64,128]{4,3,2,1,0:T(8,128)(2,1)}, bf16[2,16,2,64,128]{4,3,2,1,0:T(8,128)(2,1)S(1)}, u32[]{:S(2)}, u32[]{:S(2)}) %collective-permute-start.3) | collective-permute-done | bytes 1048608 | tf_op jit(solution)/shard_map/ppermute | solution.py:417
  67.9 4.5 beam_sums.8
  73.8 3.6 sort_dishes.5
  81.5 5.4 channelize.8
  86.9 4.6 beam_sums.9
  93.0 4.3 collective-permute-start.8
  102.5 5.4 channelize.9
  108.0 13.1 %collective-permute-done.8.refs_1_ = bf16[2,16,2,64,128]{4,3,2,1,0:T(8,128)(2,1)S(1)} collective-permute-done((bf16[2,16,2,64,128]{4,3,2,1,0:T(8,128)(2,1)}, bf16[2,16,2,64,128]{4,3,2,1,0:T(8,128)(2,1)S(1)}, u32[]{:S(2)}, u32[]{:S(2)}) %collective-permute-start.8) | collective-permute-done | bytes 1048608 | tf_op jit(solution)/shard_map/ppermute | solution.py:417
  121.1 19.9 %collective-permute-done.10.refs_3_ = bf16[2,16,2,64,128]{4,3,2,1,0:T(8,128)(2,1)S(1)} collective-permute-done((bf16[2,16,2,64,128]{4,3,2,1,0:T(8,128)(2,1)}, bf16[2,16,2,64,128]{4,3,2,1,0:T(8,128)(2,1)S(1)}, u32[]{:S(2)}, u32[]{:S(2)}) %collective-permute-start.10) | collective-permute-done | bytes 1048608 | tf_op jit(solution)/shard_map/ppermute | solution.py:417
  142.0 4.5 beam_sums.10
  147.9 3.6 sort_dishes.6
  153.3 5.4 channelize.10
  158.8 4.6 beam_sums.11
  164.7 6.0 collective-permute-start.13
  172.4 3.9 collective-permute-start.15
  178.1 5.4 channelize.11
  183.6 10.9 %collective-permute-done.13.refs_1_ = bf16[2,16,2,64,128]{4,3,2,1,0:T(8,128)(2,1)S(1)} collective-permute-done((bf16[2,16,2,64,128]{4,3,2,1,0:T(8,128)(2,1)}, bf16[2,16,2,64,128]{4,3,2,1,0:T(8,128)(2,1)S(1)}, u32[]{:S(2)}, u32[]{:S(2)}) %collective-permute-start.13) | collective-permute-done | bytes 1048608 | tf_op jit(solution)/shard_map/ppermute | solution.py:417
  194.5 19.8 %collective-permute-done.15.refs_3_ = bf16[2,16,2,64,128]{4,3,2,1,0:T(8,128)(2,1)} collective-permute-done((bf16[2,16,2,64,128]{4,3,2,1,0:T(8,128)(2,1)}, bf16[2,16,2,64,128]{4,3,2,1,0:T(8,128)(2,1)}, u32[]{:S(2)}, u32[]{:S(2)}) %collective-permute-start.15) | collective-permute-done | bytes 1048608 | tf_op jit(solution)/shard_map/ppermute | solution.py:417
  214.3 4.5 beam_sums.12
  220.2 3.6 sort_dishes.7
  225.7 5.4 channelize.12
  231.1 4.6 beam_sums.13
  238.0 5.7 collective-permute-start.18
  245.4 3.9 collective-permute-start.20
  250.1 5.4 channelize.13
  255.5 12.0 %collective-permute-done.18.refs_1_ = bf16[2,16,2,64,128]{4,3,2,1,0:T(8,128)(2,1)S(1)} collective-permute-done((bf16[2,16,2,64,128]{4,3,2,1,0:T(8,128)(2,1)}, bf16[2,16,2,64,128]{4,3,2,1,0:T(8,128)(2,1)S(1)}, u32[]{:S(2)}, u32[]{:S(2)}) %collective-permute-start.18) | collective-permute-done | bytes 1048608 | tf_op jit(solution)/shard_map/ppermute | solution.py:417
  267.5 18.8 %collective-permute-done.20.refs_3_ = bf16[2,16,2,64,128]{4,3,2,1,0:T(8,128)(2,1)} collective-permute-done((bf16[2,16,2,64,128]{4,3,2,1,0:T(8,128)(2,1)}, bf16[2,16,2,64,128]{4,3,2,1,0:T(8,128)(2,1)}, u32[]{:S(2)}, u32[]{:S(2)}) %collective-permute-start.20) | collective-permute-done | bytes 1048608 | tf_op jit(solution)/shard_map/ppermute | solution.py:417
  286.3 4.6 beam_sums.14
  294.9 5.4 channelize.14
  300.2 4.6 beam_sums.15
  304.8 3.2 collective-permute-start.22
  317.5 5.4 channelize.15
  323.8 10.1 %psum.7 = f32[2,8,16]{2,1,0:T(8,128)S(1)} all-reduce(f32[2,8,16]{2,1,0:T(8,128)S(1)} %maximum_add_fusion), channel_id=1, replica_groups=mesh['tm'=2,'stn'=4,'chan'=4] {'chan'}, use_global_device_ids=true, to_apply=%region_15.16 | all-reduce | flops 256 | bytes 2048 | tf_op jit(solution)/shard_map/psum | solution.py:441
  333.9 3.5 collective-permute-done.25.refs_5_
  338.1 21.8 %collective-permute-done.26.refs_5_ = bf16[4,2,16,32,128]{4,3,2,1,0:T(8,128)(2,1)} collective-permute-done((bf16[4,2,16,32,128]{4,3,2,1,0:T(8,128)(2,1)S(1)}, bf16[4,2,16,32,128]{4,3,2,1,0:T(8,128)(2,1)}, u32[]{:S(2)}, u32[]{:S(2)}) %collective-permute-start.26) | collective-permute-done | bytes 1048608 | tf_op jit(solution)/shard_map/ppermute | solution.py:434
  361.2 21.2 %collective-permute-done.27.refs_7_ = bf16[4,2,16,32,128]{4,3,2,1,0:T(8,128)(2,1)} collective-permute-done((bf16[4,2,16,32,128]{4,3,2,1,0:T(8,128)(2,1)}, bf16[4,2,16,32,128]{4,3,2,1,0:T(8,128)(2,1)}, u32[]{:S(2)}, u32[]{:S(2)}) %collective-permute-start.27) | collective-permute-done | bytes 1048608 | tf_op jit(solution)/shard_map/ppermute | solution.py:434
  383.6 21.2 %collective-permute-done.28.refs_7_ = bf16[4,2,16,32,128]{4,3,2,1,0:T(8,128)(2,1)} collective-permute-done((bf16[4,2,16,32,128]{4,3,2,1,0:T(8,128)(2,1)S(1)}, bf16[4,2,16,32,128]{4,3,2,1,0:T(8,128)(2,1)}, u32[]{:S(2)}, u32[]{:S(2)}) %collective-permute-start.28) | collective-permute-done | bytes 1048608 | tf_op jit(solution)/shard_map/ppermute | solution.py:434
  409.4 17.8 %collective-permute-done.29.refs_5_ = bf16[4,2,16,32,128]{4,3,2,1,0:T(8,128)(2,1)} collective-permute-done((bf16[4,2,16,32,128]{4,3,2,1,0:T(8,128)(2,1)}, bf16[4,2,16,32,128]{4,3,2,1,0:T(8,128)(2,1)}, u32[]{:S(2)}, u32[]{:S(2)}) %collective-permute-start.29) | collective-permute-done | bytes 1048608 | tf_op jit(solution)/shard_map/ppermute | solution.py:434
  429.2 20.6 %collective-permute-done.30.refs_5_ = bf16[4,2,16,32,128]{4,3,2,1,0:T(8,128)(2,1)} collective-permute-done((bf16[4,2,16,32,128]{4,3,2,1,0:T(8,128)(2,1)}, bf16[4,2,16,32,128]{4,3,2,1,0:T(8,128)(2,1)}, u32[]{:S(2)}, u32[]{:S(2)}) %collective-permute-start.30) | collective-permute-done | bytes 1048608 | tf_op jit(solution)/shard_map/ppermute | solution.py:434
  451.5 20.8 %collective-permute-done.31.refs_7_ = bf16[4,2,16,32,128]{4,3,2,1,0:T(8,128)(2,1)} collective-permute-done((bf16[4,2,16,32,128]{4,3,2,1,0:T(8,128)(2,1)}, bf16[4,2,16,32,128]{4,3,2,1,0:T(8,128)(2,1)}, u32[]{:S(2)}, u32[]{:S(2)}) %collective-permute-start.31) | collective-permute-done | bytes 1048608 | tf_op jit(solution)/shard_map/ppermute | solution.py:434
  473.9 18.8 %collective-permute-done.24 = f32[2,2,8,16]{3,2,1,0:T(8,128)S(1)} collective-permute-done((f32[2,2,8,16]{3,2,1,0:T(8,128)S(1)}, f32[2,2,8,16]{3,2,1,0:T(8,128)S(1)}, u32[]{:S(2)}, u32[]{:S(2)}) %collective-permute-start.24) | collective-permute-done | bytes 2080 | tf_op jit(solution)/shard_map/ppermute | solution.py:447
  498.1 2.7 select_select_fusion.1.refs_0_
  503.0 14.2 %shard_map.55.refs_9_ = f32[2,2,8,32,8,8,128]{6,5,4,3,2,1,0:T(8,128)} custom-call(s32[2]{0:T(128)} %pad_add_fusion.4.scalar_ref, bf16[4,2,16,32,128]{4,3,2,1,0:T(8,128)(2,1)} %select_select_fusion.1.refs_0_, f32[8,8,8,128]{3,2,1,0:T(8,128)} %broadcast_in_dim.112.refs_1_, bf16[64,32]{1,0:T(8,128)(2,1)} %get-tuple-element.196.refs_2_, ...), custom_call_target="tpu_custom_call" | custom-call | tf_op jit(solution)/shard_map/pallas_call | solution.py:290
  524.4 2.4 select_select_fusion.2.refs_0_
  529.2 2.7 select_select_fusion.3.refs_0_
  531.9 14.3 %shard_map.56.refs_9_ = f32[2,2,8,32,8,8,128]{6,5,4,3,2,1,0:T(8,128)} custom-call(s32[2]{0:T(128)} %pad_add_fusion.4.scalar_ref, bf16[4,2,16,32,128]{4,3,2,1,0:T(8,128)(2,1)} %select_select_fusion.2.refs_0_, f32[8,8,8,128]{3,2,1,0:T(8,128)} %broadcast_in_dim.112.refs_1_, bf16[64,32]{1,0:T(8,128)(2,1)} %get-tuple-element.196.refs_2_, ...), custom_call_target="tpu_custom_call", output_to_operand_aliasing={{}: (10, {})} | custom-call | tf_op jit(solution)/shard_map/pallas_call | solution.py:290
  546.2 14.2 %shard_map.57.refs_9_ = f32[2,2,8,32,8,8,128]{6,5,4,3,2,1,0:T(8,128)} custom-call(s32[2]{0:T(128)} %pad_add_fusion.4.scalar_ref, bf16[4,2,16,32,128]{4,3,2,1,0:T(8,128)(2,1)} %select_select_fusion.refs_0_, f32[8,8,8,128]{3,2,1,0:T(8,128)} %broadcast_in_dim.112.refs_1_, bf16[64,32]{1,0:T(8,128)(2,1)} %get-tuple-element.196.refs_2_, ...), custom_call_target="tpu_custom_call", output_to_operand_aliasing={{}: (10, {})} | custom-call | tf_op jit(solution)/shard_map/pallas_call | solution.py:290
  560.4 14.3 %shard_map.58.refs_7_ = f32[2,2,8,32,8,8,128]{6,5,4,3,2,1,0:T(8,128)} custom-call(s32[2]{0:T(128)} %pad_add_fusion.4.scalar_ref, bf16[4,2,16,32,128]{4,3,2,1,0:T(8,128)(2,1)} %select_select_fusion.3.refs_0_, f32[8,8,8,128]{3,2,1,0:T(8,128)} %broadcast_in_dim.112.refs_1_, bf16[64,32]{1,0:T(8,128)(2,1)} %get-tuple-element.196.refs_2_, ...), custom_call_target="tpu_custom_call", output_to_operand_aliasing={{}: (10, {})} | custom-call | tf_op jit(solution)/shard_map/pallas_call | solution.py:290
  574.7 8.9 %shard_map.59.refs_7_ = f32[2,2,8,32,8,8,128]{6,5,4,3,2,1,0:T(8,128)} custom-call(s32[2]{0:T(128)} %pad_add_fusion.3.scalar_ref, bf16[4,2,16,32,128]{4,3,2,1,0:T(8,128)(2,1)} %select_select_fusion.1.refs_0_, f32[8,8,8,128]{3,2,1,0:T(8,128)} %broadcast_in_dim.112.refs_1_, bf16[64,32]{1,0:T(8,128)(2,1)} %get-tuple-element.196.refs_2_, ...), custom_call_target="tpu_custom_call", output_to_operand_aliasing={{}: (8, {})} | custom-call | tf_op jit(solution)/shard_map/pallas_call | solution.py:290
  583.7 9.0 %shard_map.60.refs_7_ = f32[2,2,8,32,8,8,128]{6,5,4,3,2,1,0:T(8,128)} custom-call(s32[2]{0:T(128)} %pad_add_fusion.3.scalar_ref, bf16[4,2,16,32,128]{4,3,2,1,0:T(8,128)(2,1)} %select_select_fusion.2.refs_0_, f32[8,8,8,128]{3,2,1,0:T(8,128)} %broadcast_in_dim.112.refs_1_, bf16[64,32]{1,0:T(8,128)(2,1)} %get-tuple-element.196.refs_2_, ...), custom_call_target="tpu_custom_call", output_to_operand_aliasing={{}: (8, {})} | custom-call | tf_op jit(solution)/shard_map/pallas_call | solution.py:290
  600.0 8.9 %shard_map.61.refs_7_ = f32[2,2,8,32,8,8,128]{6,5,4,3,2,1,0:T(8,128)} custom-call(s32[2]{0:T(128)} %pad_add_fusion.2.scalar_ref, bf16[4,2,16,32,128]{4,3,2,1,0:T(8,128)(2,1)} %select_select_fusion.1.refs_0_, f32[8,8,8,128]{3,2,1,0:T(8,128)} %broadcast_in_dim.112.refs_1_, bf16[64,32]{1,0:T(8,128)(2,1)} %get-tuple-element.196.refs_2_, ...), custom_call_target="tpu_custom_call", output_to_operand_aliasing={{}: (8, {})} | custom-call | tf_op jit(solution)/shard_map/pallas_call | solution.py:290
  608.9 52.8 %collective-permute-done.47.refs_5_ = bf16[4,2,16,32,128]{4,3,2,1,0:T(8,128)(2,1)} collective-permute-done((bf16[4,2,16,32,128]{4,3,2,1,0:T(8,128)(2,1)}, bf16[4,2,16,32,128]{4,3,2,1,0:T(8,128)(2,1)}, u32[]{:S(2)}, u32[]{:S(2)}) %collective-permute-start.47) | collective-permute-done | bytes 1048608 | tf_op jit(solution)/shard_map/ppermute | solution.py:458
  661.6 9.1 %shard_map.62.refs_7_ = f32[2,2,8,32,8,8,128]{6,5,4,3,2,1,0:T(8,128)} custom-call(s32[2]{0:T(128)} %pad_add_fusion.2.scalar_ref, bf16[4,2,16,32,128]{4,3,2,1,0:T(8,128)(2,1)} %select_select_fusion.2.refs_0_, f32[8,8,8,128]{3,2,1,0:T(8,128)} %broadcast_in_dim.112.refs_1_, bf16[64,32]{1,0:T(8,128)(2,1)} %get-tuple-element.196.refs_2_, ...), custom_call_target="tpu_custom_call", output_to_operand_aliasing={{}: (8, {})} | custom-call | tf_op jit(solution)/shard_map/pallas_call | solution.py:290
  670.7 13.4 %collective-permute-done.46.refs_5_ = bf16[4,2,16,32,128]{4,3,2,1,0:T(8,128)(2,1)} collective-permute-done((bf16[4,2,16,32,128]{4,3,2,1,0:T(8,128)(2,1)}, bf16[4,2,16,32,128]{4,3,2,1,0:T(8,128)(2,1)}, u32[]{:S(2)}, u32[]{:S(2)}) %collective-permute-start.46) | collective-permute-done | bytes 1048608 | tf_op jit(solution)/shard_map/ppermute | solution.py:458
  684.1 8.9 %shard_map.63.refs_7_ = f32[2,2,8,32,8,8,128]{6,5,4,3,2,1,0:T(8,128)} custom-call(s32[2]{0:T(128)} %pad_add_fusion.3.scalar_ref, bf16[4,2,16,32,128]{4,3,2,1,0:T(8,128)(2,1)} %select_select_fusion.refs_0_, f32[8,8,8,128]{3,2,1,0:T(8,128)} %broadcast_in_dim.112.refs_1_, bf16[64,32]{1,0:T(8,128)(2,1)} %get-tuple-element.196.refs_2_, ...), custom_call_target="tpu_custom_call", output_to_operand_aliasing={{}: (8, {})} | custom-call | tf_op jit(solution)/shard_map/pallas_call | solution.py:290
  693.1 13.4 %collective-permute-done.45.refs_5_ = bf16[4,2,16,32,128]{4,3,2,1,0:T(8,128)(2,1)S(1)} collective-permute-done((bf16[4,2,16,32,128]{4,3,2,1,0:T(8,128)(2,1)}, bf16[4,2,16,32,128]{4,3,2,1,0:T(8,128)(2,1)S(1)}, u32[]{:S(2)}, u32[]{:S(2)}) %collective-permute-start.45) | collective-permute-done | bytes 1048608 | tf_op jit(solution)/shard_map/ppermute | solution.py:458
  707.4 9.0 %shard_map.64.refs_7_ = f32[2,2,8,32,8,8,128]{6,5,4,3,2,1,0:T(8,128)} custom-call(s32[2]{0:T(128)} %pad_add_fusion.3.scalar_ref, bf16[4,2,16,32,128]{4,3,2,1,0:T(8,128)(2,1)} %select_select_fusion.3.refs_0_, f32[8,8,8,128]{3,2,1,0:T(8,128)} %broadcast_in_dim.112.refs_1_, bf16[64,32]{1,0:T(8,128)(2,1)} %get-tuple-element.196.refs_2_, ...), custom_call_target="tpu_custom_call", output_to_operand_aliasing={{}: (8, {})} | custom-call | tf_op jit(solution)/shard_map/pallas_call | solution.py:290
  716.4 12.5 %collective-permute-done.44.refs_5_ = bf16[4,2,16,32,128]{4,3,2,1,0:T(8,128)(2,1)S(1)} collective-permute-done((bf16[4,2,16,32,128]{4,3,2,1,0:T(8,128)(2,1)}, bf16[4,2,16,32,128]{4,3,2,1,0:T(8,128)(2,1)S(1)}, u32[]{:S(2)}, u32[]{:S(2)}) %collective-permute-start.44) | collective-permute-done | bytes 1048608 | tf_op jit(solution)/shard_map/ppermute | solution.py:458
  729.9 8.9 %shard_map.65.refs_7_ = f32[2,2,8,32,8,8,128]{6,5,4,3,2,1,0:T(8,128)} custom-call(s32[2]{0:T(128)} %pad_add_fusion.2.scalar_ref, bf16[4,2,16,32,128]{4,3,2,1,0:T(8,128)(2,1)} %select_select_fusion.refs_0_, f32[8,8,8,128]{3,2,1,0:T(8,128)} %broadcast_in_dim.112.refs_1_, bf16[64,32]{1,0:T(8,128)(2,1)} %get-tuple-element.196.refs_2_, ...), custom_call_target="tpu_custom_call", output_to_operand_aliasing={{}: (8, {})} | custom-call | tf_op jit(solution)/shard_map/pallas_call | solution.py:290
  738.8 5.8 collective-permute-done.43.refs_5_
  745.6 9.0 %shard_map.66 = f32[2,2,8,32,8,8,128]{6,5,4,3,2,1,0:T(8,128)} custom-call(s32[2]{0:T(128)} %pad_add_fusion.2.scalar_ref, bf16[4,2,16,32,128]{4,3,2,1,0:T(8,128)(2,1)} %select_select_fusion.3.refs_0_, f32[8,8,8,128]{3,2,1,0:T(8,128)} %broadcast_in_dim.112.refs_1_, bf16[64,32]{1,0:T(8,128)(2,1)} %get-tuple-element.196.refs_2_, ...), custom_call_target="tpu_custom_call", output_to_operand_aliasing={{}: (8, {})} | custom-call | tf_op jit(solution)/shard_map/pallas_call | solution.py:290
  (196 shorter events, 97.1 us)
Async XLA Ops:
  0.7 22.4 %collective-permute-start.2 = (s32[2,128]{1,0:T(2,128)S(1)}, s32[2,128]{1,0:T(2,128)S(1)}, u32[]{:S(2)}, u32[]{:S(2)}) collective-permute-start(s32[2,128]{1,0:T(2,128)S(1)} %pad_add_fusion.1), channel_id=1, source_target_pairs={{0,8},{12,4},{1,9},{13,5},{2,10},{14,6},{3,11},{15,7},{16,24},{28,... | collective-permute-start | bytes 3080 | tf_op jit(solution)/shard_map/ppermute | solution.py:407
  6.6 17.8 %collective-permute-start = (s32[2,128]{1,0:T(2,128)S(1)}, s32[2,128]{1,0:T(2,128)S(1)}, u32[]{:S(2)}, u32[]{:S(2)}) collective-permute-start(s32[2,128]{1,0:T(2,128)S(1)} %pad_add_fusion.1), channel_id=1, source_target_pairs={{0,4},{12,8},{1,5},{13,9},{2,6},{14,10},{3,7},{15,11},{16,20},{28,... | collective-permute-start | bytes 3080 | tf_op jit(solution)/shard_map/ppermute | solution.py:407
  7.9 16.6 %collective-permute-start.1 = (s32[2,128]{1,0:T(2,128)S(1)}, s32[2,128]{1,0:T(2,128)S(1)}, u32[]{:S(2)}, u32[]{:S(2)}) collective-permute-start(s32[2,128]{1,0:T(2,128)S(1)} %pad_add_fusion.1), channel_id=1, source_target_pairs={{4,8},{8,4},{5,9},{9,5},{6,10},{10,6},{7,11},{11,7},{20,24},{24,20... | collective-permute-start | bytes 3080 | tf_op jit(solution)/shard_map/ppermute | solution.py:407
  14.4 51.2 %collective-permute-start.4 = (bf16[2,16,2,64,128]{4,3,2,1,0:T(8,128)(2,1)}, bf16[2,16,2,64,128]{4,3,2,1,0:T(8,128)(2,1)S(1)}, u32[]{:S(2)}, u32[]{:S(2)}) collective-permute-start(bf16[2,16,2,64,128]{4,3,2,1,0:T(8,128)(2,1)} %bitcast.184), channel_id=1, source_target_pairs={{4,8},{8,4},{5,9},{9,5},{6,10},{10,6},{7,11},{11,7},{20,24},{24,20... | collective-permute-start | bytes 3145736 | tf_op jit(solution)/shard_map/ppermute | solution.py:417
  15.1 50.4 %collective-permute-start.5 = (bf16[2,16,2,64,128]{4,3,2,1,0:T(8,128)(2,1)}, bf16[2,16,2,64,128]{4,3,2,1,0:T(8,128)(2,1)S(1)}, u32[]{:S(2)}, u32[]{:S(2)}) collective-permute-start(bf16[2,16,2,64,128]{4,3,2,1,0:T(8,128)(2,1)} %bitcast.185), channel_id=1, source_target_pairs={{0,8},{12,4},{1,9},{13,5},{2,10},{14,6},{3,11},{15,7},{16,24},{28,... | collective-permute-start | bytes 3145736 | tf_op jit(solution)/shard_map/ppermute | solution.py:417
  23.1 42.4 %collective-permute-start.3 = (bf16[2,16,2,64,128]{4,3,2,1,0:T(8,128)(2,1)}, bf16[2,16,2,64,128]{4,3,2,1,0:T(8,128)(2,1)S(1)}, u32[]{:S(2)}, u32[]{:S(2)}) collective-permute-start(bf16[2,16,2,64,128]{4,3,2,1,0:T(8,128)(2,1)} %bitcast.146), channel_id=1, source_target_pairs={{0,4},{12,8},{1,5},{13,9},{2,6},{14,10},{3,7},{15,11},{16,20},{28,... | collective-permute-start | bytes 3145736 | tf_op jit(solution)/shard_map/ppermute | solution.py:417
  65.6 1.4 copy-start.3
  72.5 7.6 %collective-permute-start.6 = (bf16[16,128,256]{2,1,0:T(8,128)(2,1)}, bf16[16,128,256]{2,1,0:T(8,128)(2,1)S(1)}, u32[]{:S(2)}, u32[]{:S(2)}) collective-permute-start(bf16[16,128,256]{2,1,0:T(8,128)(2,1)} %beam_sums.8), channel_id=1, source_target_pairs={{0,16},{1,17},{2,18},{3,19},{4,20},{5,21},{6,22},{7,23},{8,24},{9,... | collective-permute-start | bytes 3145736 | tf_op jit(solution)/shard_map/ppermute | solution.py:22
  80.1 1.4 copy-start.14
  91.5 221.8 %copy-start.18 = (f32[4,16,128]{2,1,0:T(8,128)S(1)}, f32[4,16,128]{2,1,0:T(8,128)}, u32[]{:S(2)}) copy-start(f32[4,16,128]{2,1,0:T(8,128)} %get-tuple-element.129) | copy-start | bytes 98308
  91.5 10.1 %collective-permute-start.7 = (bf16[16,128,256]{2,1,0:T(8,128)(2,1)}, bf16[16,128,256]{2,1,0:T(8,128)(2,1)S(1)}, u32[]{:S(2)}, u32[]{:S(2)}) collective-permute-start(bf16[16,128,256]{2,1,0:T(8,128)(2,1)} %beam_sums.9), channel_id=1, source_target_pairs={{0,16},{1,17},{2,18},{3,19},{4,20},{5,21},{6,22},{7,23},{8,24},{9,... | collective-permute-start | bytes 3145736 | tf_op jit(solution)/shard_map/ppermute | solution.py:22
  93.0 28.1 %collective-permute-start.8 = (bf16[2,16,2,64,128]{4,3,2,1,0:T(8,128)(2,1)}, bf16[2,16,2,64,128]{4,3,2,1,0:T(8,128)(2,1)S(1)}, u32[]{:S(2)}, u32[]{:S(2)}) collective-permute-start(bf16[2,16,2,64,128]{4,3,2,1,0:T(8,128)(2,1)} %bitcast.149), channel_id=1, source_target_pairs={{0,4},{12,8},{1,5},{13,9},{2,6},{14,10},{3,7},{15,11},{16,20},{28,... | collective-permute-start | bytes 3145736 | tf_op jit(solution)/shard_map/ppermute | solution.py:417
  97.3 43.7 %collective-permute-start.10 = (bf16[2,16,2,64,128]{4,3,2,1,0:T(8,128)(2,1)}, bf16[2,16,2,64,128]{4,3,2,1,0:T(8,128)(2,1)S(1)}, u32[]{:S(2)}, u32[]{:S(2)}) collective-permute-start(bf16[2,16,2,64,128]{4,3,2,1,0:T(8,128)(2,1)} %bitcast.186), channel_id=1, source_target_pairs={{0,8},{12,4},{1,9},{13,5},{2,10},{14,6},{3,11},{15,7},{16,24},{28,... | collective-permute-start | bytes 3145736 | tf_op jit(solution)/shard_map/ppermute | solution.py:417
  98.7 42.3 %collective-permute-start.9 = (bf16[2,16,2,64,128]{4,3,2,1,0:T(8,128)(2,1)}, bf16[2,16,2,64,128]{4,3,2,1,0:T(8,128)(2,1)}, u32[]{:S(2)}, u32[]{:S(2)}) collective-permute-start(bf16[2,16,2,64,128]{4,3,2,1,0:T(8,128)(2,1)} %bitcast.187), channel_id=1, source_target_pairs={{4,8},{8,4},{5,9},{9,5},{6,10},{10,6},{7,11},{11,7},{20,24},{24,20... | collective-permute-start | bytes 3145736 | tf_op jit(solution)/shard_map/ppermute | solution.py:417
  108.0 201.4 %copy-start = (bf16[4,2,16,32,128]{4,3,2,1,0:T(8,128)(2,1)S(1)}, bf16[4,2,16,32,128]{4,3,2,1,0:T(8,128)(2,1)}, u32[]{:S(2)}) copy-start(bf16[4,2,16,32,128]{4,3,2,1,0:T(8,128)(2,1)} %get-tuple-element.92.refs_4_) | copy-start | bytes 3145732
  108.0 205.4 %copy-start.19 = (f32[4,16,128]{2,1,0:T(8,128)S(1)}, f32[4,16,128]{2,1,0:T(8,128)}, u32[]{:S(2)}) copy-start(f32[4,16,128]{2,1,0:T(8,128)} %get-tuple-element.130) | copy-start | bytes 98308
  121.1 19.9 %copy-start.6 = (bf16[2,16,2,64,128]{4,3,2,1,0:T(8,128)(2,1)}, bf16[2,16,2,64,128]{4,3,2,1,0:T(8,128)(2,1)S(1)}, u32[]{:S(2)}) copy-start(bf16[2,16,2,64,128]{4,3,2,1,0:T(8,128)(2,1)S(1)} %collective-permute-done.8.refs_1_) | copy-start | bytes 3145732
  141.0 1.0 copy-start.8
  146.6 5.8 collective-permute-start.11
  158.8 154.7 %copy-start.20 = (f32[4,16,128]{2,1,0:T(8,128)S(1)}, f32[4,16,128]{2,1,0:T(8,128)}, u32[]{:S(2)}) copy-start(f32[4,16,128]{2,1,0:T(8,128)} %get-tuple-element.131) | copy-start | bytes 98308
  163.3 13.8 %collective-permute-start.12 = (bf16[16,128,256]{2,1,0:T(8,128)(2,1)}, bf16[16,128,256]{2,1,0:T(8,128)(2,1)S(1)}, u32[]{:S(2)}, u32[]{:S(2)}) collective-permute-start(bf16[16,128,256]{2,1,0:T(8,128)(2,1)} %beam_sums.11), channel_id=1, source_target_pairs={{0,16},{1,17},{2,18},{3,19},{4,20},{5,21},{6,22},{7,23},{8,24},{9,... | collective-permute-start | bytes 3145736 | tf_op jit(solution)/shard_map/ppermute | solution.py:22
  164.7 29.8 %collective-permute-start.13 = (bf16[2,16,2,64,128]{4,3,2,1,0:T(8,128)(2,1)}, bf16[2,16,2,64,128]{4,3,2,1,0:T(8,128)(2,1)S(1)}, u32[]{:S(2)}, u32[]{:S(2)}) collective-permute-start(bf16[2,16,2,64,128]{4,3,2,1,0:T(8,128)(2,1)} %bitcast.152), channel_id=1, source_target_pairs={{0,4},{12,8},{1,5},{13,9},{2,6},{14,10},{3,7},{15,11},{16,20},{28,... | collective-permute-start | bytes 3145736 | tf_op jit(solution)/shard_map/ppermute | solution.py:417
  170.7 23.8 %collective-permute-start.14 = (bf16[2,16,2,64,128]{4,3,2,1,0:T(8,128)(2,1)}, bf16[2,16,2,64,128]{4,3,2,1,0:T(8,128)(2,1)}, u32[]{:S(2)}, u32[]{:S(2)}) collective-permute-start(bf16[2,16,2,64,128]{4,3,2,1,0:T(8,128)(2,1)} %bitcast.190), channel_id=1, source_target_pairs={{4,8},{8,4},{5,9},{9,5},{6,10},{10,6},{7,11},{11,7},{20,24},{24,20... | collective-permute-start | bytes 3145736 | tf_op jit(solution)/shard_map/ppermute | solution.py:417
  172.4 41.9 %collective-permute-start.15 = (bf16[2,16,2,64,128]{4,3,2,1,0:T(8,128)(2,1)}, bf16[2,16,2,64,128]{4,3,2,1,0:T(8,128)(2,1)}, u32[]{:S(2)}, u32[]{:S(2)}) collective-permute-start(bf16[2,16,2,64,128]{4,3,2,1,0:T(8,128)(2,1)} %bitcast.191), channel_id=1, source_target_pairs={{0,8},{12,4},{1,9},{13,5},{2,10},{14,6},{3,11},{15,7},{16,24},{28,... | collective-permute-start | bytes 3145736 | tf_op jit(solution)/shard_map/ppermute | solution.py:417
  177.1 1.0 copy-start.15
  183.6 128.4 %copy-start.1 = (bf16[4,2,16,32,128]{4,3,2,1,0:T(8,128)(2,1)S(1)}, bf16[4,2,16,32,128]{4,3,2,1,0:T(8,128)(2,1)}, u32[]{:S(2)}) copy-start(bf16[4,2,16,32,128]{4,3,2,1,0:T(8,128)(2,1)} %get-tuple-element.149.refs_6_) | copy-start | bytes 3145732
  183.6 130.0 %copy-start.21 = (f32[4,16,128]{2,1,0:T(8,128)S(1)}, f32[4,16,128]{2,1,0:T(8,128)}, u32[]{:S(2)}) copy-start(f32[4,16,128]{2,1,0:T(8,128)} %get-tuple-element.132) | copy-start | bytes 98308
  194.5 19.8 %copy-start.7 = (bf16[2,16,2,64,128]{4,3,2,1,0:T(8,128)(2,1)}, bf16[2,16,2,64,128]{4,3,2,1,0:T(8,128)(2,1)S(1)}, u32[]{:S(2)}) copy-start(bf16[2,16,2,64,128]{4,3,2,1,0:T(8,128)(2,1)S(1)} %collective-permute-done.13.refs_1_) | copy-start | bytes 3145732
  218.8 5.9 collective-permute-start.16
  224.7 1.0 copy-start.16
  235.7 14.5 %collective-permute-start.17 = (bf16[16,128,256]{2,1,0:T(8,128)(2,1)}, bf16[16,128,256]{2,1,0:T(8,128)(2,1)}, u32[]{:S(2)}, u32[]{:S(2)}) collective-permute-start(bf16[16,128,256]{2,1,0:T(8,128)(2,1)} %beam_sums.13), channel_id=1, source_target_pairs={{0,16},{1,17},{2,18},{3,19},{4,20},{5,21},{6,22},{7,23},{8,24},{9,... | collective-permute-start | bytes 3145736 | tf_op jit(solution)/shard_map/ppermute | solution.py:22
  238.0 29.5 %collective-permute-start.18 = (bf16[2,16,2,64,128]{4,3,2,1,0:T(8,128)(2,1)}, bf16[2,16,2,64,128]{4,3,2,1,0:T(8,128)(2,1)S(1)}, u32[]{:S(2)}, u32[]{:S(2)}) collective-permute-start(bf16[2,16,2,64,128]{4,3,2,1,0:T(8,128)(2,1)} %bitcast.155), channel_id=1, source_target_pairs={{0,4},{12,8},{1,5},{13,9},{2,6},{14,10},{3,7},{15,11},{16,20},{28,... | collective-permute-start | bytes 3145736 | tf_op jit(solution)/shard_map/ppermute | solution.py:417
  243.7 23.8 %collective-permute-start.19 = (bf16[2,16,2,64,128]{4,3,2,1,0:T(8,128)(2,1)}, bf16[2,16,2,64,128]{4,3,2,1,0:T(8,128)(2,1)}, u32[]{:S(2)}, u32[]{:S(2)}) collective-permute-start(bf16[2,16,2,64,128]{4,3,2,1,0:T(8,128)(2,1)} %bitcast.188), channel_id=1, source_target_pairs={{4,8},{8,4},{5,9},{9,5},{6,10},{10,6},{7,11},{11,7},{20,24},{24,20... | collective-permute-start | bytes 3145736 | tf_op jit(solution)/shard_map/ppermute | solution.py:417
  245.4 40.9 %collective-permute-start.20 = (bf16[2,16,2,64,128]{4,3,2,1,0:T(8,128)(2,1)}, bf16[2,16,2,64,128]{4,3,2,1,0:T(8,128)(2,1)}, u32[]{:S(2)}, u32[]{:S(2)}) collective-permute-start(bf16[2,16,2,64,128]{4,3,2,1,0:T(8,128)(2,1)} %bitcast.189), channel_id=1, source_target_pairs={{0,8},{12,4},{1,9},{13,5},{2,10},{14,6},{3,11},{15,7},{16,24},{28,... | collective-permute-start | bytes 3145736 | tf_op jit(solution)/shard_map/ppermute | solution.py:417
  267.5 18.8 %copy-start.9 = (bf16[2,16,2,64,128]{4,3,2,1,0:T(8,128)(2,1)}, bf16[2,16,2,64,128]{4,3,2,1,0:T(8,128)(2,1)S(1)}, u32[]{:S(2)}) copy-start(bf16[2,16,2,64,128]{4,3,2,1,0:T(8,128)(2,1)S(1)} %collective-permute-done.18.refs_1_) | copy-start | bytes 3145732
  286.3 240.5 %copy-start.2 = (bf16[4,2,16,32,128]{4,3,2,1,0:T(8,128)(2,1)S(1)}, bf16[4,2,16,32,128]{4,3,2,1,0:T(8,128)(2,1)}, u32[]{:S(2)}) copy-start(bf16[4,2,16,32,128]{4,3,2,1,0:T(8,128)(2,1)} %get-tuple-element.151.refs_4_) | copy-start | bytes 3145732
  291.0 3.9 collective-permute-start.21
  304.8 11.4 %collective-permute-start.22 = (bf16[16,128,256]{2,1,0:T(8,128)(2,1)}, bf16[16,128,256]{2,1,0:T(8,128)(2,1)}, u32[]{:S(2)}, u32[]{:S(2)}) collective-permute-start(bf16[16,128,256]{2,1,0:T(8,128)(2,1)} %beam_sums.15), channel_id=1, source_target_pairs={{0,16},{1,17},{2,18},{3,19},{4,20},{5,21},{6,22},{7,23},{8,24},{9,... | collective-permute-start | bytes 3145736 | tf_op jit(solution)/shard_map/ppermute | solution.py:22
  308.1 29.3 %collective-permute-start.25 = (bf16[4,2,16,32,128]{4,3,2,1,0:T(8,128)(2,1)}, bf16[4,2,16,32,128]{4,3,2,1,0:T(8,128)(2,1)}, u32[]{:S(2)}, u32[]{:S(2)}) collective-permute-start(bf16[4,2,16,32,128]{4,3,2,1,0:T(8,128)(2,1)} %get-tuple-element.87.refs_4_), channel_id=1, source_target_pairs={{4,0},{8,12},{5,1},{9,13},{6,2},{10,14},{7,3},{11,15},{20,16},{24,... | collective-permute-start | bytes 3145736 | tf_op jit(solution)/shard_map/ppermute | solution.py:434
  309.4 50.5 %collective-permute-start.26 = (bf16[4,2,16,32,128]{4,3,2,1,0:T(8,128)(2,1)S(1)}, bf16[4,2,16,32,128]{4,3,2,1,0:T(8,128)(2,1)}, u32[]{:S(2)}, u32[]{:S(2)}) collective-permute-start(bf16[4,2,16,32,128]{4,3,2,1,0:T(8,128)(2,1)S(1)} %copy-done), channel_id=1, source_target_pairs={{4,0},{8,12},{5,1},{9,13},{6,2},{10,14},{7,3},{11,15},{20,16},{24,... | collective-permute-start | bytes 3145736 | tf_op jit(solution)/shard_map/ppermute | solution.py:434
  310.7 71.7 %collective-permute-start.27 = (bf16[4,2,16,32,128]{4,3,2,1,0:T(8,128)(2,1)}, bf16[4,2,16,32,128]{4,3,2,1,0:T(8,128)(2,1)}, u32[]{:S(2)}, u32[]{:S(2)}) collective-permute-start(bf16[4,2,16,32,128]{4,3,2,1,0:T(8,128)(2,1)} %get-tuple-element.147.refs_6_), channel_id=1, source_target_pairs={{4,0},{8,12},{5,1},{9,13},{6,2},{10,14},{7,3},{11,15},{20,16},{24,... | collective-permute-start | bytes 3145736 | tf_op jit(solution)/shard_map/ppermute | solution.py:434
  312.0 92.8 %collective-permute-start.28 = (bf16[4,2,16,32,128]{4,3,2,1,0:T(8,128)(2,1)S(1)}, bf16[4,2,16,32,128]{4,3,2,1,0:T(8,128)(2,1)}, u32[]{:S(2)}, u32[]{:S(2)}) collective-permute-start(bf16[4,2,16,32,128]{4,3,2,1,0:T(8,128)(2,1)S(1)} %copy-done.1), channel_id=1, source_target_pairs={{4,0},{8,12},{5,1},{9,13},{6,2},{10,14},{7,3},{11,15},{20,16},{24,... | collective-permute-start | bytes 3145736 | tf_op jit(solution)/shard_map/ppermute | solution.py:434
  316.2 111.1 %collective-permute-start.29 = (bf16[4,2,16,32,128]{4,3,2,1,0:T(8,128)(2,1)}, bf16[4,2,16,32,128]{4,3,2,1,0:T(8,128)(2,1)}, u32[]{:S(2)}, u32[]{:S(2)}) collective-permute-start(bf16[4,2,16,32,128]{4,3,2,1,0:T(8,128)(2,1)} %get-tuple-element.151.refs_4_), channel_id=1, source_target_pairs={{4,0},{8,12},{5,1},{9,13},{6,2},{10,14},{7,3},{11,15},{20,16},{24,... | collective-permute-start | bytes 3145736 | tf_op jit(solution)/shard_map/ppermute | solution.py:434
  337.4 68.7 %collective-permute-start.23 = (f32[2,8,16]{2,1,0:T(8,128)S(1)}, f32[2,8,16]{2,1,0:T(8,128)S(1)}, u32[]{:S(2)}, u32[]{:S(2)}) collective-permute-start(f32[2,8,16]{2,1,0:T(8,128)S(1)} %psum.7), channel_id=1, source_target_pairs={{4,8},{8,4},{5,9},{9,5},{6,10},{10,6},{7,11},{11,7},{20,24},{24,20... | collective-permute-start | bytes 3080 | tf_op jit(solution)/shard_map/ppermute | solution.py:442
  359.9 89.9 %collective-permute-start.30 = (bf16[4,2,16,32,128]{4,3,2,1,0:T(8,128)(2,1)}, bf16[4,2,16,32,128]{4,3,2,1,0:T(8,128)(2,1)}, u32[]{:S(2)}, u32[]{:S(2)}) collective-permute-start(bf16[4,2,16,32,128]{4,3,2,1,0:T(8,128)(2,1)} %get-tuple-element.153.refs_4_), channel_id=1, source_target_pairs={{4,0},{8,12},{5,1},{9,13},{6,2},{10,14},{7,3},{11,15},{20,16},{24,... | collective-permute-start | bytes 3145736 | tf_op jit(solution)/shard_map/ppermute | solution.py:434
  382.4 89.9 %collective-permute-start.31 = (bf16[4,2,16,32,128]{4,3,2,1,0:T(8,128)(2,1)}, bf16[4,2,16,32,128]{4,3,2,1,0:T(8,128)(2,1)}, u32[]{:S(2)}, u32[]{:S(2)}) collective-permute-start(bf16[4,2,16,32,128]{4,3,2,1,0:T(8,128)(2,1)} %get-tuple-element.155.refs_6_), channel_id=1, source_target_pairs={{4,0},{8,12},{5,1},{9,13},{6,2},{10,14},{7,3},{11,15},{20,16},{24,... | collective-permute-start | bytes 3145736 | tf_op jit(solution)/shard_map/ppermute | solution.py:434
  404.8 89.5 %collective-permute-start.32 = (bf16[4,2,16,32,128]{4,3,2,1,0:T(8,128)(2,1)}, bf16[4,2,16,32,128]{4,3,2,1,0:T(8,128)(2,1)}, u32[]{:S(2)}, u32[]{:S(2)}) collective-permute-start(bf16[4,2,16,32,128]{4,3,2,1,0:T(8,128)(2,1)} %get-tuple-element.157.refs_6_), channel_id=1, source_target_pairs={{4,0},{8,12},{5,1},{9,13},{6,2},{10,14},{7,3},{11,15},{20,16},{24,... | collective-permute-start | bytes 3145736 | tf_op jit(solution)/shard_map/ppermute | solution.py:434
  406.1 89.8 %collective-permute-start.35 = (bf16[4,2,16,32,128]{4,3,2,1,0:T(8,128)(2,1)}, bf16[4,2,16,32,128]{4,3,2,1,0:T(8,128)(2,1)}, u32[]{:S(2)}, u32[]{:S(2)}) collective-permute-start(bf16[4,2,16,32,128]{4,3,2,1,0:T(8,128)(2,1)} %get-tuple-element.87.refs_4_), channel_id=1, source_target_pairs={{4,8},{8,4},{5,9},{9,5},{6,10},{10,6},{7,11},{11,7},{20,24},{24,20... | collective-permute-start | bytes 3145736 | tf_op jit(solution)/shard_map/ppermute | solution.py:436
  427.3 65.4 %collective-permute-start.24 = (f32[2,2,8,16]{3,2,1,0:T(8,128)S(1)}, f32[2,2,8,16]{3,2,1,0:T(8,128)S(1)}, u32[]{:S(2)}, u32[]{:S(2)}) collective-permute-start(f32[2,2,8,16]{3,2,1,0:T(8,128)S(1)} %pad_maximum_fusion), channel_id=1, source_target_pairs={{4,0},{8,12},{5,1},{9,13},{6,2},{10,14},{7,3},{11,15},{20,16},{24,... | collective-permute-start | bytes 6152 | tf_op jit(solution)/shard_map/ppermute | solution.py:447
  449.8 67.4 %collective-permute-start.33 = (bf16[4,2,16,32,128]{4,3,2,1,0:T(8,128)(2,1)S(1)}, bf16[4,2,16,32,128]{4,3,2,1,0:T(8,128)(2,1)}, u32[]{:S(2)}, u32[]{:S(2)}) collective-permute-start(bf16[4,2,16,32,128]{4,3,2,1,0:T(8,128)(2,1)S(1)} %copy-done), channel_id=1, source_target_pairs={{4,8},{8,4},{5,9},{9,5},{6,10},{10,6},{7,11},{11,7},{20,24},{24,20... | collective-permute-start | bytes 3145736 | tf_op jit(solution)/shard_map/ppermute | solution.py:436
  472.2 46.2 %collective-permute-start.37 = (bf16[4,2,16,32,128]{4,3,2,1,0:T(8,128)(2,1)}, bf16[4,2,16,32,128]{4,3,2,1,0:T(8,128)(2,1)}, u32[]{:S(2)}, u32[]{:S(2)}) collective-permute-start(bf16[4,2,16,32,128]{4,3,2,1,0:T(8,128)(2,1)} %get-tuple-element.147.refs_6_), channel_id=1, source_target_pairs={{4,8},{8,4},{5,9},{9,5},{6,10},{10,6},{7,11},{11,7},{20,24},{24,20... | collective-permute-start | bytes 3145736 | tf_op jit(solution)/shard_map/ppermute | solution.py:445
  492.7 27.1 %collective-permute-start.38 = (bf16[4,2,16,32,128]{4,3,2,1,0:T(8,128)(2,1)S(1)}, bf16[4,2,16,32,128]{4,3,2,1,0:T(8,128)(2,1)}, u32[]{:S(2)}, u32[]{:S(2)}) collective-permute-start(bf16[4,2,16,32,128]{4,3,2,1,0:T(8,128)(2,1)S(1)} %copy-done.1), channel_id=1, source_target_pairs={{4,8},{8,4},{5,9},{9,5},{6,10},{10,6},{7,11},{11,7},{20,24},{24,20... | collective-permute-start | bytes 3145736 | tf_op jit(solution)/shard_map/ppermute | solution.py:445
  494.3 27.1 %collective-permute-start.39 = (bf16[4,2,16,32,128]{4,3,2,1,0:T(8,128)(2,1)}, bf16[4,2,16,32,128]{4,3,2,1,0:T(8,128)(2,1)}, u32[]{:S(2)}, u32[]{:S(2)}) collective-permute-start(bf16[4,2,16,32,128]{4,3,2,1,0:T(8,128)(2,1)} %get-tuple-element.151.refs_4_), channel_id=1, source_target_pairs={{4,8},{8,4},{5,9},{9,5},{6,10},{10,6},{7,11},{11,7},{20,24},{24,20... | collective-permute-start | bytes 3145736 | tf_op jit(solution)/shard_map/ppermute | solution.py:445
  496.0 27.1 %collective-permute-start.40 = (bf16[4,2,16,32,128]{4,3,2,1,0:T(8,128)(2,1)}, bf16[4,2,16,32,128]{4,3,2,1,0:T(8,128)(2,1)}, u32[]{:S(2)}, u32[]{:S(2)}) collective-permute-start(bf16[4,2,16,32,128]{4,3,2,1,0:T(8,128)(2,1)} %get-tuple-element.153.refs_4_), channel_id=1, source_target_pairs={{4,8},{8,4},{5,9},{9,5},{6,10},{10,6},{7,11},{11,7},{20,24},{24,20... | collective-permute-start | bytes 3145736 | tf_op jit(solution)/shard_map/ppermute | solution.py:445
  517.2 57.6 %collective-permute-start.36 = (bf16[4,2,16,32,128]{4,3,2,1,0:T(8,128)(2,1)}, bf16[4,2,16,32,128]{4,3,2,1,0:T(8,128)(2,1)}, u32[]{:S(2)}, u32[]{:S(2)}) collective-permute-start(bf16[4,2,16,32,128]{4,3,2,1,0:T(8,128)(2,1)} %collective-permute-done.35.refs_4_), channel_id=1, source_target_pairs={{4,0},{8,12},{5,1},{9,13},{6,2},{10,14},{7,3},{11,15},{20,16},{24,... | collective-permute-start | bytes 3145736 | tf_op jit(solution)/shard_map/ppermute | solution.py:458
  518.5 65.2 %collective-permute-start.34 = (bf16[4,2,16,32,128]{4,3,2,1,0:T(8,128)(2,1)}, bf16[4,2,16,32,128]{4,3,2,1,0:T(8,128)(2,1)}, u32[]{:S(2)}, u32[]{:S(2)}) collective-permute-start(bf16[4,2,16,32,128]{4,3,2,1,0:T(8,128)(2,1)} %collective-permute-done.33.refs_4_), channel_id=1, source_target_pairs={{4,0},{8,12},{5,1},{9,13},{6,2},{10,14},{7,3},{11,15},{20,16},{24,... | collective-permute-start | bytes 3145736 | tf_op jit(solution)/shard_map/ppermute | solution.py:458
  519.8 63.9 %collective-permute-start.41 = (bf16[4,2,16,32,128]{4,3,2,1,0:T(8,128)(2,1)}, bf16[4,2,16,32,128]{4,3,2,1,0:T(8,128)(2,1)}, u32[]{:S(2)}, u32[]{:S(2)}) collective-permute-start(bf16[4,2,16,32,128]{4,3,2,1,0:T(8,128)(2,1)} %get-tuple-element.155.refs_6_), channel_id=1, source_target_pairs={{4,8},{8,4},{5,9},{9,5},{6,10},{10,6},{7,11},{11,7},{20,24},{24,20... | collective-permute-start | bytes 3145736 | tf_op jit(solution)/shard_map/ppermute | solution.py:445
  521.4 71.2 %collective-permute-start.42 = (bf16[4,2,16,32,128]{4,3,2,1,0:T(8,128)(2,1)}, bf16[4,2,16,32,128]{4,3,2,1,0:T(8,128)(2,1)}, u32[]{:S(2)}, u32[]{:S(2)}) collective-permute-start(bf16[4,2,16,32,128]{4,3,2,1,0:T(8,128)(2,1)} %get-tuple-element.157.refs_6_), channel_id=1, source_target_pairs={{4,8},{8,4},{5,9},{9,5},{6,10},{10,6},{7,11},{11,7},{20,24},{24,20... | collective-permute-start | bytes 3145736 | tf_op jit(solution)/shard_map/ppermute | solution.py:445
  523.1 74.8 %collective-permute-start.48 = (bf16[4,2,16,32,128]{4,3,2,1,0:T(8,128)(2,1)}, bf16[4,2,16,32,128]{4,3,2,1,0:T(8,128)(2,1)}, u32[]{:S(2)}, u32[]{:S(2)}) collective-permute-start(bf16[4,2,16,32,128]{4,3,2,1,0:T(8,128)(2,1)} %collective-permute-done.37.refs_4_), channel_id=1, source_target_pairs={{4,0},{8,12},{5,1},{9,13},{6,2},{10,14},{7,3},{11,15},{20,16},{24,... | collective-permute-start | bytes 3145736 | tf_op jit(solution)/shard_map/ppermute | solution.py:458
  592.7 69.0 %collective-permute-start.47 = (bf16[4,2,16,32,128]{4,3,2,1,0:T(8,128)(2,1)}, bf16[4,2,16,32,128]{4,3,2,1,0:T(8,128)(2,1)}, u32[]{:S(2)}, u32[]{:S(2)}) collective-permute-start(bf16[4,2,16,32,128]{4,3,2,1,0:T(8,128)(2,1)} %collective-permute-done.38.refs_4_), channel_id=1, source_target_pairs={{4,0},{8,12},{5,1},{9,13},{6,2},{10,14},{7,3},{11,15},{20,16},{24,... | collective-permute-start | bytes 3145736 | tf_op jit(solution)/shard_map/ppermute | solution.py:458
  593.9 90.2 %collective-permute-start.46 = (bf16[4,2,16,32,128]{4,3,2,1,0:T(8,128)(2,1)}, bf16[4,2,16,32,128]{4,3,2,1,0:T(8,128)(2,1)}, u32[]{:S(2)}, u32[]{:S(2)}) collective-permute-start(bf16[4,2,16,32,128]{4,3,2,1,0:T(8,128)(2,1)} %collective-permute-done.39.refs_4_), channel_id=1, source_target_pairs={{4,0},{8,12},{5,1},{9,13},{6,2},{10,14},{7,3},{11,15},{20,16},{24,... | collective-permute-start | bytes 3145736 | tf_op jit(solution)/shard_map/ppermute | solution.py:458
  595.2 111.2 %collective-permute-start.45 = (bf16[4,2,16,32,128]{4,3,2,1,0:T(8,128)(2,1)}, bf16[4,2,16,32,128]{4,3,2,1,0:T(8,128)(2,1)S(1)}, u32[]{:S(2)}, u32[]{:S(2)}) collective-permute-start(bf16[4,2,16,32,128]{4,3,2,1,0:T(8,128)(2,1)} %collective-permute-done.40.refs_4_), channel_id=1, source_target_pairs={{4,0},{8,12},{5,1},{9,13},{6,2},{10,14},{7,3},{11,15},{20,16},{24,... | collective-permute-start | bytes 3145736 | tf_op jit(solution)/shard_map/ppermute | solution.py:458
  596.5 132.4 %collective-permute-start.44 = (bf16[4,2,16,32,128]{4,3,2,1,0:T(8,128)(2,1)}, bf16[4,2,16,32,128]{4,3,2,1,0:T(8,128)(2,1)S(1)}, u32[]{:S(2)}, u32[]{:S(2)}) collective-permute-start(bf16[4,2,16,32,128]{4,3,2,1,0:T(8,128)(2,1)} %collective-permute-done.41.refs_4_), channel_id=1, source_target_pairs={{4,0},{8,12},{5,1},{9,13},{6,2},{10,14},{7,3},{11,15},{20,16},{24,... | collective-permute-start | bytes 3145736 | tf_op jit(solution)/shard_map/ppermute | solution.py:458
  597.9 146.7 %collective-permute-start.43 = (bf16[4,2,16,32,128]{4,3,2,1,0:T(8,128)(2,1)}, bf16[4,2,16,32,128]{4,3,2,1,0:T(8,128)(2,1)S(1)}, u32[]{:S(2)}, u32[]{:S(2)}) collective-permute-start(bf16[4,2,16,32,128]{4,3,2,1,0:T(8,128)(2,1)} %collective-permute-done.42.refs_4_), channel_id=1, source_target_pairs={{4,0},{8,12},{5,1},{9,13},{6,2},{10,14},{7,3},{11,15},{20,16},{24,... | collective-permute-start | bytes 3145736 | tf_op jit(solution)/shard_map/ppermute | solution.py:458
  (7 other events, 6.8 us)
